TPU v7x, 32 devices: a whole 2x2x4 slice. The times are simulated.
32 devices in a mesh: gx: 4 (over z), gy: 4 (over y, x), gz: 2 (over core).
Axes of the slice: x: 2, y: 2, z: 4, core: 2. Of those that a mesh axis runs over, the one named last changes fastest.
Arguments:
- log_range: float32 [32, 128, 512], P('gz', 'gx', 'gy'), may hold values from -0.5 to 1.5
- sea_mask: int32 [32, 128, 512], P('gz', 'gx', 'gy'), may hold values 0 or 1
- forcing: float32 [32, 128, 512], P('gz', 'gx', 'gy'), may hold values from -24 to 24
- cotangent: float32 [32, 128, 512], P('gz', 'gx', 'gy'), may hold values from -24 to 24
Outputs:
- iterate: float32 [32, 128, 512], P('gz', 'gx', 'gy')
- range_grad: float32 [32, 128, 512], P('gz', 'gx', 'gy')
All inputs are finite; a program needn't handle non-finite values. No bound on the sum of `sea_mask` on one device may be relied on, other than what follows from the above.
Results may differ from a plain program's by a relative error of at most 0.00002.
Values sent between devices are 32-bit elements; how exact they have to be, the bound alone decides.
No kernel may reach another device: no remote copies, remote signals or barrier semaphores. Data moves between devices by JAX's collectives and lax.ppermute only.
A program may use at most 64 MiB of HBM per device.

v0:
```python
import jax
import jax.numpy as jnp
from jax import lax
from jax.sharding import PartitionSpec as P

SWEEPS = 4


relaxation = 0.9


def padded_2(shard, sides, width):
    for axis, dim in sides:
        size, length = (lax.axis_size(axis), shard.shape[dim])
        up = [(i, (i + 1) % size) for i in range(size - 1)]
        down = [(j, i) for i, j in up]
        last = lax.slice_in_dim(shard, length - width, length, axis=dim)
        initial = lax.slice_in_dim(shard, 0, width, axis=dim)
        before = lax.ppermute(last, axis, up)
        after = lax.ppermute(initial, axis, down)
        shard = jnp.concatenate([before, shard, after], axis=dim)
    return shard


def neighbours(padded):
    total = padded[2:, 1:-1, 1:-1] + padded[:-2, 1:-1, 1:-1]
    total = total + padded[1:-1, 2:, 1:-1] + padded[1:-1, :-2, 1:-1]
    total = total + padded[1:-1, 1:-1, 2:] + padded[1:-1, 1:-1, :-2]
    return total


def crop(field, margin):
    if margin == 0:
        return field
    return field[margin:-margin, margin:-margin, margin:-margin]


def forward_step(padded, margin, statics):
    sea, diagonal, source, depth_pad = statics
    outer_sea = crop(sea, depth_pad - 1 - margin)
    spread = neighbours(outer_sea * padded)
    inner = depth_pad - margin
    return (1.0 - relaxation) * crop(padded, 1) + relaxation * (
        crop(source, inner) + crop(sea, inner) * spread
    ) / crop(diagonal, inner)


def adjoint_step(padded, margin, statics):
    sea, diagonal, source, depth_pad = statics
    outer = depth_pad - 1 - margin
    scaled = crop(sea, outer) * relaxation * padded / crop(diagonal, outer)
    return (1.0 - relaxation) * crop(padded, 1) + crop(sea, depth_pad - margin) * neighbours(scaled)


def body(log_range, sea_mask, forcing, cotangent):
    sea_local = sea_mask.astype(jnp.float32)
    diagonal = sea_local * (6.0 + jnp.exp(-2.0 * log_range)) + (1.0 - sea_local)
    diagonal_wide, source_pad = (
        padded_2(diagonal, (("gx", 1), ("gy", 2), ("gz", 0)), SWEEPS),
        padded_2(forcing, (("gx", 1), ("gy", 2), ("gz", 0)), SWEEPS),
    )
    sea_pad = jnp.where(
        diagonal_wide > 3.0, jnp.ones_like(diagonal_wide), jnp.zeros_like(diagonal_wide)
    )
    diagonal_pad = jnp.maximum(diagonal_wide, 1.0)
    statics = (sea_pad, diagonal_pad, source_pad, SWEEPS)
    zeros = jnp.zeros_like(forcing)
    state = jnp.zeros_like(source_pad)
    forward_states = [zeros]
    for sweep_index in range(SWEEPS):
        margin = SWEEPS - 1 - sweep_index
        state = forward_step(state, margin, statics)
        forward_states.append(crop(state, margin))
    adjoint = padded_2(cotangent, (("gx", 1), ("gy", 2), ("gz", 0)), SWEEPS - 1)
    adjoints = [cotangent]
    for sweep_index in range(SWEEPS - 1):
        margin = SWEEPS - 2 - sweep_index
        adjoint = adjoint_step(adjoint, margin, statics)
        adjoints.append(crop(adjoint, margin))
    iterate = forward_states[-1]
    accumulated = jnp.zeros_like(forcing)
    for back in range(SWEEPS):
        level = SWEEPS - 1 - back
        accumulated = accumulated + adjoints[back] * (
            forward_states[level + 1] - (1.0 - relaxation) * forward_states[level]
        )
    range_grad = 2.0 * sea_local * jnp.exp(-2.0 * log_range) / diagonal * accumulated
    return (iterate, range_grad)


def solution(mesh):
    placed = (P("gz", "gx", "gy"), P("gz", "gx", "gy"), P("gz", "gx", "gy"), P("gz", "gx", "gy"))
    return jax.shard_map(
        body,
        mesh=mesh,
        in_specs=placed,
        out_specs=(P("gz", "gx", "gy"), P("gz", "gx", "gy")),
        check_vma=False,
    )
```

profile of v0, /device:TPU:0, one launch (start us, length us, event | category | flops | bytes accessed | tf_op | source)
XLA Modules:
  0.0 89.9 jit_solution(7769374708916871122)
XLA Ops:
  0.6 0.9 %fusion.38 = (f32[16,4,128]{2,1,0:T(4,128)S(1)}, f32[16,4,128]{2,1,0:T(4,128)S(1)}) fusion(f32[16,32,128]{2,1,0:T(8,128)} %param.6), kind=kLoop, calls=%fused_computation.106 | loop fusion | bytes 131072 | tf_op jit(solution)/shard_map/slice | solution.py:17
  1.6 5.0 %collective-permute-start = (f32[16,4,128]{2,1,0:T(4,128)S(1)}, f32[16,4,128]{2,1,0:T(4,128)S(1)}, u32[]{:S(2)}, u32[]{:S(2)}) collective-permute-start(f32[16,4,128]{2,1,0:T(4,128)S(1)} %get-tuple-element.37), channel_id=1, source_target_pairs={{0,8},{8,16},{16,24},{1,9},{9,17},{17,25},{2,10},{10,18},{18,26},{... | collective-permute-start | bytes 98312 | tf_op jit(solution)/shard_map/ppermute | solution.py:19
  6.5 1.3 %collective-permute-start.1 = (f32[16,4,128]{2,1,0:T(4,128)S(1)}, f32[16,4,128]{2,1,0:T(4,128)S(1)}, u32[]{:S(2)}, u32[]{:S(2)}) collective-permute-start(f32[16,4,128]{2,1,0:T(4,128)S(1)} %get-tuple-element.38), channel_id=1, source_target_pairs={{8,0},{16,8},{24,16},{9,1},{17,9},{25,17},{10,2},{18,10},{26,18},{... | collective-permute-start | bytes 98312 | tf_op jit(solution)/shard_map/ppermute | solution.py:20
  7.8 0.9 fusion.39
  8.7 4.5 %collective-permute-start.12 = (f32[16,3,128]{2,1,0:T(4,128)S(1)}, f32[16,3,128]{2,1,0:T(4,128)S(1)}, u32[]{:S(2)}, u32[]{:S(2)}) collective-permute-start(f32[16,3,128]{2,1,0:T(4,128)S(1)} %get-tuple-element.39), channel_id=1, source_target_pairs={{0,8},{8,16},{16,24},{1,9},{9,17},{17,25},{2,10},{10,18},{18,26},{... | collective-permute-start | bytes 73736 | tf_op jit(solution)/shard_map/ppermute | solution.py:19
  13.3 1.4 %collective-permute-start.13 = (f32[16,3,128]{2,1,0:T(4,128)S(1)}, f32[16,3,128]{2,1,0:T(4,128)S(1)}, u32[]{:S(2)}, u32[]{:S(2)}) collective-permute-start(f32[16,3,128]{2,1,0:T(4,128)S(1)} %get-tuple-element.40), channel_id=1, source_target_pairs={{8,0},{16,8},{24,16},{9,1},{17,9},{25,17},{10,2},{18,10},{26,18},{... | collective-permute-start | bytes 73736 | tf_op jit(solution)/shard_map/ppermute | solution.py:20
  14.7 1.0 %subtract_add_fusion = f32[16,32,128]{2,1,0:T(8,128)S(1)} fusion(s32[16,32,128]{2,1,0:T(8,128)S(1)} %copy-done.2, f32[16,32,128]{2,1,0:T(8,128)} %param.4), kind=kLoop, calls=%fused_computation.85 | loop fusion | flops 393216 | bytes 786432 | tf_op jit(solution)/shard_map/add | solution.py:57
  15.8 3.5 %collective-permute-done.13 = f32[16,3,128]{2,1,0:T(4,128)S(1)} collective-permute-done((f32[16,3,128]{2,1,0:T(4,128)S(1)}, f32[16,3,128]{2,1,0:T(4,128)S(1)}, u32[]{:S(2)}, u32[]{:S(2)}) %collective-permute-start.13) | collective-permute-done | bytes 24608 | tf_op jit(solution)/shard_map/ppermute | solution.py:20
  19.4 3.4 %collective-permute-start.14 = (f32[16,38,3]{2,1,0:T(8,128)S(1)}, f32[16,38,3]{2,1,0:T(8,128)S(1)}, u32[]{:S(2)}, u32[]{:S(2)}) collective-permute-start(f32[16,38,3]{2,1,0:T(8,128)S(1)} %get-tuple-element.33), channel_id=1, source_target_pairs={{0,2},{2,4},{4,6},{1,3},{3,5},{5,7},{8,10},{10,12},{12,14},{9,11},... | collective-permute-start | bytes 21896 | tf_op jit(solution)/shard_map/ppermute | solution.py:19
  22.9 1.3 %collective-permute-start.15 = (f32[16,38,3]{2,1,0:T(8,128)S(1)}, f32[16,38,3]{2,1,0:T(8,128)S(1)}, u32[]{:S(2)}, u32[]{:S(2)}) collective-permute-start(f32[16,38,3]{2,1,0:T(8,128)S(1)} %get-tuple-element.34), channel_id=1, source_target_pairs={{2,0},{4,2},{6,4},{3,1},{5,3},{7,5},{10,8},{12,10},{14,12},{11,9},... | collective-permute-start | bytes 21896 | tf_op jit(solution)/shard_map/ppermute | solution.py:20
  24.2 3.5 %collective-permute-start.6 = (f32[16,4,128]{2,1,0:T(4,128)S(1)}, f32[16,4,128]{2,1,0:T(4,128)S(1)}, u32[]{:S(2)}, u32[]{:S(2)}) collective-permute-start(f32[16,4,128]{2,1,0:T(4,128)S(1)} %get-tuple-element.41), channel_id=1, source_target_pairs={{0,8},{8,16},{16,24},{1,9},{9,17},{17,25},{2,10},{10,18},{18,26},{... | collective-permute-start | bytes 98312 | tf_op jit(solution)/shard_map/ppermute | solution.py:19
  27.8 1.3 %collective-permute-start.7 = (f32[16,4,128]{2,1,0:T(4,128)S(1)}, f32[16,4,128]{2,1,0:T(4,128)S(1)}, u32[]{:S(2)}, u32[]{:S(2)}) collective-permute-start(f32[16,4,128]{2,1,0:T(4,128)S(1)} %get-tuple-element.42), channel_id=1, source_target_pairs={{8,0},{16,8},{24,16},{9,1},{17,9},{25,17},{10,2},{18,10},{26,18},{... | collective-permute-start | bytes 98312 | tf_op jit(solution)/shard_map/ppermute | solution.py:20
  29.1 7.7 %collective-permute-done.15 = f32[16,38,3]{2,1,0:T(8,128)S(1)} collective-permute-done((f32[16,38,3]{2,1,0:T(8,128)S(1)}, f32[16,38,3]{2,1,0:T(8,128)S(1)}, u32[]{:S(2)}, u32[]{:S(2)}) %collective-permute-start.15) | collective-permute-done | bytes 7328 | tf_op jit(solution)/shard_map/ppermute | solution.py:20
  37.0 1.3 %collective-permute-start.16 = (f32[3,38,134]{2,1,0:T(8,128)S(1)}, f32[3,38,134]{2,1,0:T(8,128)S(1)}, u32[]{:S(2)}, u32[]{:S(2)}) collective-permute-start(f32[3,38,134]{2,1,0:T(8,128)S(1)} %get-tuple-element.27), channel_id=1, source_target_pairs={{0,1},{2,3},{4,5},{6,7},{8,9},{10,11},{12,13},{14,15},{16,17},{18,... | collective-permute-start | bytes 183320 | tf_op jit(solution)/shard_map/ppermute | solution.py:19
  38.3 1.3 %collective-permute-start.17 = (f32[3,38,134]{2,1,0:T(8,128)S(1)}, f32[3,38,134]{2,1,0:T(8,128)S(1)}, u32[]{:S(2)}, u32[]{:S(2)}) collective-permute-start(f32[3,38,134]{2,1,0:T(8,128)S(1)} %get-tuple-element.28), channel_id=1, source_target_pairs={{1,0},{3,2},{5,4},{7,6},{9,8},{11,10},{13,12},{15,14},{17,16},{19,... | collective-permute-start | bytes 183320 | tf_op jit(solution)/shard_map/ppermute | solution.py:20
  39.8 3.4 %collective-permute-start.8 = (f32[16,40,4]{2,1,0:T(8,128)S(1)}, f32[16,40,4]{2,1,0:T(8,128)S(1)}, u32[]{:S(2)}, u32[]{:S(2)}) collective-permute-start(f32[16,40,4]{2,1,0:T(8,128)S(1)} %get-tuple-element.35), channel_id=1, source_target_pairs={{0,2},{2,4},{4,6},{1,3},{3,5},{5,7},{8,10},{10,12},{12,14},{9,11},... | collective-permute-start | bytes 30728 | tf_op jit(solution)/shard_map/ppermute | solution.py:19
  43.3 1.3 %collective-permute-start.9 = (f32[16,40,4]{2,1,0:T(8,128)S(1)}, f32[16,40,4]{2,1,0:T(8,128)S(1)}, u32[]{:S(2)}, u32[]{:S(2)}) collective-permute-start(f32[16,40,4]{2,1,0:T(8,128)S(1)} %get-tuple-element.36), channel_id=1, source_target_pairs={{2,0},{4,2},{6,4},{3,1},{5,3},{7,5},{10,8},{12,10},{14,12},{11,9},... | collective-permute-start | bytes 30728 | tf_op jit(solution)/shard_map/ppermute | solution.py:20
  44.8 4.6 %collective-permute-start.2 = (f32[16,40,4]{2,1,0:T(8,128)S(1)}, f32[16,40,4]{2,1,0:T(8,128)S(1)}, u32[]{:S(2)}, u32[]{:S(2)}) collective-permute-start(f32[16,40,4]{2,1,0:T(8,128)S(1)} %get-tuple-element.31), channel_id=1, source_target_pairs={{0,2},{2,4},{4,6},{1,3},{3,5},{5,7},{8,10},{10,12},{12,14},{9,11},... | collective-permute-start | bytes 30728 | tf_op jit(solution)/shard_map/ppermute | solution.py:19
  49.4 1.8 %collective-permute-done.8 = f32[16,40,4]{2,1,0:T(8,128)S(1)} collective-permute-done((f32[16,40,4]{2,1,0:T(8,128)S(1)}, f32[16,40,4]{2,1,0:T(8,128)S(1)}, u32[]{:S(2)}, u32[]{:S(2)}) %collective-permute-start.8) | collective-permute-done | bytes 10272 | tf_op jit(solution)/shard_map/ppermute | solution.py:19
  51.2 1.3 %collective-permute-start.3 = (f32[16,40,4]{2,1,0:T(8,128)S(1)}, f32[16,40,4]{2,1,0:T(8,128)S(1)}, u32[]{:S(2)}, u32[]{:S(2)}) collective-permute-start(f32[16,40,4]{2,1,0:T(8,128)S(1)} %get-tuple-element.32), channel_id=1, source_target_pairs={{2,0},{4,2},{6,4},{3,1},{5,3},{7,5},{10,8},{12,10},{14,12},{11,9},... | collective-permute-start | bytes 30728 | tf_op jit(solution)/shard_map/ppermute | solution.py:20
  52.4 6.8 %collective-permute-done.9 = f32[16,40,4]{2,1,0:T(8,128)S(1)} collective-permute-done((f32[16,40,4]{2,1,0:T(8,128)S(1)}, f32[16,40,4]{2,1,0:T(8,128)S(1)}, u32[]{:S(2)}, u32[]{:S(2)}) %collective-permute-start.9) | collective-permute-done | bytes 10272 | tf_op jit(solution)/shard_map/ppermute | solution.py:20
  59.5 1.9 %collective-permute-start.10 = (f32[4,40,136]{2,1,0:T(8,128)S(1)}, f32[4,40,136]{2,1,0:T(8,128)S(1)}, u32[]{:S(2)}, u32[]{:S(2)}) collective-permute-start(f32[4,40,136]{2,1,0:T(8,128)S(1)} %get-tuple-element.29), channel_id=1, source_target_pairs={{0,1},{2,3},{4,5},{6,7},{8,9},{10,11},{12,13},{14,15},{16,17},{18,... | collective-permute-start | bytes 261128 | tf_op jit(solution)/shard_map/ppermute | solution.py:19
  61.5 1.3 %collective-permute-start.11 = (f32[4,40,136]{2,1,0:T(8,128)S(1)}, f32[4,40,136]{2,1,0:T(8,128)S(1)}, u32[]{:S(2)}, u32[]{:S(2)}) collective-permute-start(f32[4,40,136]{2,1,0:T(8,128)S(1)} %get-tuple-element.30), channel_id=1, source_target_pairs={{1,0},{3,2},{5,4},{7,6},{9,8},{11,10},{13,12},{15,14},{17,16},{19,... | collective-permute-start | bytes 261128 | tf_op jit(solution)/shard_map/ppermute | solution.py:20
  62.8 10.5 %collective-permute-done.3 = f32[16,40,4]{2,1,0:T(8,128)S(1)} collective-permute-done((f32[16,40,4]{2,1,0:T(8,128)S(1)}, f32[16,40,4]{2,1,0:T(8,128)S(1)}, u32[]{:S(2)}, u32[]{:S(2)}) %collective-permute-start.3) | collective-permute-done | bytes 10272 | tf_op jit(solution)/shard_map/ppermute | solution.py:20
  73.5 2.0 %collective-permute-start.4 = (f32[4,40,136]{2,1,0:T(8,128)S(1)}, f32[4,40,136]{2,1,0:T(8,128)S(1)}, u32[]{:S(2)}, u32[]{:S(2)}) collective-permute-start(f32[4,40,136]{2,1,0:T(8,128)S(1)} %get-tuple-element.25), channel_id=1, source_target_pairs={{0,1},{2,3},{4,5},{6,7},{8,9},{10,11},{12,13},{14,15},{16,17},{18,... | collective-permute-start | bytes 261128 | tf_op jit(solution)/shard_map/ppermute | solution.py:19
  75.5 1.5 %collective-permute-start.5 = (f32[4,40,136]{2,1,0:T(8,128)S(1)}, f32[4,40,136]{2,1,0:T(8,128)S(1)}, u32[]{:S(2)}, u32[]{:S(2)}) collective-permute-start(f32[4,40,136]{2,1,0:T(8,128)S(1)} %get-tuple-element.26), channel_id=1, source_target_pairs={{1,0},{3,2},{5,4},{7,6},{9,8},{11,10},{13,12},{15,14},{17,16},{19,... | collective-permute-start | bytes 261128 | tf_op jit(solution)/shard_map/ppermute | solution.py:20
  77.0 0.4 broadcast_multiply_fusion
  77.4 1.4 %collective-permute-done.5 = f32[4,40,136]{2,1,0:T(8,128)S(1)} collective-permute-done((f32[4,40,136]{2,1,0:T(8,128)S(1)}, f32[4,40,136]{2,1,0:T(8,128)S(1)}, u32[]{:S(2)}, u32[]{:S(2)}) %collective-permute-start.5) | collective-permute-done | bytes 87072 | tf_op jit(solution)/shard_map/ppermute | solution.py:20
  79.2 2.3 %slice_multiply_fusion.2 = (f32[22,38,134]{2,1,0:T(8,128)S(1)}, f32[22,38,134]{2,1,0:T(8,128)S(1)}, f32[22,38,134]{2,1,0:T(8,128)S(1)}, f32[22,38,134]{2,1,0:T(8,128)S(1)}) fusion(f32[24,40,136]{2,1,0:T(8,128)S(1)} %get-tuple-element.17, f32[24,40,136]{2,1,0:T(8,128)S(1)} %get-tuple-element.24, f32[24,40,136]{2,1,0:T(8,128)S(1)} %get-tuple-element.16, ...), kind=kLoop, calls=%fused_computation.34 | loop fusion | flops 2128456 | bytes 6273344 | tf_op jit(solution)/shard_map/mul | solution.py:41
  81.6 3.3 %slice_multiply_fusion.5 = (f32[20,36,132]{2,1,0:T(8,128)S(1)}, f32[20,36,132]{2,1,0:T(8,128)S(1)}, f32[20,36,132]{2,1,0:T(8,128)S(1)}, f32[20,36,132]{2,1,0:T(8,128)S(1)}) fusion(f32[24,40,136]{2,1,0:T(8,128)S(1)} %get-tuple-element.17, f32[24,40,136]{2,1,0:T(8,128)S(1)} %get-tuple-element.24, f32[22,38,134]{2,1,0:T(8,128)S(1)} %get-tuple-element.14, ...), kind=kLoop, calls=%fused_computation.55 | loop fusion | flops 2185920 | bytes 7983360 | tf_op jit(solution)/shard_map/mul | solution.py:41
  84.9 3.0 %slice_multiply_fusion.6 = (f32[18,34,130]{2,1,0:T(8,128)S(1)}, f32[18,34,130]{2,1,0:T(8,128)S(1)}, f32[18,34,130]{2,1,0:T(8,128)S(1)}, f32[18,34,130]{2,1,0:T(8,128)S(1)}) fusion(f32[24,40,136]{2,1,0:T(8,128)S(1)} %get-tuple-element.17, f32[24,40,136]{2,1,0:T(8,128)S(1)} %get-tuple-element.24, f32[20,36,132]{2,1,0:T(8,128)S(1)} %get-tuple-element.12, ...), kind=kLoop, calls=%fused_computation.56 | loop fusion | flops 1829880 | bytes 6683040 | tf_op jit(solution)/shard_map/mul | solution.py:41
  87.8 2.1 %fusion.22 = (f32[16,32,128]{2,1,0:T(8,128)}, f32[16,32,128]{2,1,0:T(8,128)}) fusion(f32[18,34,130]{2,1,0:T(8,128)S(1)} %get-tuple-element.18, f32[20,36,132]{2,1,0:T(8,128)S(1)} %get-tuple-element.21, f32[18,34,130]{2,1,0:T(8,128)S(1)} %get-tuple-element.19, f32[22,38,134]{2,1,0:T(8,128)S(1)} %get-tuple-element.15, ...), kind=kLoop, calls=%fused_computation.67 | loop fusion | flops 2686976 | bytes 6553600 | tf_op jit(solution)/shard_map/mul | solution.py:87
  (31 shorter events, 1.8 us)
Async XLA Ops:
  0.6 14.1 %copy-start.2 = (s32[16,32,128]{2,1,0:T(8,128)S(1)}, s32[16,32,128]{2,1,0:T(8,128)}, u32[]{:S(2)}) copy-start(s32[16,32,128]{2,1,0:T(8,128)} %param.5) | copy-start | bytes 786436
  1.6 41.7 %collective-permute-start = (f32[16,4,128]{2,1,0:T(4,128)S(1)}, f32[16,4,128]{2,1,0:T(4,128)S(1)}, u32[]{:S(2)}, u32[]{:S(2)}) collective-permute-start(f32[16,4,128]{2,1,0:T(4,128)S(1)} %get-tuple-element.37), channel_id=1, source_target_pairs={{0,8},{8,16},{16,24},{1,9},{9,17},{17,25},{2,10},{10,18},{18,26},{... | collective-permute-start | bytes 98312 | tf_op jit(solution)/shard_map/ppermute | solution.py:19
  6.5 38.0 %collective-permute-start.1 = (f32[16,4,128]{2,1,0:T(4,128)S(1)}, f32[16,4,128]{2,1,0:T(4,128)S(1)}, u32[]{:S(2)}, u32[]{:S(2)}) collective-permute-start(f32[16,4,128]{2,1,0:T(4,128)S(1)} %get-tuple-element.38), channel_id=1, source_target_pairs={{8,0},{16,8},{24,16},{9,1},{17,9},{25,17},{10,2},{18,10},{26,18},{... | collective-permute-start | bytes 98312 | tf_op jit(solution)/shard_map/ppermute | solution.py:20
  8.7 7.0 %collective-permute-start.12 = (f32[16,3,128]{2,1,0:T(4,128)S(1)}, f32[16,3,128]{2,1,0:T(4,128)S(1)}, u32[]{:S(2)}, u32[]{:S(2)}) collective-permute-start(f32[16,3,128]{2,1,0:T(4,128)S(1)} %get-tuple-element.39), channel_id=1, source_target_pairs={{0,8},{8,16},{16,24},{1,9},{9,17},{17,25},{2,10},{10,18},{18,26},{... | collective-permute-start | bytes 73736 | tf_op jit(solution)/shard_map/ppermute | solution.py:19
  13.3 6.0 %copy-start.1 = (f32[16,32,128]{2,1,0:T(8,128)S(1)}, f32[16,32,128]{2,1,0:T(8,128)}, u32[]{:S(2)}) copy-start(f32[16,32,128]{2,1,0:T(8,128)} %param.7) | copy-start | bytes 786436
  13.3 5.9 %collective-permute-start.13 = (f32[16,3,128]{2,1,0:T(4,128)S(1)}, f32[16,3,128]{2,1,0:T(4,128)S(1)}, u32[]{:S(2)}, u32[]{:S(2)}) collective-permute-start(f32[16,3,128]{2,1,0:T(4,128)S(1)} %get-tuple-element.40), channel_id=1, source_target_pairs={{8,0},{16,8},{24,16},{9,1},{17,9},{25,17},{10,2},{18,10},{26,18},{... | collective-permute-start | bytes 73736 | tf_op jit(solution)/shard_map/ppermute | solution.py:20
  19.4 8.4 %collective-permute-start.14 = (f32[16,38,3]{2,1,0:T(8,128)S(1)}, f32[16,38,3]{2,1,0:T(8,128)S(1)}, u32[]{:S(2)}, u32[]{:S(2)}) collective-permute-start(f32[16,38,3]{2,1,0:T(8,128)S(1)} %get-tuple-element.33), channel_id=1, source_target_pairs={{0,2},{2,4},{4,6},{1,3},{3,5},{5,7},{8,10},{10,12},{12,14},{9,11},... | collective-permute-start | bytes 21896 | tf_op jit(solution)/shard_map/ppermute | solution.py:19
  22.9 13.9 %collective-permute-start.15 = (f32[16,38,3]{2,1,0:T(8,128)S(1)}, f32[16,38,3]{2,1,0:T(8,128)S(1)}, u32[]{:S(2)}, u32[]{:S(2)}) collective-permute-start(f32[16,38,3]{2,1,0:T(8,128)S(1)} %get-tuple-element.34), channel_id=1, source_target_pairs={{2,0},{4,2},{6,4},{3,1},{5,3},{7,5},{10,8},{12,10},{14,12},{11,9},... | collective-permute-start | bytes 21896 | tf_op jit(solution)/shard_map/ppermute | solution.py:20
  24.2 14.1 %collective-permute-start.6 = (f32[16,4,128]{2,1,0:T(4,128)S(1)}, f32[16,4,128]{2,1,0:T(4,128)S(1)}, u32[]{:S(2)}, u32[]{:S(2)}) collective-permute-start(f32[16,4,128]{2,1,0:T(4,128)S(1)} %get-tuple-element.41), channel_id=1, source_target_pairs={{0,8},{8,16},{16,24},{1,9},{9,17},{17,25},{2,10},{10,18},{18,26},{... | collective-permute-start | bytes 98312 | tf_op jit(solution)/shard_map/ppermute | solution.py:19
  27.8 11.8 %collective-permute-start.7 = (f32[16,4,128]{2,1,0:T(4,128)S(1)}, f32[16,4,128]{2,1,0:T(4,128)S(1)}, u32[]{:S(2)}, u32[]{:S(2)}) collective-permute-start(f32[16,4,128]{2,1,0:T(4,128)S(1)} %get-tuple-element.42), channel_id=1, source_target_pairs={{8,0},{16,8},{24,16},{9,1},{17,9},{25,17},{10,2},{18,10},{26,18},{... | collective-permute-start | bytes 98312 | tf_op jit(solution)/shard_map/ppermute | solution.py:20
  37.0 42.2 %collective-permute-start.16 = (f32[3,38,134]{2,1,0:T(8,128)S(1)}, f32[3,38,134]{2,1,0:T(8,128)S(1)}, u32[]{:S(2)}, u32[]{:S(2)}) collective-permute-start(f32[3,38,134]{2,1,0:T(8,128)S(1)} %get-tuple-element.27), channel_id=1, source_target_pairs={{0,1},{2,3},{4,5},{6,7},{8,9},{10,11},{12,13},{14,15},{16,17},{18,... | collective-permute-start | bytes 183320 | tf_op jit(solution)/shard_map/ppermute | solution.py:19
  38.3 40.9 %collective-permute-start.17 = (f32[3,38,134]{2,1,0:T(8,128)S(1)}, f32[3,38,134]{2,1,0:T(8,128)S(1)}, u32[]{:S(2)}, u32[]{:S(2)}) collective-permute-start(f32[3,38,134]{2,1,0:T(8,128)S(1)} %get-tuple-element.28), channel_id=1, source_target_pairs={{1,0},{3,2},{5,4},{7,6},{9,8},{11,10},{13,12},{15,14},{17,16},{19,... | collective-permute-start | bytes 183320 | tf_op jit(solution)/shard_map/ppermute | solution.py:20
  39.7 4.9 %copy-start = (f32[16,32,128]{2,1,0:T(8,128)S(1)}, f32[16,32,128]{2,1,0:T(8,128)}, u32[]{:S(2)}) copy-start(f32[16,32,128]{2,1,0:T(8,128)} %param.6) | copy-start | bytes 786436
  39.8 11.3 %collective-permute-start.8 = (f32[16,40,4]{2,1,0:T(8,128)S(1)}, f32[16,40,4]{2,1,0:T(8,128)S(1)}, u32[]{:S(2)}, u32[]{:S(2)}) collective-permute-start(f32[16,40,4]{2,1,0:T(8,128)S(1)} %get-tuple-element.35), channel_id=1, source_target_pairs={{0,2},{2,4},{4,6},{1,3},{3,5},{5,7},{8,10},{10,12},{12,14},{9,11},... | collective-permute-start | bytes 30728 | tf_op jit(solution)/shard_map/ppermute | solution.py:19
  43.3 16.0 %collective-permute-start.9 = (f32[16,40,4]{2,1,0:T(8,128)S(1)}, f32[16,40,4]{2,1,0:T(8,128)S(1)}, u32[]{:S(2)}, u32[]{:S(2)}) collective-permute-start(f32[16,40,4]{2,1,0:T(8,128)S(1)} %get-tuple-element.36), channel_id=1, source_target_pairs={{2,0},{4,2},{6,4},{3,1},{5,3},{7,5},{10,8},{12,10},{14,12},{11,9},... | collective-permute-start | bytes 30728 | tf_op jit(solution)/shard_map/ppermute | solution.py:20
  44.8 16.7 %collective-permute-start.2 = (f32[16,40,4]{2,1,0:T(8,128)S(1)}, f32[16,40,4]{2,1,0:T(8,128)S(1)}, u32[]{:S(2)}, u32[]{:S(2)}) collective-permute-start(f32[16,40,4]{2,1,0:T(8,128)S(1)} %get-tuple-element.31), channel_id=1, source_target_pairs={{0,2},{2,4},{4,6},{1,3},{3,5},{5,7},{8,10},{10,12},{12,14},{9,11},... | collective-permute-start | bytes 30728 | tf_op jit(solution)/shard_map/ppermute | solution.py:19
  51.2 22.1 %collective-permute-start.3 = (f32[16,40,4]{2,1,0:T(8,128)S(1)}, f32[16,40,4]{2,1,0:T(8,128)S(1)}, u32[]{:S(2)}, u32[]{:S(2)}) collective-permute-start(f32[16,40,4]{2,1,0:T(8,128)S(1)} %get-tuple-element.32), channel_id=1, source_target_pairs={{2,0},{4,2},{6,4},{3,1},{5,3},{7,5},{10,8},{12,10},{14,12},{11,9},... | collective-permute-start | bytes 30728 | tf_op jit(solution)/shard_map/ppermute | solution.py:20
  59.5 16.0 %collective-permute-start.10 = (f32[4,40,136]{2,1,0:T(8,128)S(1)}, f32[4,40,136]{2,1,0:T(8,128)S(1)}, u32[]{:S(2)}, u32[]{:S(2)}) collective-permute-start(f32[4,40,136]{2,1,0:T(8,128)S(1)} %get-tuple-element.29), channel_id=1, source_target_pairs={{0,1},{2,3},{4,5},{6,7},{8,9},{10,11},{12,13},{14,15},{16,17},{18,... | collective-permute-start | bytes 261128 | tf_op jit(solution)/shard_map/ppermute | solution.py:19
  61.5 15.5 %collective-permute-start.11 = (f32[4,40,136]{2,1,0:T(8,128)S(1)}, f32[4,40,136]{2,1,0:T(8,128)S(1)}, u32[]{:S(2)}, u32[]{:S(2)}) collective-permute-start(f32[4,40,136]{2,1,0:T(8,128)S(1)} %get-tuple-element.30), channel_id=1, source_target_pairs={{1,0},{3,2},{5,4},{7,6},{9,8},{11,10},{13,12},{15,14},{17,16},{19,... | collective-permute-start | bytes 261128 | tf_op jit(solution)/shard_map/ppermute | solution.py:20
  73.5 3.9 %collective-permute-start.4 = (f32[4,40,136]{2,1,0:T(8,128)S(1)}, f32[4,40,136]{2,1,0:T(8,128)S(1)}, u32[]{:S(2)}, u32[]{:S(2)}) collective-permute-start(f32[4,40,136]{2,1,0:T(8,128)S(1)} %get-tuple-element.25), channel_id=1, source_target_pairs={{0,1},{2,3},{4,5},{6,7},{8,9},{10,11},{12,13},{14,15},{16,17},{18,... | collective-permute-start | bytes 261128 | tf_op jit(solution)/shard_map/ppermute | solution.py:19
  75.5 3.3 %collective-permute-start.5 = (f32[4,40,136]{2,1,0:T(8,128)S(1)}, f32[4,40,136]{2,1,0:T(8,128)S(1)}, u32[]{:S(2)}, u32[]{:S(2)}) collective-permute-start(f32[4,40,136]{2,1,0:T(8,128)S(1)} %get-tuple-element.26), channel_id=1, source_target_pairs={{1,0},{3,2},{5,4},{7,6},{9,8},{11,10},{13,12},{15,14},{17,16},{19,... | collective-permute-start | bytes 261128 | tf_op jit(solution)/shard_map/ppermute | solution.py:20
  84.9 3.0 %copy-start.3 = (f32[16,32,128]{2,1,0:T(8,128)S(1)}, f32[16,32,128]{2,1,0:T(8,128)}, u32[]{:S(2)}) copy-start(f32[16,32,128]{2,1,0:T(8,128)} %param.4) | copy-start | bytes 786436
where the time goes:
time: 90.6 us; the launch traced here: 89.9 us
  starting transfers between devices  41.5 us (46%)
  waiting for transfers between devices  31.8 us (35%)
  other arithmetic  13.3 us (15%)
  local copies, waits for them, and re-layouts  2.34 us (3%)
  between operations  1.01 us (1%)
    ppermute x9, waiting for transfers between devices, padded_2(): after = lax.ppermute(initial, axis, down)  29.9 us
    ppermute x9, starting transfers between devices, padded_2(): before = lax.ppermute(last, axis, up)  29.6 us
    ppermute x9, starting transfers between devices, padded_2(): after = lax.ppermute(initial, axis, down)  11.9 us
    mul x4, other arithmetic, forward_step(): spread = neighbours(outer_sea * padded)  9.01 us
    slice x6, local copies, waits for them, and re-layouts, padded_2(): last = lax.slice_in_dim(shard, length - width, length, axis=dim)  2.32 us
    mul x1, other arithmetic, body(): 2.0 * sea_local * jnp.exp(-2.0 * log_range) / diagonal * accumulated  2.09 us
    ppermute x9, waiting for transfers between devices, padded_2(): before = lax.ppermute(last, axis, up)  1.94 us
  transfers between devices with their start and end apart: 18, of which 7 were waited for; matrix products, arithmetic and copies ran while one was open for 4% of the time, Pallas kernels for 0%

commit v1 on v0

v1 whole, which is shorter than its diff:
```python
import functools

import jax
import jax.numpy as jnp
from jax import lax
from jax.experimental import pallas as pl
from jax.experimental.pallas import tpu as pltpu
from jax.sharding import PartitionSpec as P

SWEEPS = 4
RELAX = 0.9
KEEP = 1.0 - RELAX
SUB, LANES, DEPTH, GROUP = 8, 128, SWEEPS - 1, 6
AXES = ("gx", "gy", "gz")
ALL = slice(None)


def pair_swaps(sizes, axis, parity):
    nx, ny, nz = sizes
    pairs = []
    for i in range(nx):
        for j in range(ny):
            for k in range(nz):
                to = [i, j, k]
                other = to[axis] + (1 if to[axis] % 2 == parity else -1)
                if 0 <= other < sizes[axis]:
                    to[axis] = other
                else:
                    to[2] = 1 - k
                pairs.append(((i * ny + j) * nz + k, (to[0] * ny + to[1]) * nz + to[2]))
    return pairs


def iota(dim):
    return lax.broadcasted_iota(jnp.int32, (SUB, LANES), dim)


def level(t, lz):
    return jnp.where(lax.axis_index("gz") == 0, lz - 1 - t, t)


def prepare_kernel(lr, sea, src, cot, c_out, b_out, h_out, e_out, land_out, z_out):
    lz, lx, _ = lr.shape
    for t in range(lz):
        z = level(t, lz)
        for r in range(0, lx, SUB):
            rows = slice(r, r + SUB)
            wet = sea[z, rows, :] != 0
            decay = jnp.exp(-2.0 * lr[z, rows, :])
            c = jnp.where(wet, RELAX / (6.0 + decay), 0.0)
            f = src[z, rows, :]
            b = c * f
            h = c * cot[z, rows, :]
            c_out[t, rows, :] = c
            b_out[t, rows, :] = b
            h_out[t, rows, :] = h
            e_out[t, rows, :] = jnp.where(wet, (2.0 / RELAX) * decay, 0.0)
            land_out[t, rows, :] = jnp.where(
                wet, 0.0, RELAX * (1.0 + KEEP + KEEP**2 + KEEP**3) * f
            )
            if t < DEPTH:
                z_out[t, rows, :] = b
                z_out[DEPTH + t, rows, :] = h
            if t < DEPTH - 1:
                z_out[2 * DEPTH + t, rows, :] = c


def local_or_z(local, zin, base, depth, z):
    if z >= DEPTH:
        return local, z - DEPTH
    t = DEPTH - 1 - z
    return (zin, base + t) if t < depth else (None, 0)


def pack_x_kernel(c_in, b_in, h_in, zin, a_out, b_out):
    lz, lx, _ = c_in.shape
    odd = lax.axis_index("gx") % 2 == 1
    row = iota(0)
    for z in range(lz + DEPTH):
        faces = []
        for rows, s in ((slice(0, SUB), 1), (slice(lx - SUB, lx), -1)):
            br, bi = local_or_z(b_in, zin, 0, DEPTH, z)
            hr, hi = local_or_z(h_in, zin, DEPTH, DEPTH, z)
            cr, ci = local_or_z(c_in, zin, 2 * DEPTH, DEPTH - 1, z)
            b = br[bi, rows, :]
            h = hr[hi, rows, :]
            h = pltpu.roll(h, (s * DEPTH) % SUB, 0)
            if cr is None:
                c = jnp.zeros_like(b)
            else:
                c = pltpu.roll(cr[ci, rows, :], (s * 2 * DEPTH) % SUB, 0)
            at = row if s == 1 else SUB - 1 - row
            faces.append(jnp.where(at < DEPTH, b, jnp.where(at < 2 * DEPTH, h, c)))
        low, high = faces
        a_out[z] = jnp.where(odd, low, high)
        b_out[z] = jnp.where(odd, high, low)


def x_halo(a_in, b_in, z, index, size, row):
    odd = index % 2 == 1
    zero = jnp.zeros((SUB, LANES), jnp.float32)
    before = jnp.where(index > 0, jnp.where(odd, a_in[z], b_in[z]), zero)
    after = jnp.where(index < size - 1, jnp.where(odd, b_in[z], a_in[z]), zero)
    up = SUB - 1 - row

    def merge(depth, shift):
        lo = pltpu.roll(before, shift, 0) if shift else before
        hi = pltpu.roll(after, SUB - shift, 0) if shift else after
        return jnp.where(row < depth, hi, jnp.where(up < depth, lo, 0.0))

    return merge(DEPTH, 0), merge(DEPTH, DEPTH), merge(DEPTH - 1, 2 * DEPTH)


def place_of(lane, lz):
    group = lane // GROUP
    inside = group < lz + DEPTH - 1
    return jnp.where(inside, lane - GROUP * group, -1), jnp.where(inside, group, -1)


def turn(g):
    return (GROUP * g + DEPTH) % LANES


def pack_y_kernel(nx, c_in, b_in, h_in, zin, xa, xb, cm, bm, hm, pb_out, ph_out, ya, yb):
    lz, lx, _ = c_in.shape
    ix, iy = lax.axis_index("gx"), lax.axis_index("gy")
    row, lane = iota(0), iota(1)
    place, group = place_of(lane, lz)
    zero = jnp.zeros((SUB, LANES), jnp.float32)
    tiles = lx // SUB + 1
    halo = slice(SUB * tiles, SUB * (tiles + 1))
    acc = [[zero] * tiles for _ in range(3)]
    for z in range(lz + DEPTH):
        parts = x_halo(xa, xb, z, ix, nx, row)
        local = (
            local_or_z(b_in, zin, 0, DEPTH, z),
            local_or_z(h_in, zin, DEPTH, DEPTH, z),
            local_or_z(c_in, zin, 2 * DEPTH, DEPTH - 1, z),
        )
        for f, store in enumerate((bm, hm, cm)):
            ref, i = local[f]
            for t in range(tiles):
                if t == 0:
                    tile = parts[f]
                    store[z, halo, :] = tile
                else:
                    tile = zero if ref is None else ref[i, SUB * (t - 1) : SUB * t, :]
                store[z, SUB * t : SUB * (t + 1), :] = tile
                if z >= 1:
                    g = z - 1
                    acc[f][t] = jnp.where(
                        group == g, pltpu.roll(tile, turn(g), 1), acc[f][t]
                    )
    for store in (bm, hm, cm):
        for t in range(tiles + 1):
            store[lz + DEPTH, SUB * t : SUB * (t + 1), :] = zero
    odd = iy % 2 == 1
    for t in range(tiles):
        rows = slice(SUB * t, SUB * (t + 1))
        pb, ph, pc = acc[0][t], acc[1][t], acc[2][t]
        pb_out[rows, :] = pb
        ph_out[rows, :] = ph
        upper = jnp.where(place < DEPTH, pb, pltpu.roll(ph, DEPTH, 1))
        lower = jnp.where(place >= DEPTH, pb, pltpu.roll(ph, LANES - DEPTH, 1))
        ya[0, rows, :] = jnp.where(odd, lower, upper)
        yb[0, rows, :] = jnp.where(odd, upper, lower)
        ya[1, rows, :] = pc
        yb[1, rows, :] = pc


def sweep_kernel(
    ny, cm, bm, hm, pb, ph, ya, yb, e_in, land_in, it_out, rg_out,
    y1, y2, h1, h2, sb, sh, sc, sy1, sy2, sh1, sh2,
):
    lz, lx, _ = e_in.shape
    iy = lax.axis_index("gy")
    lane = iota(1)
    place, group = place_of(lane, lz)
    tiles = lx // SUB + 1
    halo = slice(SUB * tiles, SUB * (tiles + 1))
    zero = jnp.zeros((SUB, LANES), jnp.float32)
    first, last = lane == 0, lane == LANES - 1
    inner = (place == DEPTH - 1) | (place == DEPTH)
    in_group = jnp.where(inner, group, -1)
    below, above = place == DEPTH - 1, place == DEPTH
    odd = iy % 2 == 1

    def put(ref, t, value):
        ref[SUB * t : SUB * (t + 1), :] = value
        if t == 0:
            ref[halo, :] = value

    for t in range(tiles):
        rows = slice(SUB * t, SUB * (t + 1))
        got = []
        for k in range(2):
            a, b = ya[k, rows, :], yb[k, rows, :]
            got.append(
                (
                    jnp.where(iy > 0, jnp.where(odd, a, b), zero),
                    jnp.where(iy < ny - 1, jnp.where(odd, b, a), zero),
                )
            )
        (lo, hi), (lo_c, hi_c) = got
        near, far = (place >= 0) & (place < DEPTH), place >= DEPTH
        put(sb, t, jnp.where(near, lo, jnp.where(far, hi, 0.0)))
        put(
            sh, t,
            jnp.where(
                near, pltpu.roll(lo, LANES - DEPTH, 1),
                jnp.where(far, pltpu.roll(hi, DEPTH, 1), 0.0),
            ),
        )
        put(sc, t, jnp.where(near, lo_c, jnp.where(far, hi_c, 0.0)))

    def shifted(ref, t, pre=()):
        at = SUB * (tiles if t == 0 else t)
        minus = ref[pre + (slice(at - 1, at - 1 + SUB), ALL)]
        plus = ref[pre + (slice(SUB * t + 1, SUB * t + 1 + SUB), ALL)]
        return minus, plus

    def spread(v, strip, edge_tiles, z, t):
        rows = slice(SUB * t, SUB * (t + 1))
        here = v[z, rows, :]
        minus, plus = shifted(v, t, (z,))
        edge = pltpu.roll(edge_tiles[t], LANES - turn(z - 1), 1)
        left = pltpu.roll(jnp.where(last, edge, here), 1, 1)
        right = pltpu.roll(jnp.where(first, edge, here), LANES - 1, 1)
        return (v[z - 1, rows, :] + v[z + 1, rows, :]) + (minus + plus) + (left + right), here

    def strip_step(v, extra, source, out, ends):
        for t in range(tiles):
            rows = slice(SUB * t, SUB * (t + 1))
            here = v[rows, :]
            minus, plus = shifted(v, t)
            end = ends(t)
            near = pltpu.roll(jnp.where(above, end, here), LANES - 1, 1)
            far = pltpu.roll(jnp.where(below, end, here), 1, 1)
            total = (minus + plus) + (near + far)
            total = total + (pltpu.roll(here, GROUP, 1) + pltpu.roll(here, LANES - GROUP, 1))
            value = KEEP * here + sc[rows, :] * total
            if source is not None:
                value = value + source[rows, :]
            put(out, t, value)

    def step(v, strip, source, out, start, collect):
        ends = []
        edge_tiles = [strip[SUB * t : SUB * (t + 1), :] for t in range(tiles)]
        for t in range(tiles):
            rows = slice(SUB * t, SUB * (t + 1))
            end = zero
            for z in range(start, lz + DEPTH):
                total, here = spread(v, strip, edge_tiles, z, t)
                value = cm[z, rows, :] * total
                if source is not None:
                    value = source[z, rows, :] + value
                value = KEEP * here + value
                out[z, rows, :] = value
                if t == 0:
                    out[z, halo, :] = value
                if collect:
                    g = z - 1
                    end = jnp.where(in_group == g, pltpu.roll(value, turn(g), 1), end)
            ends.append(end)
        for ref in (out,):
            for t in range(tiles + 1):
                ref[lz + DEPTH, SUB * t : SUB * (t + 1), :] = zero
        return ends

    strip_step(sb, None, sb, sy1, lambda t: pb[SUB * t : SUB * (t + 1), :])
    strip_step(sh, None, None, sh1, lambda t: ph[SUB * t : SUB * (t + 1), :])
    ends_h = step(hm, sh, None, h1, 1, True)
    ends_y = step(bm, sb, bm, y1, 1, True)
    strip_step(sh1, None, None, sh2, lambda t: ends_h[t])
    strip_step(sy1, None, sb, sy2, lambda t: ends_y[t])
    step(h1, sh1, None, h2, 2, False)
    step(y1, sy1, bm, y2, 2, False)
    edge_h = [sh2[SUB * t : SUB * (t + 1), :] for t in range(tiles)]
    edge_y = [sy2[SUB * t : SUB * (t + 1), :] for t in range(tiles)]
    for t in range(1, tiles):
        rows, block = slice(SUB * t, SUB * (t + 1)), slice(SUB * (t - 1), SUB * t)
        for z in range(DEPTH, lz + DEPTH):
            k = z - DEPTH
            c, b = cm[z, rows, :], bm[z, rows, :]
            total_h, g2 = spread(h2, sh2, edge_h, z, t)
            total_y, x3 = spread(y2, sy2, edge_y, z, t)
            g1 = KEEP * g2 + c * total_h
            w3 = b + c * total_y
            x2 = y1[z, rows, :]
            w2 = x3 - KEEP * x2
            w1 = x2 - KEEP * b
            s = (g1 * b + g2 * w1) + (h1[z, rows, :] * w2 + hm[z, rows, :] * w3)
            out = level(k, lz)
            it_out[out, block, :] = (KEEP * x3 + w3) + land_in[k, block, :]
            rg_out[out, block, :] = e_in[k, block, :] * s


def body(nx, ny, log_range, sea_mask, forcing, cotangent):
    lz, lx, ly = forcing.shape
    f32 = jnp.float32
    sizes = (nx, ny, 2)
    vmem = pl.BlockSpec(memory_space=pltpu.VMEM)
    params = pltpu.CompilerParams(vmem_limit_bytes=32 * 2**20)

    def call(kernel, shapes, args, name, scratch=(), flops=1):
        return pl.pallas_call(
            kernel,
            out_shape=[jax.ShapeDtypeStruct(s, f32) for s in shapes],
            in_specs=[vmem] * len(args),
            out_specs=[vmem] * len(shapes),
            scratch_shapes=[pltpu.VMEM(s, f32) for s in scratch],
            compiler_params=params,
            cost_estimate=pl.CostEstimate(flops=flops, bytes_accessed=2**20, transcendentals=0),
            name=name,
        )(*args)

    block = (lz, lx, ly)
    store = (lz + DEPTH + 1, lx + 2 * SUB, ly)
    strip = (lx + 2 * SUB, LANES)
    packed = (lx + SUB, LANES)
    c, b, h, e, land, zmsg = call(
        prepare_kernel,
        [block] * 5 + [(3 * DEPTH - 1, lx, ly)],
        (log_range, sea_mask, forcing, cotangent),
        "prepare",
    )
    swap = [(d, d ^ 1) for d in range(2 * nx * ny)]
    zin = lax.ppermute(zmsg, AXES, swap)
    xa, xb = call(pack_x_kernel, [(lz + DEPTH, SUB, ly)] * 2, (c, b, h, zin), "pack_x")
    xa = lax.ppermute(xa, AXES, pair_swaps(sizes, 0, 0))
    xb = lax.ppermute(xb, AXES, pair_swaps(sizes, 0, 1))
    cm, bm, hm, pb, ph, ya, yb = call(
        functools.partial(pack_y_kernel, nx),
        [store] * 3 + [packed] * 2 + [(2,) + packed] * 2,
        (c, b, h, zin, xa, xb),
        "pack_y",
    )
    ya = lax.ppermute(ya, AXES, pair_swaps(sizes, 1, 0))
    yb = lax.ppermute(yb, AXES, pair_swaps(sizes, 1, 1))
    return call(
        functools.partial(sweep_kernel, ny),
        [block] * 2,
        (cm, bm, hm, pb, ph, ya, yb, e, land),
        "sweep",
        [store] * 4 + [strip] * 7,
    )


def solution(mesh):
    nx, ny = mesh.shape["gx"], mesh.shape["gy"]
    spec = P("gz", "gx", "gy")
    return jax.shard_map(
        lambda *args: tuple(body(nx, ny, *args)),
        mesh=mesh,
        in_specs=(spec,) * 4,
        out_specs=(spec,) * 2,
        check_vma=False,
    )
```

time: 90.6 us -> 50.6 us (0.56)
  the two profiles are of different devices: /device:TPU:0 before, /device:TPU:20 now
where the time goes in v1:
time: 50.6 us; the launch traced here: 50.3 us
  Pallas kernels  32 us (63%)
  waiting for transfers between devices  10.2 us (20%)
  local copies, waits for them, and re-layouts  3.79 us (7%)
  starting transfers between devices  3.75 us (7%)
  between operations  0.67 us (1%)
    pallas_call x4, Pallas kernels, call(): pl.pallas_call(kernel, out_shape=[jax.ShapeDtypeStruct(s, f32) for s in s...  32 us
    unnamed x8, local copies, waits for them, and re-layouts  3.79 us
    ppermute x1, waiting for transfers between devices, body(): xa = lax.ppermute(xa, AXES, pair_swaps(sizes, 0, 0))  2.83 us
    ppermute x1, waiting for transfers between devices, body(): yb = lax.ppermute(yb, AXES, pair_swaps(sizes, 1, 1))  2.39 us
    ppermute x1, waiting for transfers between devices, body(): ya = lax.ppermute(ya, AXES, pair_swaps(sizes, 1, 0))  2.03 us
    ppermute x1, starting transfers between devices, body(): xa = lax.ppermute(xa, AXES, pair_swaps(sizes, 0, 0))  1.64 us
    ppermute x1, waiting for transfers between devices, body(): xb = lax.ppermute(xb, AXES, pair_swaps(sizes, 0, 1))  1.56 us
    ppermute x1, starting transfers between devices, body(): ya = lax.ppermute(ya, AXES, pair_swaps(sizes, 1, 0))  1.56 us
  transfers between devices with their start and end apart: 5, of which 5 were waited for; matrix products, arithmetic and copies ran while one was open for 0% of the time, Pallas kernels for 0%

profile of v1, /device:TPU:20, one launch (start us, length us, event | category | flops | bytes accessed | tf_op | source)
XLA Modules:
  0.0 50.3 jit_solution(12947148020589955694)
XLA Ops:
  0.6 0.0 copy-start
  0.6 0.9 %copy-done = f32[16,32,128]{2,1,0:T(8,128)S(1)} copy-done((f32[16,32,128]{2,1,0:T(8,128)S(1)}, f32[16,32,128]{2,1,0:T(8,128)}, u32[]{:S(2)}) %copy-start) | copy-done | bytes 262168
  1.6 0.0 copy-start.1
  1.6 0.9 %copy-done.1 = s32[16,32,128]{2,1,0:T(8,128)S(1)} copy-done((s32[16,32,128]{2,1,0:T(8,128)S(1)}, s32[16,32,128]{2,1,0:T(8,128)}, u32[]{:S(2)}) %copy-start.1) | copy-done | bytes 262168
  2.5 0.0 copy-start.2
  2.5 0.9 %copy-done.2 = f32[16,32,128]{2,1,0:T(8,128)S(1)} copy-done((f32[16,32,128]{2,1,0:T(8,128)S(1)}, f32[16,32,128]{2,1,0:T(8,128)}, u32[]{:S(2)}) %copy-start.2) | copy-done | bytes 262168
  3.5 0.0 copy-start.3
  3.5 0.9 %copy-done.3 = f32[16,32,128]{2,1,0:T(8,128)S(1)} copy-done((f32[16,32,128]{2,1,0:T(8,128)S(1)}, f32[16,32,128]{2,1,0:T(8,128)}, u32[]{:S(2)}) %copy-start.3) | copy-done | bytes 262168
  4.4 0.1 prepare.1
  4.6 0.1 collective-permute-start
  4.7 1.3 %collective-permute-done.zin = f32[8,32,128]{2,1,0:T(8,128)S(1)} collective-permute-done((f32[8,32,128]{2,1,0:T(8,128)S(1)}, f32[8,32,128]{2,1,0:T(8,128)S(1)}, u32[]{:S(2)}, u32[]{:S(2)}) %collective-permute-start) | collective-permute-done | bytes 131104 | tf_op jit(solution)/shard_map/ppermute | solution.py:328
  6.0 1.6 %collective-permute-start.1 = (f32[19,8,128]{2,1,0:T(8,128)S(1)}, f32[19,8,128]{2,1,0:T(8,128)S(1)}, u32[]{:S(2)}, u32[]{:S(2)}) collective-permute-start(f32[19,8,128]{2,1,0:T(8,128)S(1)} %get-tuple-element.21), channel_id=1, source_target_pairs={{0,8},{1,9},{2,10},{3,11},{4,12},{5,13},{6,14},{7,15},{8,0},{9,1},... | collective-permute-start | bytes 233480 | tf_op jit(solution)/shard_map/ppermute | solution.py:330
  7.7 0.0 collective-permute-start.2
  7.7 2.8 %collective-permute-done.1.xa = f32[19,8,128]{2,1,0:T(8,128)S(1)} collective-permute-done((f32[19,8,128]{2,1,0:T(8,128)S(1)}, f32[19,8,128]{2,1,0:T(8,128)S(1)}, u32[]{:S(2)}, u32[]{:S(2)}) %collective-permute-start.1) | collective-permute-done | bytes 77856 | tf_op jit(solution)/shard_map/ppermute | solution.py:330
  10.5 1.6 %collective-permute-done.2.xb = f32[19,8,128]{2,1,0:T(8,128)S(1)} collective-permute-done((f32[19,8,128]{2,1,0:T(8,128)S(1)}, f32[19,8,128]{2,1,0:T(8,128)S(1)}, u32[]{:S(2)}, u32[]{:S(2)}) %collective-permute-start.2) | collective-permute-done | bytes 77856 | tf_op jit(solution)/shard_map/ppermute | solution.py:331
  12.1 0.4 pack_y.1
  12.5 1.6 %collective-permute-start.3 = (f32[2,40,128]{2,1,0:T(8,128)S(1)}, f32[2,40,128]{2,1,0:T(8,128)S(1)}, u32[]{:S(2)}, u32[]{:S(2)}) collective-permute-start(f32[2,40,128]{2,1,0:T(8,128)S(1)} %get-tuple-element.28), channel_id=1, source_target_pairs={{0,2},{1,3},{2,0},{3,1},{4,6},{5,7},{6,4},{7,5},{8,10},{9,11},{10,... | collective-permute-start | bytes 122888 | tf_op jit(solution)/shard_map/ppermute | solution.py:338
  14.0 0.5 collective-permute-start.4
  14.5 2.0 %collective-permute-done.3.ya = f32[2,40,128]{2,1,0:T(8,128)S(1)} collective-permute-done((f32[2,40,128]{2,1,0:T(8,128)S(1)}, f32[2,40,128]{2,1,0:T(8,128)S(1)}, u32[]{:S(2)}, u32[]{:S(2)}) %collective-permute-start.3) | collective-permute-done | bytes 40992 | tf_op jit(solution)/shard_map/ppermute | solution.py:338
  16.5 2.4 %collective-permute-done.4.yb = f32[2,40,128]{2,1,0:T(8,128)S(1)} collective-permute-done((f32[2,40,128]{2,1,0:T(8,128)S(1)}, f32[2,40,128]{2,1,0:T(8,128)S(1)}, u32[]{:S(2)}, u32[]{:S(2)}) %collective-permute-start.4) | collective-permute-done | bytes 40992 | tf_op jit(solution)/shard_map/ppermute | solution.py:339
  18.9 31.4 %sweep.1 = (f32[16,32,128]{2,1,0:T(8,128)}, f32[16,32,128]{2,1,0:T(8,128)}) custom-call(f32[20,48,128]{2,1,0:T(8,128)S(1)} %get-tuple-element.23.cm, f32[20,48,128]{2,1,0:T(8,128)S(1)} %get-tuple-element.24.bm, f32[20,48,128]{2,1,0:T(8,128)S(1)} %get-tuple-element.25.hm, f32[40,128]{1,0:T(8,128)S(1)} %get-tuple-element.26.pb, ...), custom_call_target="tpu_custom_call" | custom-call | flops 1 | bytes 1048576 | tf_op jit(solution)/shard_map/sweep/pallas_call | solution.py:306
  (1 shorter events, 0.0 us)
Async XLA Ops:
  0.6 1.0 %copy-start = (f32[16,32,128]{2,1,0:T(8,128)S(1)}, f32[16,32,128]{2,1,0:T(8,128)}, u32[]{:S(2)}) copy-start(f32[16,32,128]{2,1,0:T(8,128)} %lr.1) | copy-start | bytes 786436
  1.6 0.9 %copy-start.1 = (s32[16,32,128]{2,1,0:T(8,128)S(1)}, s32[16,32,128]{2,1,0:T(8,128)}, u32[]{:S(2)}) copy-start(s32[16,32,128]{2,1,0:T(8,128)} %sea.1) | copy-start | bytes 786436
  2.5 0.9 %copy-start.2 = (f32[16,32,128]{2,1,0:T(8,128)S(1)}, f32[16,32,128]{2,1,0:T(8,128)}, u32[]{:S(2)}) copy-start(f32[16,32,128]{2,1,0:T(8,128)} %src.1) | copy-start | bytes 786436
  3.5 0.9 %copy-start.3 = (f32[16,32,128]{2,1,0:T(8,128)S(1)}, f32[16,32,128]{2,1,0:T(8,128)}, u32[]{:S(2)}) copy-start(f32[16,32,128]{2,1,0:T(8,128)} %cot.1) | copy-start | bytes 786436
  4.6 1.4 %collective-permute-start = (f32[8,32,128]{2,1,0:T(8,128)S(1)}, f32[8,32,128]{2,1,0:T(8,128)S(1)}, u32[]{:S(2)}, u32[]{:S(2)}) collective-permute-start(f32[8,32,128]{2,1,0:T(8,128)S(1)} %get-tuple-element.20), channel_id=1, source_target_pairs={{0,1},{1,0},{2,3},{3,2},{4,5},{5,4},{6,7},{7,6},{8,9},{9,8},{10,11... | collective-permute-start | bytes 393224 | tf_op jit(solution)/shard_map/ppermute | solution.py:328
  6.0 4.5 %collective-permute-start.1 = (f32[19,8,128]{2,1,0:T(8,128)S(1)}, f32[19,8,128]{2,1,0:T(8,128)S(1)}, u32[]{:S(2)}, u32[]{:S(2)}) collective-permute-start(f32[19,8,128]{2,1,0:T(8,128)S(1)} %get-tuple-element.21), channel_id=1, source_target_pairs={{0,8},{1,9},{2,10},{3,11},{4,12},{5,13},{6,14},{7,15},{8,0},{9,1},... | collective-permute-start | bytes 233480 | tf_op jit(solution)/shard_map/ppermute | solution.py:330
  7.7 4.4 %collective-permute-start.2 = (f32[19,8,128]{2,1,0:T(8,128)S(1)}, f32[19,8,128]{2,1,0:T(8,128)S(1)}, u32[]{:S(2)}, u32[]{:S(2)}) collective-permute-start(f32[19,8,128]{2,1,0:T(8,128)S(1)} %get-tuple-element.22), channel_id=1, source_target_pairs={{0,1},{1,0},{2,3},{3,2},{4,5},{5,4},{6,7},{7,6},{8,16},{9,17},{10,... | collective-permute-start | bytes 233480 | tf_op jit(solution)/shard_map/ppermute | solution.py:331
  12.5 4.1 %collective-permute-start.3 = (f32[2,40,128]{2,1,0:T(8,128)S(1)}, f32[2,40,128]{2,1,0:T(8,128)S(1)}, u32[]{:S(2)}, u32[]{:S(2)}) collective-permute-start(f32[2,40,128]{2,1,0:T(8,128)S(1)} %get-tuple-element.28), channel_id=1, source_target_pairs={{0,2},{1,3},{2,0},{3,1},{4,6},{5,7},{6,4},{7,5},{8,10},{9,11},{10,... | collective-permute-start | bytes 122888 | tf_op jit(solution)/shard_map/ppermute | solution.py:338
  14.0 4.9 %collective-permute-start.4 = (f32[2,40,128]{2,1,0:T(8,128)S(1)}, f32[2,40,128]{2,1,0:T(8,128)S(1)}, u32[]{:S(2)}, u32[]{:S(2)}) collective-permute-start(f32[2,40,128]{2,1,0:T(8,128)S(1)} %get-tuple-element.29), channel_id=1, source_target_pairs={{0,1},{1,0},{2,4},{3,5},{4,2},{5,3},{6,7},{7,6},{8,9},{9,8},{10,12... | collective-permute-start | bytes 122888 | tf_op jit(solution)/shard_map/ppermute | solution.py:339

commit v2 on v1

v2 whole, which is shorter than its diff:
```python
import functools

import jax
import jax.numpy as jnp
from jax import lax
from jax.experimental import pallas as pl
from jax.experimental.pallas import tpu as pltpu
from jax.sharding import PartitionSpec as P

SWEEPS = 4
RELAX = 0.9
KEEP = 1.0 - RELAX
SUB, LANES, DEPTH = 8, 128, SWEEPS - 1
OWN = 2 * DEPTH
GROUP = 2 * (OWN + DEPTH)
STRIDE = 3
AXES = ("gx", "gy", "gz")
ALL = slice(None)


def pair_swaps(sizes, axis, parity):
    nx, ny, nz = sizes
    pairs = []
    for i in range(nx):
        for j in range(ny):
            for k in range(nz):
                to = [i, j, k]
                other = to[axis] + (1 if to[axis] % 2 == parity else -1)
                if 0 <= other < sizes[axis]:
                    to[axis] = other
                else:
                    to[2] = 1 - k
                pairs.append(((i * ny + j) * nz + k, (to[0] * ny + to[1]) * nz + to[2]))
    return pairs


def iota(dim):
    return lax.broadcasted_iota(jnp.int32, (SUB, LANES), dim)


def level(t, lz):
    return jnp.where(lax.axis_index("gz") == 0, lz - 1 - t, t)


def tile_rows(t):
    return slice(SUB * t, SUB * (t + 1))


def prepare_kernel(lr_h, sea_h, src_h, cot_h, c_out, b_out, h_out, e_out, land_out, z_out,
                   lr, sea, src, cot, sem):
    lz, lx, _ = lr.shape
    copies = [
        pltpu.make_async_copy(a, b, sem.at[i])
        for i, (a, b) in enumerate(((lr_h, lr), (sea_h, sea), (src_h, src), (cot_h, cot)))
    ]
    for copy in copies:
        copy.start()
    for copy in copies:
        copy.wait()
    for t in range(lz):
        z = level(t, lz)
        for r in range(0, lx, SUB):
            rows = slice(r, r + SUB)
            wet = sea[z, rows, :] != 0
            decay = jnp.exp(-2.0 * lr[z, rows, :])
            c = jnp.where(wet, RELAX / (6.0 + decay), 0.0)
            f = src[z, rows, :]
            b = c * f
            h = c * cot[z, rows, :]
            c_out[t, rows, :] = c
            b_out[t, rows, :] = b
            h_out[t, rows, :] = h
            e_out[t, rows, :] = jnp.where(wet, (2.0 / RELAX) * decay, 0.0)
            land_out[t, rows, :] = jnp.where(
                wet, 0.0, RELAX * (1.0 + KEEP + KEEP**2 + KEEP**3) * f
            )
            if t < DEPTH:
                z_out[t, rows, :] = b
                z_out[DEPTH + t, rows, :] = h
            if t < DEPTH - 1:
                z_out[2 * DEPTH + t, rows, :] = c


def local_or_z(local, zin, base, depth, z):
    if z >= DEPTH:
        return local, z - DEPTH
    t = DEPTH - 1 - z
    return (zin, base + t) if t < depth else (None, 0)


def pack_x_kernel(c_in, b_in, h_in, zin, a_out, b_out):
    lz, lx, _ = c_in.shape
    odd = lax.axis_index("gx") % 2 == 1
    row = iota(0)
    for z in range(lz + DEPTH):
        faces = []
        for rows, s in ((slice(0, SUB), 1), (slice(lx - SUB, lx), -1)):
            br, bi = local_or_z(b_in, zin, 0, DEPTH, z)
            hr, hi = local_or_z(h_in, zin, DEPTH, DEPTH, z)
            cr, ci = local_or_z(c_in, zin, 2 * DEPTH, DEPTH - 1, z)
            b = br[bi, rows, :]
            h = hr[hi, rows, :]
            h = pltpu.roll(h, (s * DEPTH) % SUB, 0)
            if cr is None:
                c = jnp.zeros_like(b)
            else:
                c = pltpu.roll(cr[ci, rows, :], (s * 2 * DEPTH) % SUB, 0)
            at = row if s == 1 else SUB - 1 - row
            faces.append(jnp.where(at < DEPTH, b, jnp.where(at < 2 * DEPTH, h, c)))
        low, high = faces
        a_out[z] = jnp.where(odd, low, high)
        b_out[z] = jnp.where(odd, high, low)


def x_halo(a_in, b_in, z, index, size, row):
    odd = index % 2 == 1
    zero = jnp.zeros((SUB, LANES), jnp.float32)
    before = jnp.where(index > 0, jnp.where(odd, a_in[z], b_in[z]), zero)
    after = jnp.where(index < size - 1, jnp.where(odd, b_in[z], a_in[z]), zero)
    up = SUB - 1 - row

    def merge(depth, shift):
        lo = pltpu.roll(before, shift, 0) if shift else before
        hi = pltpu.roll(after, SUB - shift, 0) if shift else after
        return jnp.where(row < depth, hi, jnp.where(up < depth, lo, 0.0))

    return merge(DEPTH, 0), merge(DEPTH, DEPTH), merge(DEPTH - 1, 2 * DEPTH)


def packed_place(lane, lz):
    group = lane // GROUP
    inside = group < -(-(lz + DEPTH) // STRIDE)
    return jnp.where(inside, group, -1), jnp.where(inside, lane - GROUP * group, -1)


def pack_y_kernel(nx, c_in, b_in, h_in, zin, xa, xb, cm, bm, hm, pc_out, pb_out, ph_out, ya, yb):
    lz, lx, _ = c_in.shape
    ix, iy = lax.axis_index("gx"), lax.axis_index("gy")
    row, lane = iota(0), iota(1)
    group, place = packed_place(lane, lz)
    zero = jnp.zeros((SUB, LANES), jnp.float32)
    tiles = lx // SUB + 1
    halo = tile_rows(tiles)
    acc = [[[zero] * tiles for _ in range(STRIDE)] for _ in range(3)]
    raw = jnp.where(place < 2 * OWN, group, -1)
    for z in range(lz + DEPTH):
        parts = x_halo(xa, xb, z, ix, nx, row)
        local = (
            local_or_z(c_in, zin, 2 * DEPTH, DEPTH - 1, z),
            local_or_z(b_in, zin, 0, DEPTH, z),
            local_or_z(h_in, zin, DEPTH, DEPTH, z),
        )
        for f, store in enumerate((cm, bm, hm)):
            ref, i = local[f]
            for t in range(tiles):
                if t == 0:
                    tile = parts[(f + 2) % 3]
                    store[z, halo, :] = tile
                else:
                    tile = zero if ref is None else ref[i, tile_rows(t - 1), :]
                store[z, tile_rows(t), :] = tile
                if f or z:
                    g, v = z // STRIDE, z % STRIDE
                    acc[f][v][t] = jnp.where(
                        raw == g, pltpu.roll(tile, (GROUP * g + OWN) % LANES, 1), acc[f][v][t]
                    )
    for store in (cm, bm, hm):
        for t in range(tiles + 1):
            store[lz + DEPTH, tile_rows(t), :] = zero
    odd = iy % 2 == 1
    for v in range(STRIDE):
        for t in range(tiles):
            rows = tile_rows(t)
            own = []
            for f in range(3):
                a = acc[f][v][t]
                moved = pltpu.roll(a, GROUP - 2 * OWN, 1)
                own.append(
                    jnp.where(place < OWN, a, jnp.where(place >= GROUP - OWN, moved, 0.0))
                )
            for ref, a in zip((pc_out, pb_out, ph_out), own):
                ref[v, rows, :] = a
            c, b, h = (acc[f][v][t] for f in range(3))
            first, last = OWN, DEPTH
            upper = jnp.where(
                place < DEPTH, pltpu.roll(b, LANES - last, 1),
                jnp.where(place < 2 * DEPTH, h, pltpu.roll(c, 2 * DEPTH - last, 1)),
            )
            lower = jnp.where(
                place < DEPTH, pltpu.roll(b, LANES - first, 1),
                jnp.where(place < 2 * DEPTH, pltpu.roll(h, LANES + DEPTH - first, 1), c),
            )
            ya[v, rows, :] = jnp.where(odd, lower, upper)
            yb[v, rows, :] = jnp.where(odd, upper, lower)


def main_kernel(cm, bm, hm, it_out, s_out, y1, y2, h1, h2):
    lz, lx, _ = it_out.shape
    tiles = lx // SUB + 1
    halo = tile_rows(tiles)
    zero = jnp.zeros((SUB, LANES), jnp.float32)

    def spread(v, z, t):
        rows = tile_rows(t)
        here = v[z, rows, :]
        at = SUB * (tiles if t == 0 else t) - 1
        total = v[z, at : at + SUB, :] + v[z, SUB * t + 1 : SUB * t + 1 + SUB, :]
        total = total + (v[z - 1, rows, :] + v[z + 1, rows, :])
        sides = pltpu.roll(here, 1, 1) + pltpu.roll(here, LANES - 1, 1)
        return total + sides, here

    def step(v, source, out, start):
        for z in range(start, lz + DEPTH):
            for t in range(tiles):
                rows = tile_rows(t)
                total, here = spread(v, z, t)
                value = cm[z, rows, :] * total
                if source is not None:
                    value = source[z, rows, :] + value
                value = KEEP * here + value
                out[z, rows, :] = value
                if t == 0:
                    out[z, halo, :] = value
        for t in range(tiles + 1):
            out[lz + DEPTH, tile_rows(t), :] = zero

    step(hm, None, h1, 1)
    step(bm, bm, y1, 1)
    step(h1, None, h2, 2)
    step(y1, bm, y2, 2)
    for z in range(DEPTH, lz + DEPTH):
        for t in range(1, tiles):
            rows, block = tile_rows(t), tile_rows(t - 1)
            k = z - DEPTH
            c, b = cm[z, rows, :], bm[z, rows, :]
            total_h, g2 = spread(h2, z, t)
            total_y, x3 = spread(y2, z, t)
            x2 = y1[z, rows, :]
            g1 = KEEP * g2 + c * total_h
            w3 = b + c * total_y
            it_out[k, block, :] = KEEP * x3 + w3
            s_out[k, block, :] = (g1 * b + g2 * (x2 - KEEP * b)) + (
                h1[z, rows, :] * (x3 - KEEP * x2) + hm[z, rows, :] * w3
            )


def edge_kernel(ny, pc, pb, ph, ya, yb, it_in, s_in, e_in, land_in, it_hbm, rg_hbm,
                cs, bs, hs, y1, y2, h1, h2, it_out, rg_out, sem):
    lz, lx, _ = e_in.shape
    iy = lax.axis_index("gy")
    lane = iota(1)
    group, place = packed_place(lane, lz)
    tiles = lx // SUB + 1
    halo = tile_rows(tiles)
    zero = jnp.zeros((SUB, LANES), jnp.float32)
    odd = iy % 2 == 1
    after = (place >= OWN) & (place < OWN + DEPTH)
    before = (place >= OWN + DEPTH) & (place < OWN + 2 * DEPTH)

    def put(ref, v, t, value):
        ref[v, tile_rows(t), :] = value
        if t == 0:
            ref[v, halo, :] = value

    for v in range(STRIDE):
        for t in range(tiles):
            rows = tile_rows(t)
            a, b = ya[v, rows, :], yb[v, rows, :]
            lo = jnp.where(iy > 0, jnp.where(odd, a, b), zero)
            hi = jnp.where(iy < ny - 1, jnp.where(odd, b, a), zero)
            for k, (ref, own) in enumerate(((bs, pb), (hs, ph), (cs, pc))):
                from_lo = pltpu.roll(lo, (OWN + DEPTH - k * DEPTH) % LANES, 1)
                from_hi = pltpu.roll(hi, (OWN - k * DEPTH) % LANES, 1) if k != 2 else hi
                put(ref, v, t,
                    jnp.where(before, from_lo, jnp.where(after, from_hi, own[v, rows, :])))

    def spread(ref, v, t):
        rows = tile_rows(t)
        here = ref[v, rows, :]
        at = SUB * (tiles if t == 0 else t) - 1
        total = ref[v, at : at + SUB, :] + ref[v, SUB * t + 1 : SUB * t + 1 + SUB, :]
        down = ref[(v - 1) % STRIDE, rows, :]
        up = ref[(v + 1) % STRIDE, rows, :]
        if v == 0:
            down = pltpu.roll(down, GROUP, 1)
        if v == STRIDE - 1:
            up = pltpu.roll(up, LANES - GROUP, 1)
        sides = pltpu.roll(here, 1, 1) + pltpu.roll(here, LANES - 1, 1)
        return total + (down + up) + sides, here

    def step(src, source, out):
        for v in range(STRIDE):
            for t in range(tiles):
                rows = tile_rows(t)
                total, here = spread(src, v, t)
                value = cs[v, rows, :] * total
                if source is not None:
                    value = source[v, rows, :] + value
                put(out, v, t, KEEP * here + value)

    step(hs, None, h1)
    step(bs, bs, y1)
    step(h1, None, h2)
    step(y1, bs, y2)
    its, ss = {}, {}
    for v in range(STRIDE):
        for t in range(1, tiles):
            rows = tile_rows(t)
            c, b = cs[v, rows, :], bs[v, rows, :]
            total_h, g2 = spread(h2, v, t)
            total_y, x3 = spread(y2, v, t)
            x2 = y1[v, rows, :]
            g1 = KEEP * g2 + c * total_h
            w3 = b + c * total_y
            it = KEEP * x3 + w3
            s = (g1 * b + g2 * (x2 - KEEP * b)) + (
                h1[v, rows, :] * (x3 - KEEP * x2) + hs[v, rows, :] * w3
            )
            its[v, t] = jnp.where(place < OWN, it, pltpu.roll(it, LANES - OWN, 1))
            ss[v, t] = jnp.where(place < OWN, s, pltpu.roll(s, LANES - OWN, 1))
    rim = (lane < DEPTH) | (lane >= LANES - DEPTH)
    copies = []
    for k in range(lz):
        z = level(k, lz)
        g, v = (k + DEPTH) // STRIDE, (k + DEPTH) % STRIDE
        shift = (LANES - DEPTH - (GROUP * g + DEPTH)) % LANES
        for t in range(1, tiles):
            block = tile_rows(t - 1)
            it = jnp.where(rim, pltpu.roll(its[v, t], shift, 1), it_in[k, block, :])
            s = jnp.where(rim, pltpu.roll(ss[v, t], shift, 1), s_in[k, block, :])
            it_out[k, block, :] = it + land_in[k, block, :]
            rg_out[k, block, :] = e_in[k, block, :] * s
        for i, (a, b) in enumerate(((it_out, it_hbm), (rg_out, rg_hbm))):
            copies.append(pltpu.make_async_copy(a.at[k], b.at[z], sem.at[i, k]))
            copies[-1].start()
    for copy in copies:
        copy.wait()


def body(nx, ny, log_range, sea_mask, forcing, cotangent):
    lz, lx, ly = forcing.shape
    f32 = jnp.float32
    sizes = (nx, ny, 2)
    vmem = pl.BlockSpec(memory_space=pltpu.VMEM)
    hbm = pl.BlockSpec(memory_space=pltpu.HBM)

    def call(kernel, shapes, args, name, scratch=(), flops=10**6, ins=vmem, outs=vmem):
        return pl.pallas_call(
            kernel,
            out_shape=[jax.ShapeDtypeStruct(s, f32) for s in shapes],
            in_specs=[ins] * len(args),
            out_specs=[outs] * len(shapes),
            scratch_shapes=[pltpu.VMEM(s, f32) if isinstance(s, tuple) else s for s in scratch],
            compiler_params=pltpu.CompilerParams(vmem_limit_bytes=16 * 2**20),
            cost_estimate=pl.CostEstimate(flops=flops, bytes_accessed=2**20, transcendentals=0),
            name=name,
        )(*args)

    block = (lz, lx, ly)
    store = (lz + DEPTH + 1, lx + 2 * SUB, ly)
    strip = (STRIDE, lx + 2 * SUB, LANES)
    packed = (STRIDE, lx + SUB, LANES)
    c, b, h, e, land, zmsg = call(
        prepare_kernel,
        [block] * 5 + [(3 * DEPTH - 1, lx, ly)],
        [
            pltpu.with_memory_space_constraint(a, pltpu.HBM)
            for a in (log_range, sea_mask, forcing, cotangent)
        ],
        "prepare",
        [block, pltpu.VMEM(block, jnp.int32), block, block, pltpu.SemaphoreType.DMA((4,))],
        ins=hbm,
    )
    swap = [(d, d ^ 1) for d in range(2 * nx * ny)]
    zin = lax.ppermute(zmsg, AXES, swap)
    xa, xb = call(pack_x_kernel, [(lz + DEPTH, SUB, ly)] * 2, (c, b, h, zin), "pack_x")
    xa = lax.ppermute(xa, AXES, pair_swaps(sizes, 0, 0))
    xb = lax.ppermute(xb, AXES, pair_swaps(sizes, 0, 1))
    cm, bm, hm, pc, pb, ph, ya, yb = call(
        functools.partial(pack_y_kernel, nx),
        [store] * 3 + [packed] * 5,
        (c, b, h, zin, xa, xb),
        "pack_y",
    )
    ya = lax.ppermute(ya, AXES, pair_swaps(sizes, 1, 0))
    yb = lax.ppermute(yb, AXES, pair_swaps(sizes, 1, 1))
    it, s = call(
        main_kernel, [block] * 2, (cm, bm, hm), "main", [store] * 4, flops=2 * 10**8
    )
    return call(
        functools.partial(edge_kernel, ny),
        [block] * 2,
        (pc, pb, ph, ya, yb, it, s, e, land),
        "edge",
        [strip] * 7 + [block] * 2 + [pltpu.SemaphoreType.DMA((2, lz))],
        outs=hbm,
    )


def solution(mesh):
    nx, ny = mesh.shape["gx"], mesh.shape["gy"]
    spec = P("gz", "gx", "gy")
    return jax.shard_map(
        lambda *args: tuple(body(nx, ny, *args)),
        mesh=mesh,
        in_specs=(spec,) * 4,
        out_specs=(spec,) * 2,
        check_vma=False,
    )
```

time: 50.6 us -> 18.7 us (0.37)
  Pallas kernels: 32 us -> 4.95 us
  local copies, waits for them, and re-layouts: 3.79 us -> 0 us
  waiting for transfers between devices: 10.2 us -> 9.21 us
    pallas_call x4 -> x5, Pallas kernels: 32 us -> 4.95 us  [call(): pl.pallas_call(kernel, out_shape=[jax.ShapeDtypeStruct(s, f32) for s in s...]
    unnamed x8 -> x0, local copies, waits for them, and re-layouts: 3.79 us -> none
    ppermute x1, waiting for transfers between devices: 2.03 us -> 1.09 us  [body(): ya = lax.ppermute(ya, AXES, pair_swaps(sizes, 1, 0))]
  transfers between devices with their start and end apart: 5 -> 5, of which waited for: 5 -> 5; matrix products, arithmetic and copies ran while one was open for 0% -> 0% of each run, Pallas kernels for 0% -> 6%
where the time goes in v2:
time: 18.7 us; the launch traced here: 18.6 us
  waiting for transfers between devices  9.21 us (49%)
  Pallas kernels  4.95 us (26%)
  starting transfers between devices  3.75 us (20%)
  between operations  0.67 us (4%)
    pallas_call x5, Pallas kernels, call(): pl.pallas_call(kernel, out_shape=[jax.ShapeDtypeStruct(s, f32) for s in s...  4.95 us
    ppermute x1, waiting for transfers between devices, body(): xa = lax.ppermute(xa, AXES, pair_swaps(sizes, 0, 0))  2.83 us
    ppermute x1, waiting for transfers between devices, body(): yb = lax.ppermute(yb, AXES, pair_swaps(sizes, 1, 1))  2.39 us
    ppermute x1, starting transfers between devices, body(): xa = lax.ppermute(xa, AXES, pair_swaps(sizes, 0, 0))  1.64 us
    ppermute x1, waiting for transfers between devices, body(): xb = lax.ppermute(xb, AXES, pair_swaps(sizes, 0, 1))  1.56 us
    ppermute x1, starting transfers between devices, body(): ya = lax.ppermute(ya, AXES, pair_swaps(sizes, 1, 0))  1.56 us
    ppermute x1, waiting for transfers between devices, body(): zin = lax.ppermute(zmsg, AXES, swap)  1.33 us
    ppermute x1, waiting for transfers between devices, body(): ya = lax.ppermute(ya, AXES, pair_swaps(sizes, 1, 0))  1.09 us
  transfers between devices with their start and end apart: 5, of which 5 were waited for; matrix products, arithmetic and copies ran while one was open for 0% of the time, Pallas kernels for 6%

profile of v2, /device:TPU:20, one launch (start us, length us, event | category | flops | bytes accessed | tf_op | source)
XLA Modules:
  0.0 18.6 jit_solution(16845828478835470606)
XLA Ops:
  0.6 1.4 %prepare.1 = (f32[16,32,128]{2,1,0:T(8,128)S(1)}, f32[16,32,128]{2,1,0:T(8,128)S(1)}, f32[16,32,128]{2,1,0:T(8,128)S(1)}, f32[16,32,128]{2,1,0:T(8,128)S(1)}, f3...) custom-call(f32[16,32,128]{2,1,0:T(8,128)} %lr_h.1, s32[16,32,128]{2,1,0:T(8,128)} %sea_h.1, f32[16,32,128]{2,1,0:T(8,128)} %src_h.1, ...), custom_call_target="tpu_custom_call" | custom-call | flops 1000000 | bytes 1048576 | tf_op jit(solution)/shard_map/prepare/pallas_call | solution.py:348
  2.0 0.1 collective-permute-start
  2.1 1.3 %collective-permute-done.zin = f32[8,32,128]{2,1,0:T(8,128)S(1)} collective-permute-done((f32[8,32,128]{2,1,0:T(8,128)S(1)}, f32[8,32,128]{2,1,0:T(8,128)S(1)}, u32[]{:S(2)}, u32[]{:S(2)}) %collective-permute-start) | collective-permute-done | bytes 131104 | tf_op jit(solution)/shard_map/ppermute | solution.py:375
  3.5 1.6 %collective-permute-start.1 = (f32[19,8,128]{2,1,0:T(8,128)S(1)}, f32[19,8,128]{2,1,0:T(8,128)S(1)}, u32[]{:S(2)}, u32[]{:S(2)}) collective-permute-start(f32[19,8,128]{2,1,0:T(8,128)S(1)} %get-tuple-element.24), channel_id=1, source_target_pairs={{0,8},{1,9},{2,10},{3,11},{4,12},{5,13},{6,14},{7,15},{8,0},{9,1},... | collective-permute-start | bytes 233480 | tf_op jit(solution)/shard_map/ppermute | solution.py:377
  5.1 0.0 collective-permute-start.2
  5.1 2.8 %collective-permute-done.1.xa = f32[19,8,128]{2,1,0:T(8,128)S(1)} collective-permute-done((f32[19,8,128]{2,1,0:T(8,128)S(1)}, f32[19,8,128]{2,1,0:T(8,128)S(1)}, u32[]{:S(2)}, u32[]{:S(2)}) %collective-permute-start.1) | collective-permute-done | bytes 77856 | tf_op jit(solution)/shard_map/ppermute | solution.py:377
  7.9 1.6 %collective-permute-done.2.xb = f32[19,8,128]{2,1,0:T(8,128)S(1)} collective-permute-done((f32[19,8,128]{2,1,0:T(8,128)S(1)}, f32[19,8,128]{2,1,0:T(8,128)S(1)}, u32[]{:S(2)}, u32[]{:S(2)}) %collective-permute-start.2) | collective-permute-done | bytes 77856 | tf_op jit(solution)/shard_map/ppermute | solution.py:378
  9.5 0.5 %pack_y.1 = (f32[20,48,128]{2,1,0:T(8,128)S(1)}, f32[20,48,128]{2,1,0:T(8,128)S(1)}, f32[20,48,128]{2,1,0:T(8,128)S(1)}, f32[3,40,128]{2,1,0:T(8,128)S(1)}, f32[...) custom-call(f32[16,32,128]{2,1,0:T(8,128)S(1)} %get-tuple-element.20.c, ...), custom_call_target="tpu_custom_call" | custom-call | flops 1000000 | bytes 1048576 | tf_op jit(solution)/shard_map/pack_y/pallas_call | solution.py:348
  10.1 1.6 %collective-permute-start.3 = (f32[3,40,128]{2,1,0:T(8,128)S(1)}, f32[3,40,128]{2,1,0:T(8,128)S(1)}, u32[]{:S(2)}, u32[]{:S(2)}) collective-permute-start(f32[3,40,128]{2,1,0:T(8,128)S(1)} %get-tuple-element.29), channel_id=1, source_target_pairs={{0,2},{1,3},{2,0},{3,1},{4,6},{5,7},{6,4},{7,5},{8,10},{9,11},{10,... | collective-permute-start | bytes 184328 | tf_op jit(solution)/shard_map/ppermute | solution.py:385
  11.6 0.5 %collective-permute-start.4 = (f32[3,40,128]{2,1,0:T(8,128)S(1)}, f32[3,40,128]{2,1,0:T(8,128)S(1)}, u32[]{:S(2)}, u32[]{:S(2)}) collective-permute-start(f32[3,40,128]{2,1,0:T(8,128)S(1)} %get-tuple-element.30), channel_id=1, source_target_pairs={{0,1},{1,0},{2,4},{3,5},{4,2},{5,3},{6,7},{7,6},{8,9},{9,8},{10,12... | collective-permute-start | bytes 184328 | tf_op jit(solution)/shard_map/ppermute | solution.py:386
  12.1 1.2 %main.1 = (f32[16,32,128]{2,1,0:T(8,128)S(1)}, f32[16,32,128]{2,1,0:T(8,128)S(1)}) custom-call(f32[20,48,128]{2,1,0:T(8,128)S(1)} %get-tuple-element.31.cm, f32[20,48,128]{2,1,0:T(8,128)S(1)} %get-tuple-element.32.bm, f32[20,48,128]{2,1,0:T(8,128)S(1)} %get-tuple-element.33.hm), custom_call_target="tpu_custom_call" | custom-call | flops 200000000 | bytes 1048576 | tf_op jit(solution)/shard_map/main/pallas_call | solution.py:348
  13.2 1.1 %collective-permute-done.3.ya = f32[3,40,128]{2,1,0:T(8,128)S(1)} collective-permute-done((f32[3,40,128]{2,1,0:T(8,128)S(1)}, f32[3,40,128]{2,1,0:T(8,128)S(1)}, u32[]{:S(2)}, u32[]{:S(2)}) %collective-permute-start.3) | collective-permute-done | bytes 61472 | tf_op jit(solution)/shard_map/ppermute | solution.py:385
  14.3 2.4 %collective-permute-done.4.yb = f32[3,40,128]{2,1,0:T(8,128)S(1)} collective-permute-done((f32[3,40,128]{2,1,0:T(8,128)S(1)}, f32[3,40,128]{2,1,0:T(8,128)S(1)}, u32[]{:S(2)}, u32[]{:S(2)}) %collective-permute-start.4) | collective-permute-done | bytes 61472 | tf_op jit(solution)/shard_map/ppermute | solution.py:386
  16.7 1.8 %edge.1 = (f32[16,32,128]{2,1,0:T(8,128)}, f32[16,32,128]{2,1,0:T(8,128)}) custom-call(f32[3,40,128]{2,1,0:T(8,128)S(1)} %get-tuple-element.26.pc, f32[3,40,128]{2,1,0:T(8,128)S(1)} %get-tuple-element.27.pb, f32[3,40,128]{2,1,0:T(8,128)S(1)} %get-tuple-element.28.ph, f32[3,40,128]{2,1,0:T(8,128)S(1)} %collective-permute-done.3.ya, ...), custom_call_target="tpu_custom_call" | custom-call | flops 1000000 | bytes 1048576 | tf_op jit(solution)/shard_map/edge/pallas_call | solution.py:348
  (1 shorter events, 0.0 us)
Async XLA Ops:
  2.0 1.4 %collective-permute-start = (f32[8,32,128]{2,1,0:T(8,128)S(1)}, f32[8,32,128]{2,1,0:T(8,128)S(1)}, u32[]{:S(2)}, u32[]{:S(2)}) collective-permute-start(f32[8,32,128]{2,1,0:T(8,128)S(1)} %get-tuple-element.23), channel_id=1, source_target_pairs={{0,1},{1,0},{2,3},{3,2},{4,5},{5,4},{6,7},{7,6},{8,9},{9,8},{10,11... | collective-permute-start | bytes 393224 | tf_op jit(solution)/shard_map/ppermute | solution.py:375
  3.5 4.5 %collective-permute-start.1 = (f32[19,8,128]{2,1,0:T(8,128)S(1)}, f32[19,8,128]{2,1,0:T(8,128)S(1)}, u32[]{:S(2)}, u32[]{:S(2)}) collective-permute-start(f32[19,8,128]{2,1,0:T(8,128)S(1)} %get-tuple-element.24), channel_id=1, source_target_pairs={{0,8},{1,9},{2,10},{3,11},{4,12},{5,13},{6,14},{7,15},{8,0},{9,1},... | collective-permute-start | bytes 233480 | tf_op jit(solution)/shard_map/ppermute | solution.py:377
  5.1 4.4 %collective-permute-start.2 = (f32[19,8,128]{2,1,0:T(8,128)S(1)}, f32[19,8,128]{2,1,0:T(8,128)S(1)}, u32[]{:S(2)}, u32[]{:S(2)}) collective-permute-start(f32[19,8,128]{2,1,0:T(8,128)S(1)} %get-tuple-element.25), channel_id=1, source_target_pairs={{0,1},{1,0},{2,3},{3,2},{4,5},{5,4},{6,7},{7,6},{8,16},{9,17},{10,... | collective-permute-start | bytes 233480 | tf_op jit(solution)/shard_map/ppermute | solution.py:378
  10.1 4.3 %collective-permute-start.3 = (f32[3,40,128]{2,1,0:T(8,128)S(1)}, f32[3,40,128]{2,1,0:T(8,128)S(1)}, u32[]{:S(2)}, u32[]{:S(2)}) collective-permute-start(f32[3,40,128]{2,1,0:T(8,128)S(1)} %get-tuple-element.29), channel_id=1, source_target_pairs={{0,2},{1,3},{2,0},{3,1},{4,6},{5,7},{6,4},{7,5},{8,10},{9,11},{10,... | collective-permute-start | bytes 184328 | tf_op jit(solution)/shard_map/ppermute | solution.py:385
  11.6 5.1 %collective-permute-start.4 = (f32[3,40,128]{2,1,0:T(8,128)S(1)}, f32[3,40,128]{2,1,0:T(8,128)S(1)}, u32[]{:S(2)}, u32[]{:S(2)}) collective-permute-start(f32[3,40,128]{2,1,0:T(8,128)S(1)} %get-tuple-element.30), channel_id=1, source_target_pairs={{0,1},{1,0},{2,4},{3,5},{4,2},{5,3},{6,7},{7,6},{8,9},{9,8},{10,12... | collective-permute-start | bytes 184328 | tf_op jit(solution)/shard_map/ppermute | solution.py:386

commit v3 on v2

--- a/solution.py
+++ b/solution.py
@@ -133,72 +133,122 @@
     return jnp.where(inside, group, -1), jnp.where(inside, lane - GROUP * group, -1)
 
 
-def pack_y_kernel(nx, c_in, b_in, h_in, zin, xa, xb, cm, bm, hm, pc_out, pb_out, ph_out, ya, yb):
+def pack_own(tiles, group, place, sweep):
+    zero = jnp.zeros((SUB, LANES), jnp.float32)
+    raw = jnp.where(place < 2 * OWN, group, -1)
+    levels = tiles[0]
+    count = tiles[1]
+    acc = [[[zero] * count for _ in range(STRIDE)] for _ in range(3)]
+    for z in range(levels):
+        g, v = z // STRIDE, z % STRIDE
+        for f in range(3):
+            for t, tile in enumerate(sweep(f, z)):
+                if tile is not None:
+                    acc[f][v][t] = jnp.where(
+                        raw == g, pltpu.roll(tile, (GROUP * g + OWN) % LANES, 1), acc[f][v][t]
+                    )
+    own = [[[None] * count for _ in range(STRIDE)] for _ in range(3)]
+    sides = [[[None] * count for _ in range(STRIDE)] for _ in range(2)]
+    for v in range(STRIDE):
+        base = GROUP // 2 if v == 1 else 0
+        at = place - base
+        for t in range(count):
+            for f in range(3):
+                a = acc[f][v][t]
+                moved = pltpu.roll(a, GROUP - 2 * OWN, 1)
+                own[f][v][t] = jnp.where(
+                    place < OWN, a, jnp.where(place >= GROUP - OWN, moved, 0.0)
+                )
+            for side, first in enumerate((DEPTH, OWN)):
+                b, h, c = (
+                    pltpu.roll(acc[f][v][t], (LANES + base + k * DEPTH - first) % LANES, 1)
+                    if (base + k * DEPTH - first) % LANES
+                    else acc[f][v][t]
+                    for k, f in enumerate((1, 2, 0))
+                )
+                sides[side][v][t] = jnp.where(at < DEPTH, b, jnp.where(at < 2 * DEPTH, h, c))
+    return own, sides
+
+
+def put_messages(ya, yb, sides, place, odd, t, row):
+    rows = tile_rows(row)
+    for i, pick in enumerate((lambda s: jnp.where(place < GROUP // 2, s[0][t], s[1][t]),
+                              lambda s: s[2][t])):
+        upper, lower = pick(sides[0]), pick(sides[1])
+        ya[i, rows, :] = jnp.where(odd, lower, upper)
+        yb[i, rows, :] = jnp.where(odd, upper, lower)
+
+
+def pack_block_kernel(c_in, b_in, h_in, zin, pc_out, pb_out, ph_out, ya, yb):
     lz, lx, _ = c_in.shape
-    ix, iy = lax.axis_index("gx"), lax.axis_index("gy")
-    row, lane = iota(0), iota(1)
-    group, place = packed_place(lane, lz)
-    zero = jnp.zeros((SUB, LANES), jnp.float32)
+    group, place = packed_place(iota(1), lz)
+    odd = lax.axis_index("gy") % 2 == 1
+    tiles = lx // SUB
+
+    def sweep(f, z):
+        ref, i = local_or_z(*(
+            (c_in, zin, 2 * DEPTH, DEPTH - 1, z),
+            (b_in, zin, 0, DEPTH, z),
+            (h_in, zin, DEPTH, DEPTH, z),
+        )[f])
+        return [None if ref is None else ref[i, tile_rows(t), :] for t in range(tiles)]
+
+    own, sides = pack_own((lz + DEPTH, tiles), group, place, sweep)
+    for t in range(tiles):
+        for f, ref in enumerate((pc_out, pb_out, ph_out)):
+            for v in range(STRIDE):
+                ref[v, tile_rows(t), :] = own[f][v][t]
+        put_messages(ya, yb, sides, place, odd, t, t)
+
+
+def pack_halo_kernel(nx, lz, xa, xb, ya_in, yb_in, pc_out, pb_out, ph_out, ya, yb):
+    ix = lax.axis_index("gx")
+    group, place = packed_place(iota(1), lz)
+    odd = lax.axis_index("gy") % 2 == 1
+    row = iota(0)
+    parts = {}
+
+    def sweep(f, z):
+        if z not in parts:
+            parts[z] = x_halo(xa, xb, z, ix, nx, row)
+        return [parts[z][(f + 2) % 3]]
+
+    own, sides = pack_own((lz + DEPTH, 1), group, place, sweep)
+    for f, ref in enumerate((pc_out, pb_out, ph_out)):
+        for v in range(STRIDE):
+            ref[v] = own[f][v][0]
+    put_messages(ya, yb, sides, place, odd, 0, 0)
+    for src, dst in ((ya_in, ya), (yb_in, yb)):
+        for i in range(STRIDE - 1):
+            for t in range(src.shape[1] // SUB):
+                dst[i, tile_rows(t + 1), :] = src[i, tile_rows(t), :]
+
+
+def main_kernel(nx, c_in, b_in, h_in, zin, xa, xb, it_out, s_out, cm, bm, hm, y1, y2, h1, h2):
+    lz, lx, _ = it_out.shape
     tiles = lx // SUB + 1
     halo = tile_rows(tiles)
-    acc = [[[zero] * tiles for _ in range(STRIDE)] for _ in range(3)]
-    raw = jnp.where(place < 2 * OWN, group, -1)
+    zero = jnp.zeros((SUB, LANES), jnp.float32)
+    ix, row = lax.axis_index("gx"), iota(0)
     for z in range(lz + DEPTH):
         parts = x_halo(xa, xb, z, ix, nx, row)
         local = (
-            local_or_z(c_in, zin, 2 * DEPTH, DEPTH - 1, z),
             local_or_z(b_in, zin, 0, DEPTH, z),
             local_or_z(h_in, zin, DEPTH, DEPTH, z),
+            local_or_z(c_in, zin, 2 * DEPTH, DEPTH - 1, z),
         )
-        for f, store in enumerate((cm, bm, hm)):
+        for f, store in enumerate((bm, hm, cm)):
             ref, i = local[f]
             for t in range(tiles):
                 if t == 0:
-                    tile = parts[(f + 2) % 3]
+                    tile = parts[f]
                     store[z, halo, :] = tile
                 else:
                     tile = zero if ref is None else ref[i, tile_rows(t - 1), :]
                 store[z, tile_rows(t), :] = tile
-                if f or z:
-                    g, v = z // STRIDE, z % STRIDE
-                    acc[f][v][t] = jnp.where(
-                        raw == g, pltpu.roll(tile, (GROUP * g + OWN) % LANES, 1), acc[f][v][t]
-                    )
     for store in (cm, bm, hm):
         for t in range(tiles + 1):
             store[lz + DEPTH, tile_rows(t), :] = zero
-    odd = iy % 2 == 1
-    for v in range(STRIDE):
-        for t in range(tiles):
-            rows = tile_rows(t)
-            own = []
-            for f in range(3):
-                a = acc[f][v][t]
-                moved = pltpu.roll(a, GROUP - 2 * OWN, 1)
-                own.append(
-                    jnp.where(place < OWN, a, jnp.where(place >= GROUP - OWN, moved, 0.0))
-                )
-            for ref, a in zip((pc_out, pb_out, ph_out), own):
-                ref[v, rows, :] = a
-            c, b, h = (acc[f][v][t] for f in range(3))
-            first, last = OWN, DEPTH
-            upper = jnp.where(
-                place < DEPTH, pltpu.roll(b, LANES - last, 1),
-                jnp.where(place < 2 * DEPTH, h, pltpu.roll(c, 2 * DEPTH - last, 1)),
-            )
-            lower = jnp.where(
-                place < DEPTH, pltpu.roll(b, LANES - first, 1),
-                jnp.where(place < 2 * DEPTH, pltpu.roll(h, LANES + DEPTH - first, 1), c),
-            )
-            ya[v, rows, :] = jnp.where(odd, lower, upper)
-            yb[v, rows, :] = jnp.where(odd, upper, lower)
-
-
-def main_kernel(cm, bm, hm, it_out, s_out, y1, y2, h1, h2):
-    lz, lx, _ = it_out.shape
-    tiles = lx // SUB + 1
-    halo = tile_rows(tiles)
-    zero = jnp.zeros((SUB, LANES), jnp.float32)
 
     def spread(v, z, t):
         rows = tile_rows(t)
@@ -244,7 +294,7 @@
             )
 
 
-def edge_kernel(ny, pc, pb, ph, ya, yb, it_in, s_in, e_in, land_in, it_hbm, rg_hbm,
+def edge_kernel(ny, pc, pb, ph, qc, qb, qh, ya, yb, it_in, s_in, e_in, land_in, it_hbm, rg_hbm,
                 cs, bs, hs, y1, y2, h1, h2, it_out, rg_out, sem):
     lz, lx, _ = e_in.shape
     iy = lax.axis_index("gy")
@@ -265,14 +315,16 @@
     for v in range(STRIDE):
         for t in range(tiles):
             rows = tile_rows(t)
-            a, b = ya[v, rows, :], yb[v, rows, :]
+            a, b = ya[v // 2, rows, :], yb[v // 2, rows, :]
             lo = jnp.where(iy > 0, jnp.where(odd, a, b), zero)
             hi = jnp.where(iy < ny - 1, jnp.where(odd, b, a), zero)
-            for k, (ref, own) in enumerate(((bs, pb), (hs, ph), (cs, pc))):
-                from_lo = pltpu.roll(lo, (OWN + DEPTH - k * DEPTH) % LANES, 1)
-                from_hi = pltpu.roll(hi, (OWN - k * DEPTH) % LANES, 1) if k != 2 else hi
-                put(ref, v, t,
-                    jnp.where(before, from_lo, jnp.where(after, from_hi, own[v, rows, :])))
+            base = GROUP // 2 if v == 1 else 0
+            for k, (ref, block, tile) in enumerate(((bs, pb, qb), (hs, ph, qh), (cs, pc, qc))):
+                own = tile[v] if t == 0 else block[v, tile_rows(t - 1), :]
+                shift = OWN - k * DEPTH - base
+                from_lo = pltpu.roll(lo, (shift + DEPTH) % LANES, 1)
+                from_hi = pltpu.roll(hi, shift % LANES, 1) if shift else hi
+                put(ref, v, t, jnp.where(before, from_lo, jnp.where(after, from_hi, own)))
 
     def spread(ref, v, t):
         rows = tile_rows(t)
@@ -359,7 +411,6 @@
     block = (lz, lx, ly)
     store = (lz + DEPTH + 1, lx + 2 * SUB, ly)
     strip = (STRIDE, lx + 2 * SUB, LANES)
-    packed = (STRIDE, lx + SUB, LANES)
     c, b, h, e, land, zmsg = call(
         prepare_kernel,
         [block] * 5 + [(3 * DEPTH - 1, lx, ly)],
@@ -376,21 +427,33 @@
     xa, xb = call(pack_x_kernel, [(lz + DEPTH, SUB, ly)] * 2, (c, b, h, zin), "pack_x")
     xa = lax.ppermute(xa, AXES, pair_swaps(sizes, 0, 0))
     xb = lax.ppermute(xb, AXES, pair_swaps(sizes, 0, 1))
-    cm, bm, hm, pc, pb, ph, ya, yb = call(
-        functools.partial(pack_y_kernel, nx),
-        [store] * 3 + [packed] * 5,
-        (c, b, h, zin, xa, xb),
-        "pack_y",
+    pc, pb, ph, ya, yb = call(
+        pack_block_kernel,
+        [(STRIDE, lx, LANES)] * 3 + [(STRIDE - 1, lx, LANES)] * 2,
+        (c, b, h, zin),
+        "pack_block",
+        flops=10**8,
+    )
+    qc, qb, qh, ya, yb = call(
+        functools.partial(pack_halo_kernel, nx, lz),
+        [(STRIDE, SUB, LANES)] * 3 + [(STRIDE - 1, lx + SUB, LANES)] * 2,
+        (xa, xb, ya, yb),
+        "pack_halo",
     )
     ya = lax.ppermute(ya, AXES, pair_swaps(sizes, 1, 0))
     yb = lax.ppermute(yb, AXES, pair_swaps(sizes, 1, 1))
     it, s = call(
-        main_kernel, [block] * 2, (cm, bm, hm), "main", [store] * 4, flops=2 * 10**8
+        functools.partial(main_kernel, nx),
+        [block] * 2,
+        (c, b, h, zin, xa, xb),
+        "main",
+        [store] * 7,
+        flops=2 * 10**8,
     )
     return call(
         functools.partial(edge_kernel, ny),
         [block] * 2,
-        (pc, pb, ph, ya, yb, it, s, e, land),
+        (pc, pb, ph, qc, qb, qh, ya, yb, it, s, e, land),
         "edge",
         [strip] * 7 + [block] * 2 + [pltpu.SemaphoreType.DMA((2, lz))],
         outs=hbm,

time: 18.7 us -> 18.2 us (0.973)
  waiting for transfers between devices: 9.21 us -> 8.5 us
    ppermute x1, waiting for transfers between devices: 2.83 us -> 2.37 us  [body(): xa = lax.ppermute(xa, AXES, pair_swaps(sizes, 0, 0))]
    ppermute x1, waiting for transfers between devices: 1.09 us -> 0.84 us  [body(): ya = lax.ppermute(ya, AXES, pair_swaps(sizes, 1, 0))]
    pallas_call x5 -> x6, Pallas kernels: 4.95 us -> 5.11 us  [call(): pl.pallas_call(kernel, out_shape=[jax.ShapeDtypeStruct(s, f32) for s in s...]
  transfers between devices with their start and end apart: 5 -> 5, of which waited for: 5 -> 5; matrix products, arithmetic and copies ran while one was open for 0% -> 0% of each run, Pallas kernels for 6% -> 9%
where the time goes in v3:
time: 18.2 us; the launch traced here: 18 us
  waiting for transfers between devices  8.5 us (47%)
  Pallas kernels  5.11 us (28%)
  starting transfers between devices  3.75 us (21%)
  between operations  0.67 us (4%)
    pallas_call x6, Pallas kernels, call(): pl.pallas_call(kernel, out_shape=[jax.ShapeDtypeStruct(s, f32) for s in s...  5.11 us
    ppermute x1, waiting for transfers between devices, body(): yb = lax.ppermute(yb, AXES, pair_swaps(sizes, 1, 1))  2.39 us
    ppermute x1, waiting for transfers between devices, body(): xa = lax.ppermute(xa, AXES, pair_swaps(sizes, 0, 0))  2.37 us
    ppermute x1, starting transfers between devices, body(): xa = lax.ppermute(xa, AXES, pair_swaps(sizes, 0, 0))  1.64 us
    ppermute x1, waiting for transfers between devices, body(): xb = lax.ppermute(xb, AXES, pair_swaps(sizes, 0, 1))  1.56 us
    ppermute x1, starting transfers between devices, body(): ya = lax.ppermute(ya, AXES, pair_swaps(sizes, 1, 0))  1.56 us
    ppermute x1, waiting for transfers between devices, body(): zin = lax.ppermute(zmsg, AXES, swap)  1.33 us
    ppermute x1, waiting for transfers between devices, body(): ya = lax.ppermute(ya, AXES, pair_swaps(sizes, 1, 0))  0.84 us
  transfers between devices with their start and end apart: 5, of which 5 were waited for; matrix products, arithmetic and copies ran while one was open for 0% of the time, Pallas kernels for 9%

profile of v3, /device:TPU:20, one launch (start us, length us, event | category | flops | bytes accessed | tf_op | source)
XLA Modules:
  0.0 18.0 jit_solution(10754063455357069195)
XLA Ops:
  0.6 1.4 %prepare.1 = (f32[16,32,128]{2,1,0:T(8,128)S(1)}, f32[16,32,128]{2,1,0:T(8,128)S(1)}, f32[16,32,128]{2,1,0:T(8,128)S(1)}, f32[16,32,128]{2,1,0:T(8,128)S(1)}, f3...) custom-call(f32[16,32,128]{2,1,0:T(8,128)} %lr_h.1, s32[16,32,128]{2,1,0:T(8,128)} %sea_h.1, f32[16,32,128]{2,1,0:T(8,128)} %src_h.1, ...), custom_call_target="tpu_custom_call" | custom-call | flops 1000000 | bytes 1048576 | tf_op jit(solution)/shard_map/prepare/pallas_call | solution.py:400
  2.0 0.1 collective-permute-start
  2.1 1.3 %collective-permute-done.zin = f32[8,32,128]{2,1,0:T(8,128)S(1)} collective-permute-done((f32[8,32,128]{2,1,0:T(8,128)S(1)}, f32[8,32,128]{2,1,0:T(8,128)S(1)}, u32[]{:S(2)}, u32[]{:S(2)}) %collective-permute-start) | collective-permute-done | bytes 131104 | tf_op jit(solution)/shard_map/ppermute | solution.py:426
  3.5 1.6 %collective-permute-start.1 = (f32[19,8,128]{2,1,0:T(8,128)S(1)}, f32[19,8,128]{2,1,0:T(8,128)S(1)}, u32[]{:S(2)}, u32[]{:S(2)}) collective-permute-start(f32[19,8,128]{2,1,0:T(8,128)S(1)} %get-tuple-element.29), channel_id=1, source_target_pairs={{0,8},{1,9},{2,10},{3,11},{4,12},{5,13},{6,14},{7,15},{8,0},{9,1},... | collective-permute-start | bytes 233480 | tf_op jit(solution)/shard_map/ppermute | solution.py:428
  5.1 0.0 collective-permute-start.2
  5.1 0.4 %pack_block.1 = (f32[3,32,128]{2,1,0:T(8,128)S(1)}, f32[3,32,128]{2,1,0:T(8,128)S(1)}, f32[3,32,128]{2,1,0:T(8,128)S(1)}, f32[2,32,128]{2,1,0:T(8,128)S(1)}, f32[2,32,128]{2,1,0:T(8,128)S(1)}) custom-call(f32[16,32,128]{2,1,0:T(8,128)S(1)} %get-tuple-element.22.c_in, f32[16,32,128]{2,1,0:T(8,128)S(1)} %get-tuple-element.23.b_in, ...), custom_call_target="tpu_custom_call" | custom-call | flops 100000000 | bytes 1048576 | tf_op jit(solution)/shard_map/pack_block/pallas_call | solution.py:400
  5.6 2.4 %collective-permute-done.1.xa = f32[19,8,128]{2,1,0:T(8,128)S(1)} collective-permute-done((f32[19,8,128]{2,1,0:T(8,128)S(1)}, f32[19,8,128]{2,1,0:T(8,128)S(1)}, u32[]{:S(2)}, u32[]{:S(2)}) %collective-permute-start.1) | collective-permute-done | bytes 77856 | tf_op jit(solution)/shard_map/ppermute | solution.py:428
  7.9 1.6 %collective-permute-done.2.xb = f32[19,8,128]{2,1,0:T(8,128)S(1)} collective-permute-done((f32[19,8,128]{2,1,0:T(8,128)S(1)}, f32[19,8,128]{2,1,0:T(8,128)S(1)}, u32[]{:S(2)}, u32[]{:S(2)}) %collective-permute-start.2) | collective-permute-done | bytes 77856 | tf_op jit(solution)/shard_map/ppermute | solution.py:429
  9.5 0.2 %pack_halo.1 = (f32[3,8,128]{2,1,0:T(8,128)S(1)}, f32[3,8,128]{2,1,0:T(8,128)S(1)}, f32[3,8,128]{2,1,0:T(8,128)S(1)}, f32[2,40,128]{2,1,0:T(8,128)S(1)}, f32[2,40,128]{2,1,0:T(8,128)S(1)}) custom-call(f32[19,8,128]{2,1,0:T(8,128)S(1)} %collective-permute-done.1.xa, f32[19,8,128]{2,1,0:T(8,128)S(1)} %collective-permute-done.2.xb, ...), custom_call_target="tpu_custom_call" | custom-call | flops 1000000 | bytes 1048576 | tf_op jit(solution)/shard_map/pack_halo/pallas_call | solution.py:400
  9.7 1.6 %collective-permute-start.3 = (f32[2,40,128]{2,1,0:T(8,128)S(1)}, f32[2,40,128]{2,1,0:T(8,128)S(1)}, u32[]{:S(2)}, u32[]{:S(2)}) collective-permute-start(f32[2,40,128]{2,1,0:T(8,128)S(1)} %get-tuple-element.36), channel_id=1, source_target_pairs={{0,2},{1,3},{2,0},{3,1},{4,6},{5,7},{6,4},{7,5},{8,10},{9,11},{10,... | collective-permute-start | bytes 122888 | tf_op jit(solution)/shard_map/ppermute | solution.py:443
  11.3 0.5 %collective-permute-start.4 = (f32[2,40,128]{2,1,0:T(8,128)S(1)}, f32[2,40,128]{2,1,0:T(8,128)S(1)}, u32[]{:S(2)}, u32[]{:S(2)}) collective-permute-start(f32[2,40,128]{2,1,0:T(8,128)S(1)} %get-tuple-element.37), channel_id=1, source_target_pairs={{0,1},{1,0},{2,4},{3,5},{4,2},{5,3},{6,7},{7,6},{8,9},{9,8},{10,12... | collective-permute-start | bytes 122888 | tf_op jit(solution)/shard_map/ppermute | solution.py:444
  11.8 1.2 %main.1 = (f32[16,32,128]{2,1,0:T(8,128)S(1)}, f32[16,32,128]{2,1,0:T(8,128)S(1)}) custom-call(f32[16,32,128]{2,1,0:T(8,128)S(1)} %get-tuple-element.22.c_in, f32[16,32,128]{2,1,0:T(8,128)S(1)} %get-tuple-element.23.b_in, f32[16,32,128]{2,1,0:T(8,128)S(1)} %get-tuple-element.24.h_in, f32[8,32,128]{2,1,0:T(8,128)S(1)} %collective-permute-done.zin, ...), custom_call_target="tpu_custom_call" | custom-call | flops 200000000 | bytes 1048576 | tf_op jit(solution)/shard_map/main/pallas_call | solution.py:400
  13.0 0.8 %collective-permute-done.3.ya = f32[2,40,128]{2,1,0:T(8,128)S(1)} collective-permute-done((f32[2,40,128]{2,1,0:T(8,128)S(1)}, f32[2,40,128]{2,1,0:T(8,128)S(1)}, u32[]{:S(2)}, u32[]{:S(2)}) %collective-permute-start.3) | collective-permute-done | bytes 40992 | tf_op jit(solution)/shard_map/ppermute | solution.py:443
  13.8 2.4 %collective-permute-done.4.yb = f32[2,40,128]{2,1,0:T(8,128)S(1)} collective-permute-done((f32[2,40,128]{2,1,0:T(8,128)S(1)}, f32[2,40,128]{2,1,0:T(8,128)S(1)}, u32[]{:S(2)}, u32[]{:S(2)}) %collective-permute-start.4) | collective-permute-done | bytes 40992 | tf_op jit(solution)/shard_map/ppermute | solution.py:444
  16.2 1.8 %edge.1 = (f32[16,32,128]{2,1,0:T(8,128)}, f32[16,32,128]{2,1,0:T(8,128)}) custom-call(f32[3,32,128]{2,1,0:T(8,128)S(1)} %get-tuple-element.26.pc, f32[3,32,128]{2,1,0:T(8,128)S(1)} %get-tuple-element.27.pb, f32[3,32,128]{2,1,0:T(8,128)S(1)} %get-tuple-element.28.ph, f32[3,8,128]{2,1,0:T(8,128)S(1)} %get-tuple-element.33.qc, ...), custom_call_target="tpu_custom_call" | custom-call | flops 1000000 | bytes 1048576 | tf_op jit(solution)/shard_map/edge/pallas_call | solution.py:400
  (1 shorter events, 0.0 us)
Async XLA Ops:
  2.0 1.4 %collective-permute-start = (f32[8,32,128]{2,1,0:T(8,128)S(1)}, f32[8,32,128]{2,1,0:T(8,128)S(1)}, u32[]{:S(2)}, u32[]{:S(2)}) collective-permute-start(f32[8,32,128]{2,1,0:T(8,128)S(1)} %get-tuple-element.25), channel_id=1, source_target_pairs={{0,1},{1,0},{2,3},{3,2},{4,5},{5,4},{6,7},{7,6},{8,9},{9,8},{10,11... | collective-permute-start | bytes 393224 | tf_op jit(solution)/shard_map/ppermute | solution.py:426
  3.5 4.5 %collective-permute-start.1 = (f32[19,8,128]{2,1,0:T(8,128)S(1)}, f32[19,8,128]{2,1,0:T(8,128)S(1)}, u32[]{:S(2)}, u32[]{:S(2)}) collective-permute-start(f32[19,8,128]{2,1,0:T(8,128)S(1)} %get-tuple-element.29), channel_id=1, source_target_pairs={{0,8},{1,9},{2,10},{3,11},{4,12},{5,13},{6,14},{7,15},{8,0},{9,1},... | collective-permute-start | bytes 233480 | tf_op jit(solution)/shard_map/ppermute | solution.py:428
  5.1 4.4 %collective-permute-start.2 = (f32[19,8,128]{2,1,0:T(8,128)S(1)}, f32[19,8,128]{2,1,0:T(8,128)S(1)}, u32[]{:S(2)}, u32[]{:S(2)}) collective-permute-start(f32[19,8,128]{2,1,0:T(8,128)S(1)} %get-tuple-element.30), channel_id=1, source_target_pairs={{0,1},{1,0},{2,3},{3,2},{4,5},{5,4},{6,7},{7,6},{8,16},{9,17},{10,... | collective-permute-start | bytes 233480 | tf_op jit(solution)/shard_map/ppermute | solution.py:429
  9.7 4.1 %collective-permute-start.3 = (f32[2,40,128]{2,1,0:T(8,128)S(1)}, f32[2,40,128]{2,1,0:T(8,128)S(1)}, u32[]{:S(2)}, u32[]{:S(2)}) collective-permute-start(f32[2,40,128]{2,1,0:T(8,128)S(1)} %get-tuple-element.36), channel_id=1, source_target_pairs={{0,2},{1,3},{2,0},{3,1},{4,6},{5,7},{6,4},{7,5},{8,10},{9,11},{10,... | collective-permute-start | bytes 122888 | tf_op jit(solution)/shard_map/ppermute | solution.py:443
  11.3 4.9 %collective-permute-start.4 = (f32[2,40,128]{2,1,0:T(8,128)S(1)}, f32[2,40,128]{2,1,0:T(8,128)S(1)}, u32[]{:S(2)}, u32[]{:S(2)}) collective-permute-start(f32[2,40,128]{2,1,0:T(8,128)S(1)} %get-tuple-element.37), channel_id=1, source_target_pairs={{0,1},{1,0},{2,4},{3,5},{4,2},{5,3},{6,7},{7,6},{8,9},{9,8},{10,12... | collective-permute-start | bytes 122888 | tf_op jit(solution)/shard_map/ppermute | solution.py:444

commit v4 on v3

--- a/solution.py
+++ b/solution.py
@@ -46,27 +46,48 @@
     return slice(SUB * t, SUB * (t + 1))
 
 
-def prepare_kernel(lr_h, sea_h, src_h, cot_h, c_out, b_out, h_out, e_out, land_out, z_out,
-                   lr, sea, src, cot, sem):
-    lz, lx, _ = lr.shape
+def coefficients(log_range, sea, source, cotangent):
+    wet = sea != 0
+    decay = jnp.exp(-2.0 * log_range)
+    c = jnp.where(wet, RELAX / (6.0 + decay), 0.0)
+    return wet, decay, c, c * source, c * cotangent
+
+
+def prepare_z_kernel(lr_h, sea_h, src_h, cot_h, z_out, lr, sea, src, cot, sem):
+    lz, lx = lr_h.shape[0], lr_h.shape[1]
+    low = lax.axis_index("gz") == 0
+    start = jnp.where(low, lz - DEPTH, 0)
     copies = [
-        pltpu.make_async_copy(a, b, sem.at[i])
+        pltpu.make_async_copy(a.at[pl.ds(start, DEPTH)], b, sem.at[i])
         for i, (a, b) in enumerate(((lr_h, lr), (sea_h, sea), (src_h, src), (cot_h, cot)))
     ]
     for copy in copies:
         copy.start()
     for copy in copies:
         copy.wait()
+    for t in range(DEPTH):
+        z = jnp.where(low, DEPTH - 1 - t, t)
+        for r in range(lx // SUB):
+            rows = tile_rows(r)
+            _, _, c, b, h = coefficients(
+                lr[z, rows, :], sea[z, rows, :], src[z, rows, :], cot[z, rows, :]
+            )
+            z_out[t, rows, :] = b
+            z_out[DEPTH + t, rows, :] = h
+            if t < DEPTH - 1:
+                z_out[2 * DEPTH + t, rows, :] = c
+
+
+def prepare_kernel(lr, sea, src, cot, c_out, b_out, h_out, e_out, land_out):
+    lz, lx, _ = lr.shape
     for t in range(lz):
         z = level(t, lz)
-        for r in range(0, lx, SUB):
-            rows = slice(r, r + SUB)
-            wet = sea[z, rows, :] != 0
-            decay = jnp.exp(-2.0 * lr[z, rows, :])
-            c = jnp.where(wet, RELAX / (6.0 + decay), 0.0)
+        for r in range(lx // SUB):
+            rows = tile_rows(r)
             f = src[z, rows, :]
-            b = c * f
-            h = c * cot[z, rows, :]
+            wet, decay, c, b, h = coefficients(
+                lr[z, rows, :], sea[z, rows, :], f, cot[z, rows, :]
+            )
             c_out[t, rows, :] = c
             b_out[t, rows, :] = b
             h_out[t, rows, :] = h
@@ -74,11 +95,6 @@
             land_out[t, rows, :] = jnp.where(
                 wet, 0.0, RELAX * (1.0 + KEEP + KEEP**2 + KEEP**3) * f
             )
-            if t < DEPTH:
-                z_out[t, rows, :] = b
-                z_out[DEPTH + t, rows, :] = h
-            if t < DEPTH - 1:
-                z_out[2 * DEPTH + t, rows, :] = c
 
 
 def local_or_z(local, zin, base, depth, z):
@@ -88,43 +104,61 @@
     return (zin, base + t) if t < depth else (None, 0)
 
 
+FACE = ((DEPTH, 0), (DEPTH, DEPTH), (DEPTH - 1, 2 * DEPTH))
+CORNER = {1: ((2, 0), (2, 3), (1, 6)), 2: ((1, 2), (1, 5), (0, 0))}
+
+
 def pack_x_kernel(c_in, b_in, h_in, zin, a_out, b_out):
     lz, lx, _ = c_in.shape
     odd = lax.axis_index("gx") % 2 == 1
     row = iota(0)
-    for z in range(lz + DEPTH):
+    for z in range(lz + 1):
         faces = []
         for rows, s in ((slice(0, SUB), 1), (slice(lx - SUB, lx), -1)):
-            br, bi = local_or_z(b_in, zin, 0, DEPTH, z)
-            hr, hi = local_or_z(h_in, zin, DEPTH, DEPTH, z)
-            cr, ci = local_or_z(c_in, zin, 2 * DEPTH, DEPTH - 1, z)
-            b = br[bi, rows, :]
-            h = hr[hi, rows, :]
-            h = pltpu.roll(h, (s * DEPTH) % SUB, 0)
-            if cr is None:
-                c = jnp.zeros_like(b)
+            at = row if s == 1 else SUB - 1 - row
+            if z < lz:
+                parts = [(r[z, rows, :], q) for r, (_, q) in zip((b_in, h_in, c_in), FACE)]
             else:
-                c = pltpu.roll(cr[ci, rows, :], (s * 2 * DEPTH) % SUB, 0)
-            at = row if s == 1 else SUB - 1 - row
-            faces.append(jnp.where(at < DEPTH, b, jnp.where(at < 2 * DEPTH, h, c)))
+                parts = [
+                    (zin[DEPTH * f + t - 1, rows, :], CORNER[t][f][1])
+                    for f in range(3)
+                    for t in CORNER
+                    if CORNER[t][f][0]
+                ]
+            parts.sort(key=lambda part: -part[1])
+            face = None
+            for tile, place in parts:
+                if place:
+                    tile = pltpu.roll(tile, (s * place) % SUB, 0)
+                face = tile if face is None else jnp.where(at < limit, tile, face)
+                limit = place
+            faces.append(face)
         low, high = faces
         a_out[z] = jnp.where(odd, low, high)
         b_out[z] = jnp.where(odd, high, low)
 
 
 def x_halo(a_in, b_in, z, index, size, row):
+    zero = jnp.zeros((SUB, LANES), jnp.float32)
+    if z >= DEPTH:
+        at, fields = z - DEPTH, FACE
+    else:
+        at, fields = a_in.shape[0] - 1, CORNER.get(DEPTH - z)
+    if fields is None:
+        return zero, zero, zero
     odd = index % 2 == 1
-    zero = jnp.zeros((SUB, LANES), jnp.float32)
-    before = jnp.where(index > 0, jnp.where(odd, a_in[z], b_in[z]), zero)
-    after = jnp.where(index < size - 1, jnp.where(odd, b_in[z], a_in[z]), zero)
+    before = jnp.where(index > 0, jnp.where(odd, a_in[at], b_in[at]), zero)
+    after = jnp.where(index < size - 1, jnp.where(odd, b_in[at], a_in[at]), zero)
     up = SUB - 1 - row
 
     def merge(depth, shift):
+        if not depth:
+            return zero
         lo = pltpu.roll(before, shift, 0) if shift else before
         hi = pltpu.roll(after, SUB - shift, 0) if shift else after
         return jnp.where(row < depth, hi, jnp.where(up < depth, lo, 0.0))
 
-    return merge(DEPTH, 0), merge(DEPTH, DEPTH), merge(DEPTH - 1, 2 * DEPTH)
+    return tuple(merge(*field) for field in fields)
 
 
 def packed_place(lane, lz):
@@ -411,20 +445,20 @@
     block = (lz, lx, ly)
     store = (lz + DEPTH + 1, lx + 2 * SUB, ly)
     strip = (STRIDE, lx + 2 * SUB, LANES)
-    c, b, h, e, land, zmsg = call(
-        prepare_kernel,
-        [block] * 5 + [(3 * DEPTH - 1, lx, ly)],
-        [
-            pltpu.with_memory_space_constraint(a, pltpu.HBM)
-            for a in (log_range, sea_mask, forcing, cotangent)
-        ],
-        "prepare",
-        [block, pltpu.VMEM(block, jnp.int32), block, block, pltpu.SemaphoreType.DMA((4,))],
+    args = (log_range, sea_mask, forcing, cotangent)
+    face = (DEPTH, lx, ly)
+    (zmsg,) = call(
+        prepare_z_kernel,
+        [(3 * DEPTH - 1, lx, ly)],
+        [pltpu.with_memory_space_constraint(a, pltpu.HBM) for a in args],
+        "prepare_z",
+        [face, pltpu.VMEM(face, jnp.int32), face, face, pltpu.SemaphoreType.DMA((4,))],
         ins=hbm,
     )
+    c, b, h, e, land = call(prepare_kernel, [block] * 5, args, "prepare", flops=10**8)
     swap = [(d, d ^ 1) for d in range(2 * nx * ny)]
     zin = lax.ppermute(zmsg, AXES, swap)
-    xa, xb = call(pack_x_kernel, [(lz + DEPTH, SUB, ly)] * 2, (c, b, h, zin), "pack_x")
+    xa, xb = call(pack_x_kernel, [(lz + 1, SUB, ly)] * 2, (c, b, h, zin), "pack_x")
     xa = lax.ppermute(xa, AXES, pair_swaps(sizes, 0, 0))
     xb = lax.ppermute(xb, AXES, pair_swaps(sizes, 0, 1))
     pc, pb, ph, ya, yb = call(

time: 18.2 us -> 17.8 us (0.978)
  Pallas kernels: 5.11 us -> 4.81 us
  waiting for transfers between devices: 8.5 us -> 8.23 us
    pallas_call x6 -> x7, Pallas kernels: 5.11 us -> 4.81 us  [call(): pl.pallas_call(kernel, out_shape=[jax.ShapeDtypeStruct(s, f32) for s in s...]
    ppermute x1, waiting for transfers between devices: 1.33 us -> 1.05 us  [body(): zin = lax.ppermute(zmsg, AXES, swap)]
  transfers between devices with their start and end apart: 5 -> 5, of which waited for: 5 -> 5; matrix products, arithmetic and copies ran while one was open for 0% -> 0% of each run, Pallas kernels for 9% -> 10%
where the time goes in v4:
time: 17.8 us; the launch traced here: 17.6 us
  waiting for transfers between devices  8.23 us (46%)
  Pallas kernels  4.81 us (27%)
  starting transfers between devices  3.75 us (21%)
  between operations  0.73 us (4%)
    pallas_call x7, Pallas kernels, call(): pl.pallas_call(kernel, out_shape=[jax.ShapeDtypeStruct(s, f32) for s in s...  4.81 us
    ppermute x1, waiting for transfers between devices, body(): yb = lax.ppermute(yb, AXES, pair_swaps(sizes, 1, 1))  2.39 us
    ppermute x1, waiting for transfers between devices, body(): xa = lax.ppermute(xa, AXES, pair_swaps(sizes, 0, 0))  2.27 us
    ppermute x1, starting transfers between devices, body(): xa = lax.ppermute(xa, AXES, pair_swaps(sizes, 0, 0))  1.64 us
    ppermute x1, waiting for transfers between devices, body(): xb = lax.ppermute(xb, AXES, pair_swaps(sizes, 0, 1))  1.58 us
    ppermute x1, starting transfers between devices, body(): ya = lax.ppermute(ya, AXES, pair_swaps(sizes, 1, 0))  1.56 us
    ppermute x1, waiting for transfers between devices, body(): zin = lax.ppermute(zmsg, AXES, swap)  1.05 us
    ppermute x1, waiting for transfers between devices, body(): ya = lax.ppermute(ya, AXES, pair_swaps(sizes, 1, 0))  0.94 us
  transfers between devices with their start and end apart: 5, of which 5 were waited for; matrix products, arithmetic and copies ran while one was open for 0% of the time, Pallas kernels for 10%

profile of v4, /device:TPU:20, one launch (start us, length us, event | category | flops | bytes accessed | tf_op | source)
XLA Modules:
  0.0 17.6 jit_solution(13177906965581624394)
XLA Ops:
  0.6 0.0 copy-start.3
  0.6 0.0 copy-start.2
  0.7 0.0 copy-start.1
  0.7 0.0 copy-start
  0.7 1.0 %prepare_z.1 = f32[8,32,128]{2,1,0:T(8,128)S(1)} custom-call(f32[16,32,128]{2,1,0:T(8,128)} %lr_h.1, s32[16,32,128]{2,1,0:T(8,128)} %sea_h.1, f32[16,32,128]{2,1,0:T(8,128)} %src_h.1, f32[16,32,128]{2,1,0:T(8,128)} %cot_h.1), custom_call_target="tpu_custom_call" | custom-call | flops 1000000 | bytes 1048576 | tf_op jit(solution)/shard_map/prepare_z/pallas_call | solution.py:434
  1.7 0.1 collective-permute-start
  1.8 0.0 copy-done.3
  1.8 0.0 copy-done.2
  1.8 0.0 copy-done.1
  1.8 0.1 copy-done
  1.9 0.1 prepare.1
  2.1 1.1 %collective-permute-done.zin = f32[8,32,128]{2,1,0:T(8,128)S(1)} collective-permute-done((f32[8,32,128]{2,1,0:T(8,128)S(1)}, f32[8,32,128]{2,1,0:T(8,128)S(1)}, u32[]{:S(2)}, u32[]{:S(2)}) %collective-permute-start) | collective-permute-done | bytes 131104 | tf_op jit(solution)/shard_map/ppermute | solution.py:460
  3.2 1.6 %collective-permute-start.1 = (f32[17,8,128]{2,1,0:T(8,128)S(1)}, f32[17,8,128]{2,1,0:T(8,128)S(1)}, u32[]{:S(2)}, u32[]{:S(2)}) collective-permute-start(f32[17,8,128]{2,1,0:T(8,128)S(1)} %get-tuple-element.27), channel_id=1, source_target_pairs={{0,8},{1,9},{2,10},{3,11},{4,12},{5,13},{6,14},{7,15},{8,0},{9,1},... | collective-permute-start | bytes 208904 | tf_op jit(solution)/shard_map/ppermute | solution.py:462
  4.8 0.0 collective-permute-start.2
  4.8 0.5 %pack_block.1 = (f32[3,32,128]{2,1,0:T(8,128)S(1)}, f32[3,32,128]{2,1,0:T(8,128)S(1)}, f32[3,32,128]{2,1,0:T(8,128)S(1)}, f32[2,32,128]{2,1,0:T(8,128)S(1)}, f32[2,32,128]{2,1,0:T(8,128)S(1)}) custom-call(f32[16,32,128]{2,1,0:T(8,128)S(1)} %get-tuple-element.21.c_in, f32[16,32,128]{2,1,0:T(8,128)S(1)} %get-tuple-element.22.b_in, ...), custom_call_target="tpu_custom_call" | custom-call | flops 100000000 | bytes 1048576 | tf_op jit(solution)/shard_map/pack_block/pallas_call | solution.py:434
  5.3 2.3 %collective-permute-done.1.xa = f32[17,8,128]{2,1,0:T(8,128)S(1)} collective-permute-done((f32[17,8,128]{2,1,0:T(8,128)S(1)}, f32[17,8,128]{2,1,0:T(8,128)S(1)}, u32[]{:S(2)}, u32[]{:S(2)}) %collective-permute-start.1) | collective-permute-done | bytes 69664 | tf_op jit(solution)/shard_map/ppermute | solution.py:462
  7.5 1.6 %collective-permute-done.2.xb = f32[17,8,128]{2,1,0:T(8,128)S(1)} collective-permute-done((f32[17,8,128]{2,1,0:T(8,128)S(1)}, f32[17,8,128]{2,1,0:T(8,128)S(1)}, u32[]{:S(2)}, u32[]{:S(2)}) %collective-permute-start.2) | collective-permute-done | bytes 69664 | tf_op jit(solution)/shard_map/ppermute | solution.py:463
  9.1 0.2 %pack_halo.1 = (f32[3,8,128]{2,1,0:T(8,128)S(1)}, f32[3,8,128]{2,1,0:T(8,128)S(1)}, f32[3,8,128]{2,1,0:T(8,128)S(1)}, f32[2,40,128]{2,1,0:T(8,128)S(1)}, f32[2,40,128]{2,1,0:T(8,128)S(1)}) custom-call(f32[17,8,128]{2,1,0:T(8,128)S(1)} %collective-permute-done.1.xa, f32[17,8,128]{2,1,0:T(8,128)S(1)} %collective-permute-done.2.xb, ...), custom_call_target="tpu_custom_call" | custom-call | flops 1000000 | bytes 1048576 | tf_op jit(solution)/shard_map/pack_halo/pallas_call | solution.py:434
  9.3 1.6 %collective-permute-start.3 = (f32[2,40,128]{2,1,0:T(8,128)S(1)}, f32[2,40,128]{2,1,0:T(8,128)S(1)}, u32[]{:S(2)}, u32[]{:S(2)}) collective-permute-start(f32[2,40,128]{2,1,0:T(8,128)S(1)} %get-tuple-element.34), channel_id=1, source_target_pairs={{0,2},{1,3},{2,0},{3,1},{4,6},{5,7},{6,4},{7,5},{8,10},{9,11},{10,... | collective-permute-start | bytes 122888 | tf_op jit(solution)/shard_map/ppermute | solution.py:477
  10.9 0.5 %collective-permute-start.4 = (f32[2,40,128]{2,1,0:T(8,128)S(1)}, f32[2,40,128]{2,1,0:T(8,128)S(1)}, u32[]{:S(2)}, u32[]{:S(2)}) collective-permute-start(f32[2,40,128]{2,1,0:T(8,128)S(1)} %get-tuple-element.35), channel_id=1, source_target_pairs={{0,1},{1,0},{2,4},{3,5},{4,2},{5,3},{6,7},{7,6},{8,9},{9,8},{10,12... | collective-permute-start | bytes 122888 | tf_op jit(solution)/shard_map/ppermute | solution.py:478
  11.4 1.1 %main.1 = (f32[16,32,128]{2,1,0:T(8,128)S(1)}, f32[16,32,128]{2,1,0:T(8,128)S(1)}) custom-call(f32[16,32,128]{2,1,0:T(8,128)S(1)} %get-tuple-element.21.c_in, f32[16,32,128]{2,1,0:T(8,128)S(1)} %get-tuple-element.22.b_in, f32[16,32,128]{2,1,0:T(8,128)S(1)} %get-tuple-element.23.h_in, f32[8,32,128]{2,1,0:T(8,128)S(1)} %collective-permute-done.zin, ...), custom_call_target="tpu_custom_call" | custom-call | flops 200000000 | bytes 1048576 | tf_op jit(solution)/shard_map/main/pallas_call | solution.py:434
  12.5 0.9 %collective-permute-done.3.ya = f32[2,40,128]{2,1,0:T(8,128)S(1)} collective-permute-done((f32[2,40,128]{2,1,0:T(8,128)S(1)}, f32[2,40,128]{2,1,0:T(8,128)S(1)}, u32[]{:S(2)}, u32[]{:S(2)}) %collective-permute-start.3) | collective-permute-done | bytes 40992 | tf_op jit(solution)/shard_map/ppermute | solution.py:477
  13.4 2.4 %collective-permute-done.4.yb = f32[2,40,128]{2,1,0:T(8,128)S(1)} collective-permute-done((f32[2,40,128]{2,1,0:T(8,128)S(1)}, f32[2,40,128]{2,1,0:T(8,128)S(1)}, u32[]{:S(2)}, u32[]{:S(2)}) %collective-permute-start.4) | collective-permute-done | bytes 40992 | tf_op jit(solution)/shard_map/ppermute | solution.py:478
  15.8 1.8 %edge.1 = (f32[16,32,128]{2,1,0:T(8,128)}, f32[16,32,128]{2,1,0:T(8,128)}) custom-call(f32[3,32,128]{2,1,0:T(8,128)S(1)} %get-tuple-element.24.pc, f32[3,32,128]{2,1,0:T(8,128)S(1)} %get-tuple-element.25.pb, f32[3,32,128]{2,1,0:T(8,128)S(1)} %get-tuple-element.26.ph, f32[3,8,128]{2,1,0:T(8,128)S(1)} %get-tuple-element.31.qc, ...), custom_call_target="tpu_custom_call" | custom-call | flops 1000000 | bytes 1048576 | tf_op jit(solution)/shard_map/edge/pallas_call | solution.py:434
  (1 shorter events, 0.0 us)
Async XLA Ops:
  0.6 1.2 %copy-start.3 = (f32[16,32,128]{2,1,0:T(8,128)S(1)}, f32[16,32,128]{2,1,0:T(8,128)}, u32[]{:S(2)}) copy-start(f32[16,32,128]{2,1,0:T(8,128)} %cot_h.1) | copy-start | bytes 786436
  0.6 1.2 %copy-start.2 = (f32[16,32,128]{2,1,0:T(8,128)S(1)}, f32[16,32,128]{2,1,0:T(8,128)}, u32[]{:S(2)}) copy-start(f32[16,32,128]{2,1,0:T(8,128)} %src_h.1) | copy-start | bytes 786436
  0.7 1.2 %copy-start.1 = (s32[16,32,128]{2,1,0:T(8,128)S(1)}, s32[16,32,128]{2,1,0:T(8,128)}, u32[]{:S(2)}) copy-start(s32[16,32,128]{2,1,0:T(8,128)} %sea_h.1) | copy-start | bytes 786436
  0.7 1.3 %copy-start = (f32[16,32,128]{2,1,0:T(8,128)S(1)}, f32[16,32,128]{2,1,0:T(8,128)}, u32[]{:S(2)}) copy-start(f32[16,32,128]{2,1,0:T(8,128)} %lr_h.1) | copy-start | bytes 786436
  1.7 1.4 %collective-permute-start = (f32[8,32,128]{2,1,0:T(8,128)S(1)}, f32[8,32,128]{2,1,0:T(8,128)S(1)}, u32[]{:S(2)}, u32[]{:S(2)}) collective-permute-start(f32[8,32,128]{2,1,0:T(8,128)S(1)} %prepare_z.1), channel_id=1, source_target_pairs={{0,1},{1,0},{2,3},{3,2},{4,5},{5,4},{6,7},{7,6},{8,9},{9,8},{10,11... | collective-permute-start | bytes 393224 | tf_op jit(solution)/shard_map/ppermute | solution.py:460
  3.2 4.4 %collective-permute-start.1 = (f32[17,8,128]{2,1,0:T(8,128)S(1)}, f32[17,8,128]{2,1,0:T(8,128)S(1)}, u32[]{:S(2)}, u32[]{:S(2)}) collective-permute-start(f32[17,8,128]{2,1,0:T(8,128)S(1)} %get-tuple-element.27), channel_id=1, source_target_pairs={{0,8},{1,9},{2,10},{3,11},{4,12},{5,13},{6,14},{7,15},{8,0},{9,1},... | collective-permute-start | bytes 208904 | tf_op jit(solution)/shard_map/ppermute | solution.py:462
  4.8 4.3 %collective-permute-start.2 = (f32[17,8,128]{2,1,0:T(8,128)S(1)}, f32[17,8,128]{2,1,0:T(8,128)S(1)}, u32[]{:S(2)}, u32[]{:S(2)}) collective-permute-start(f32[17,8,128]{2,1,0:T(8,128)S(1)} %get-tuple-element.28), channel_id=1, source_target_pairs={{0,1},{1,0},{2,3},{3,2},{4,5},{5,4},{6,7},{7,6},{8,16},{9,17},{10,... | collective-permute-start | bytes 208904 | tf_op jit(solution)/shard_map/ppermute | solution.py:463
  9.3 4.1 %collective-permute-start.3 = (f32[2,40,128]{2,1,0:T(8,128)S(1)}, f32[2,40,128]{2,1,0:T(8,128)S(1)}, u32[]{:S(2)}, u32[]{:S(2)}) collective-permute-start(f32[2,40,128]{2,1,0:T(8,128)S(1)} %get-tuple-element.34), channel_id=1, source_target_pairs={{0,2},{1,3},{2,0},{3,1},{4,6},{5,7},{6,4},{7,5},{8,10},{9,11},{10,... | collective-permute-start | bytes 122888 | tf_op jit(solution)/shard_map/ppermute | solution.py:477
  10.9 4.9 %collective-permute-start.4 = (f32[2,40,128]{2,1,0:T(8,128)S(1)}, f32[2,40,128]{2,1,0:T(8,128)S(1)}, u32[]{:S(2)}, u32[]{:S(2)}) collective-permute-start(f32[2,40,128]{2,1,0:T(8,128)S(1)} %get-tuple-element.35), channel_id=1, source_target_pairs={{0,1},{1,0},{2,4},{3,5},{4,2},{5,3},{6,7},{7,6},{8,9},{9,8},{10,12... | collective-permute-start | bytes 122888 | tf_op jit(solution)/shard_map/ppermute | solution.py:478

commit v5 on v4

--- a/solution.py
+++ b/solution.py
@@ -167,11 +167,29 @@
     return jnp.where(inside, group, -1), jnp.where(inside, lane - GROUP * group, -1)
 
 
-def pack_own(tiles, group, place, sweep):
+BLOCK_FIELDS = ((1, DEPTH, 0), (2, DEPTH, DEPTH), (0, DEPTH, 2 * DEPTH))
+HALO_FIELDS = ((1, DEPTH - 1, 0), (2, DEPTH - 1, DEPTH - 1), (0, DEPTH - 2, 2 * DEPTH - 2))
+
+
+def message_slot(v, t, tiles):
+    if t == 0:
+        return 0, OWN * v
+    if v < STRIDE - 1:
+        return t, GROUP // 2 * v
+    return tiles + (t - 1) // 2, GROUP // 2 * ((t - 1) % 2)
+
+
+def message_length(tiles):
+    return tiles + tiles // 2
+
+
+def lane_roll(x, shift):
+    return pltpu.roll(x, shift % LANES, 1) if shift % LANES else x
+
+
+def pack_own(levels, first, count, tiles, place, group, sweep):
     zero = jnp.zeros((SUB, LANES), jnp.float32)
     raw = jnp.where(place < 2 * OWN, group, -1)
-    levels = tiles[0]
-    count = tiles[1]
     acc = [[[zero] * count for _ in range(STRIDE)] for _ in range(3)]
     for z in range(levels):
         g, v = z // STRIDE, z % STRIDE
@@ -182,35 +200,35 @@
                         raw == g, pltpu.roll(tile, (GROUP * g + OWN) % LANES, 1), acc[f][v][t]
                     )
     own = [[[None] * count for _ in range(STRIDE)] for _ in range(3)]
-    sides = [[[None] * count for _ in range(STRIDE)] for _ in range(2)]
-    for v in range(STRIDE):
-        base = GROUP // 2 if v == 1 else 0
-        at = place - base
-        for t in range(count):
+    sides = [{}, {}]
+    for t in range(count):
+        fields = BLOCK_FIELDS if first + t else HALO_FIELDS
+        for v in range(STRIDE):
+            slot, base = message_slot(v, first + t, tiles)
+            for side in range(2):
+                message = sides[side].get(slot)
+                for f, depth, offset in fields:
+                    at = OWN - depth if side == 0 else OWN
+                    part = lane_roll(acc[f][v][t], base + offset - at)
+                    if message is None:
+                        message = part
+                    else:
+                        message = jnp.where(place >= base + offset, part, message)
+                sides[side][slot] = message
             for f in range(3):
                 a = acc[f][v][t]
                 moved = pltpu.roll(a, GROUP - 2 * OWN, 1)
                 own[f][v][t] = jnp.where(
                     place < OWN, a, jnp.where(place >= GROUP - OWN, moved, 0.0)
                 )
-            for side, first in enumerate((DEPTH, OWN)):
-                b, h, c = (
-                    pltpu.roll(acc[f][v][t], (LANES + base + k * DEPTH - first) % LANES, 1)
-                    if (base + k * DEPTH - first) % LANES
-                    else acc[f][v][t]
-                    for k, f in enumerate((1, 2, 0))
-                )
-                sides[side][v][t] = jnp.where(at < DEPTH, b, jnp.where(at < 2 * DEPTH, h, c))
     return own, sides
 
 
-def put_messages(ya, yb, sides, place, odd, t, row):
-    rows = tile_rows(row)
-    for i, pick in enumerate((lambda s: jnp.where(place < GROUP // 2, s[0][t], s[1][t]),
-                              lambda s: s[2][t])):
-        upper, lower = pick(sides[0]), pick(sides[1])
-        ya[i, rows, :] = jnp.where(odd, lower, upper)
-        yb[i, rows, :] = jnp.where(odd, upper, lower)
+def put_messages(ya, yb, sides, odd):
+    for slot in sides[0]:
+        upper, lower = sides[0][slot], sides[1][slot]
+        ya[slot] = jnp.where(odd, lower, upper)
+        yb[slot] = jnp.where(odd, upper, lower)
 
 
 def pack_block_kernel(c_in, b_in, h_in, zin, pc_out, pb_out, ph_out, ya, yb):
@@ -227,15 +245,15 @@
         )[f])
         return [None if ref is None else ref[i, tile_rows(t), :] for t in range(tiles)]
 
-    own, sides = pack_own((lz + DEPTH, tiles), group, place, sweep)
+    own, sides = pack_own(lz + DEPTH, 1, tiles, tiles + 1, place, group, sweep)
+    put_messages(ya, yb, sides, odd)
     for t in range(tiles):
         for f, ref in enumerate((pc_out, pb_out, ph_out)):
             for v in range(STRIDE):
                 ref[v, tile_rows(t), :] = own[f][v][t]
-        put_messages(ya, yb, sides, place, odd, t, t)
-
-
-def pack_halo_kernel(nx, lz, xa, xb, ya_in, yb_in, pc_out, pb_out, ph_out, ya, yb):
+
+
+def pack_halo_kernel(nx, lz, xa, xb, ya_in, yb_in, pc_out, pb_out, ph_out, yb, ya):
     ix = lax.axis_index("gx")
     group, place = packed_place(iota(1), lz)
     odd = lax.axis_index("gy") % 2 == 1
@@ -247,15 +265,14 @@
             parts[z] = x_halo(xa, xb, z, ix, nx, row)
         return [parts[z][(f + 2) % 3]]
 
-    own, sides = pack_own((lz + DEPTH, 1), group, place, sweep)
+    own, sides = pack_own(lz + DEPTH, 0, 1, 0, place, group, sweep)
+    put_messages(ya, yb, sides, odd)
+    for src, dst in ((ya_in, ya), (yb_in, yb)):
+        for i in range(1, src.shape[0]):
+            dst[i] = src[i]
     for f, ref in enumerate((pc_out, pb_out, ph_out)):
         for v in range(STRIDE):
             ref[v] = own[f][v][0]
-    put_messages(ya, yb, sides, place, odd, 0, 0)
-    for src, dst in ((ya_in, ya), (yb_in, yb)):
-        for i in range(STRIDE - 1):
-            for t in range(src.shape[1] // SUB):
-                dst[i, tile_rows(t + 1), :] = src[i, tile_rows(t), :]
 
 
 def main_kernel(nx, c_in, b_in, h_in, zin, xa, xb, it_out, s_out, cm, bm, hm, y1, y2, h1, h2):
@@ -328,7 +345,7 @@
             )
 
 
-def edge_kernel(ny, pc, pb, ph, qc, qb, qh, ya, yb, it_in, s_in, e_in, land_in, it_hbm, rg_hbm,
+def edge_kernel(ny, pc, pb, ph, qc, qb, qh, yb, ya, it_in, s_in, e_in, land_in, it_hbm, rg_hbm,
                 cs, bs, hs, y1, y2, h1, h2, it_out, rg_out, sem):
     lz, lx, _ = e_in.shape
     iy = lax.axis_index("gy")
@@ -338,27 +355,35 @@
     halo = tile_rows(tiles)
     zero = jnp.zeros((SUB, LANES), jnp.float32)
     odd = iy % 2 == 1
-    after = (place >= OWN) & (place < OWN + DEPTH)
-    before = (place >= OWN + DEPTH) & (place < OWN + 2 * DEPTH)
 
     def put(ref, v, t, value):
         ref[v, tile_rows(t), :] = value
         if t == 0:
             ref[v, halo, :] = value
 
-    for v in range(STRIDE):
-        for t in range(tiles):
-            rows = tile_rows(t)
-            a, b = ya[v // 2, rows, :], yb[v // 2, rows, :]
-            lo = jnp.where(iy > 0, jnp.where(odd, a, b), zero)
-            hi = jnp.where(iy < ny - 1, jnp.where(odd, b, a), zero)
-            base = GROUP // 2 if v == 1 else 0
-            for k, (ref, block, tile) in enumerate(((bs, pb, qb), (hs, ph, qh), (cs, pc, qc))):
-                own = tile[v] if t == 0 else block[v, tile_rows(t - 1), :]
-                shift = OWN - k * DEPTH - base
-                from_lo = pltpu.roll(lo, (shift + DEPTH) % LANES, 1)
-                from_hi = pltpu.roll(hi, shift % LANES, 1) if shift else hi
-                put(ref, v, t, jnp.where(before, from_lo, jnp.where(after, from_hi, own)))
+    slots = []
+    for i in range(ya.shape[0]):
+        a, b = ya[i], yb[i]
+        slots.append(
+            (
+                jnp.where(iy > 0, jnp.where(odd, a, b), zero),
+                jnp.where(iy < ny - 1, jnp.where(odd, b, a), zero),
+            )
+        )
+    stores = (cs, bs, hs)
+    blocks, halos = (pc, pb, ph), (qc, qb, qh)
+    for t in range(tiles):
+        for v in range(STRIDE):
+            slot, base = message_slot(v, t, tiles)
+            lo, hi = slots[slot]
+            for f, depth, offset in BLOCK_FIELDS if t else HALO_FIELDS:
+                end = OWN + 2 * DEPTH
+                before = (place >= end - depth) & (place < end)
+                after = (place >= OWN) & (place < OWN + depth)
+                from_lo = lane_roll(lo, end - depth - base - offset)
+                from_hi = lane_roll(hi, OWN - base - offset)
+                own = blocks[f][v, tile_rows(t - 1), :] if t else halos[f][v]
+                put(stores[f], v, t, jnp.where(before, from_lo, jnp.where(after, from_hi, own)))
 
     def spread(ref, v, t):
         rows = tile_rows(t)
@@ -445,6 +470,7 @@
     block = (lz, lx, ly)
     store = (lz + DEPTH + 1, lx + 2 * SUB, ly)
     strip = (STRIDE, lx + 2 * SUB, LANES)
+    slots = message_length(lx // SUB + 1)
     args = (log_range, sea_mask, forcing, cotangent)
     face = (DEPTH, lx, ly)
     (zmsg,) = call(
@@ -463,19 +489,19 @@
     xb = lax.ppermute(xb, AXES, pair_swaps(sizes, 0, 1))
     pc, pb, ph, ya, yb = call(
         pack_block_kernel,
-        [(STRIDE, lx, LANES)] * 3 + [(STRIDE - 1, lx, LANES)] * 2,
+        [(STRIDE, lx, LANES)] * 3 + [(slots, SUB, LANES)] * 2,
         (c, b, h, zin),
         "pack_block",
         flops=10**8,
     )
-    qc, qb, qh, ya, yb = call(
+    qc, qb, qh, yb, ya = call(
         functools.partial(pack_halo_kernel, nx, lz),
-        [(STRIDE, SUB, LANES)] * 3 + [(STRIDE - 1, lx + SUB, LANES)] * 2,
+        [(STRIDE, SUB, LANES)] * 3 + [(slots, SUB, LANES)] * 2,
         (xa, xb, ya, yb),
         "pack_halo",
     )
+    yb = lax.ppermute(yb, AXES, pair_swaps(sizes, 1, 1))
     ya = lax.ppermute(ya, AXES, pair_swaps(sizes, 1, 0))
-    yb = lax.ppermute(yb, AXES, pair_swaps(sizes, 1, 1))
     it, s = call(
         functools.partial(main_kernel, nx),
         [block] * 2,
@@ -487,7 +513,7 @@
     return call(
         functools.partial(edge_kernel, ny),
         [block] * 2,
-        (pc, pb, ph, qc, qb, qh, ya, yb, it, s, e, land),
+        (pc, pb, ph, qc, qb, qh, yb, ya, it, s, e, land),
         "edge",
         [strip] * 7 + [block] * 2 + [pltpu.SemaphoreType.DMA((2, lz))],
         outs=hbm,

time: 17.8 us -> 16.8 us (0.944)
  waiting for transfers between devices: 8.23 us -> 7.54 us
  starting transfers between devices: 3.75 us -> 3.35 us
    ppermute x1, starting transfers between devices: 1.56 us -> 0.14 us  [body(): ya = lax.ppermute(ya, AXES, pair_swaps(sizes, 1, 0))]
    ppermute x1, starting transfers between devices: 0.48 us -> 1.5 us  [body(): yb = lax.ppermute(yb, AXES, pair_swaps(sizes, 1, 1))]
    ppermute x1, waiting for transfers between devices: 0.94 us -> 0.53 us  [body(): ya = lax.ppermute(ya, AXES, pair_swaps(sizes, 1, 0))]
    ppermute x1, waiting for transfers between devices: 2.39 us -> 2.1 us  [body(): yb = lax.ppermute(yb, AXES, pair_swaps(sizes, 1, 1))]
where the time goes in v5:
time: 16.8 us; the launch traced here: 16.6 us
  waiting for transfers between devices  7.54 us (45%)
  Pallas kernels  4.83 us (29%)
  starting transfers between devices  3.35 us (20%)
  between operations  0.73 us (4%)
    pallas_call x7, Pallas kernels, call(): pl.pallas_call(kernel, out_shape=[jax.ShapeDtypeStruct(s, f32) for s in s...  4.83 us
    ppermute x1, waiting for transfers between devices, body(): xa = lax.ppermute(xa, AXES, pair_swaps(sizes, 0, 0))  2.27 us
    ppermute x1, waiting for transfers between devices, body(): yb = lax.ppermute(yb, AXES, pair_swaps(sizes, 1, 1))  2.1 us
    ppermute x1, starting transfers between devices, body(): xa = lax.ppermute(xa, AXES, pair_swaps(sizes, 0, 0))  1.64 us
    ppermute x1, waiting for transfers between devices, body(): xb = lax.ppermute(xb, AXES, pair_swaps(sizes, 0, 1))  1.58 us
    ppermute x1, starting transfers between devices, body(): yb = lax.ppermute(yb, AXES, pair_swaps(sizes, 1, 1))  1.5 us
    ppermute x1, waiting for transfers between devices, body(): zin = lax.ppermute(zmsg, AXES, swap)  1.05 us
    ppermute x1, waiting for transfers between devices, body(): ya = lax.ppermute(ya, AXES, pair_swaps(sizes, 1, 0))  0.53 us
  transfers between devices with their start and end apart: 5, of which 5 were waited for; matrix products, arithmetic and copies ran while one was open for 0% of the time, Pallas kernels for 10%

profile of v5, /device:TPU:20, one launch (start us, length us, event | category | flops | bytes accessed | tf_op | source)
XLA Modules:
  0.0 16.6 jit_solution(13030106995210628234)
XLA Ops:
  0.6 0.0 copy-start.3
  0.6 0.0 copy-start.2
  0.7 0.0 copy-start.1
  0.7 0.0 copy-start
  0.7 1.0 %prepare_z.1 = f32[8,32,128]{2,1,0:T(8,128)S(1)} custom-call(f32[16,32,128]{2,1,0:T(8,128)} %lr_h.1, s32[16,32,128]{2,1,0:T(8,128)} %sea_h.1, f32[16,32,128]{2,1,0:T(8,128)} %src_h.1, f32[16,32,128]{2,1,0:T(8,128)} %cot_h.1), custom_call_target="tpu_custom_call" | custom-call | flops 1000000 | bytes 1048576 | tf_op jit(solution)/shard_map/prepare_z/pallas_call | solution.py:459
  1.7 0.1 collective-permute-start
  1.8 0.0 copy-done.3
  1.8 0.0 copy-done.2
  1.8 0.0 copy-done.1
  1.8 0.1 copy-done
  1.9 0.1 prepare.1
  2.1 1.1 %collective-permute-done.zin = f32[8,32,128]{2,1,0:T(8,128)S(1)} collective-permute-done((f32[8,32,128]{2,1,0:T(8,128)S(1)}, f32[8,32,128]{2,1,0:T(8,128)S(1)}, u32[]{:S(2)}, u32[]{:S(2)}) %collective-permute-start) | collective-permute-done | bytes 131104 | tf_op jit(solution)/shard_map/ppermute | solution.py:486
  3.2 1.6 %collective-permute-start.1 = (f32[17,8,128]{2,1,0:T(8,128)S(1)}, f32[17,8,128]{2,1,0:T(8,128)S(1)}, u32[]{:S(2)}, u32[]{:S(2)}) collective-permute-start(f32[17,8,128]{2,1,0:T(8,128)S(1)} %get-tuple-element.27), channel_id=1, source_target_pairs={{0,8},{1,9},{2,10},{3,11},{4,12},{5,13},{6,14},{7,15},{8,0},{9,1},... | collective-permute-start | bytes 208904 | tf_op jit(solution)/shard_map/ppermute | solution.py:488
  4.8 0.0 collective-permute-start.2
  4.8 0.5 %pack_block.1 = (f32[3,32,128]{2,1,0:T(8,128)S(1)}, f32[3,32,128]{2,1,0:T(8,128)S(1)}, f32[3,32,128]{2,1,0:T(8,128)S(1)}, f32[7,8,128]{2,1,0:T(8,128)S(1)}, f32[7,8,128]{2,1,0:T(8,128)S(1)}) custom-call(f32[16,32,128]{2,1,0:T(8,128)S(1)} %get-tuple-element.21.c_in, f32[16,32,128]{2,1,0:T(8,128)S(1)} %get-tuple-element.22.b_in, ...), custom_call_target="tpu_custom_call" | custom-call | flops 100000000 | bytes 1048576 | tf_op jit(solution)/shard_map/pack_block/pallas_call | solution.py:459
  5.3 2.3 %collective-permute-done.1.xa = f32[17,8,128]{2,1,0:T(8,128)S(1)} collective-permute-done((f32[17,8,128]{2,1,0:T(8,128)S(1)}, f32[17,8,128]{2,1,0:T(8,128)S(1)}, u32[]{:S(2)}, u32[]{:S(2)}) %collective-permute-start.1) | collective-permute-done | bytes 69664 | tf_op jit(solution)/shard_map/ppermute | solution.py:488
  7.5 1.6 %collective-permute-done.2.xb = f32[17,8,128]{2,1,0:T(8,128)S(1)} collective-permute-done((f32[17,8,128]{2,1,0:T(8,128)S(1)}, f32[17,8,128]{2,1,0:T(8,128)S(1)}, u32[]{:S(2)}, u32[]{:S(2)}) %collective-permute-start.2) | collective-permute-done | bytes 69664 | tf_op jit(solution)/shard_map/ppermute | solution.py:489
  9.1 0.2 %pack_halo.1 = (f32[3,8,128]{2,1,0:T(8,128)S(1)}, f32[3,8,128]{2,1,0:T(8,128)S(1)}, f32[3,8,128]{2,1,0:T(8,128)S(1)}, f32[7,8,128]{2,1,0:T(8,128)S(1)}, f32[7,8,128]{2,1,0:T(8,128)S(1)}) custom-call(f32[17,8,128]{2,1,0:T(8,128)S(1)} %collective-permute-done.1.xa, f32[17,8,128]{2,1,0:T(8,128)S(1)} %collective-permute-done.2.xb, ...), custom_call_target="tpu_custom_call" | custom-call | flops 1000000 | bytes 1048576 | tf_op jit(solution)/shard_map/pack_halo/pallas_call | solution.py:459
  9.3 1.5 %collective-permute-start.3 = (f32[7,8,128]{2,1,0:T(8,128)S(1)}, f32[7,8,128]{2,1,0:T(8,128)S(1)}, u32[]{:S(2)}, u32[]{:S(2)}) collective-permute-start(f32[7,8,128]{2,1,0:T(8,128)S(1)} %get-tuple-element.34), channel_id=1, source_target_pairs={{0,1},{1,0},{2,4},{3,5},{4,2},{5,3},{6,7},{7,6},{8,9},{9,8},{10,12... | collective-permute-start | bytes 86024 | tf_op jit(solution)/shard_map/ppermute | solution.py:503
  10.8 0.1 collective-permute-start.4
  11.0 1.1 %main.1 = (f32[16,32,128]{2,1,0:T(8,128)S(1)}, f32[16,32,128]{2,1,0:T(8,128)S(1)}) custom-call(f32[16,32,128]{2,1,0:T(8,128)S(1)} %get-tuple-element.21.c_in, f32[16,32,128]{2,1,0:T(8,128)S(1)} %get-tuple-element.22.b_in, f32[16,32,128]{2,1,0:T(8,128)S(1)} %get-tuple-element.23.h_in, f32[8,32,128]{2,1,0:T(8,128)S(1)} %collective-permute-done.zin, ...), custom_call_target="tpu_custom_call" | custom-call | flops 200000000 | bytes 1048576 | tf_op jit(solution)/shard_map/main/pallas_call | solution.py:459
  12.1 2.1 %collective-permute-done.3.yb = f32[7,8,128]{2,1,0:T(8,128)S(1)} collective-permute-done((f32[7,8,128]{2,1,0:T(8,128)S(1)}, f32[7,8,128]{2,1,0:T(8,128)S(1)}, u32[]{:S(2)}, u32[]{:S(2)}) %collective-permute-start.3) | collective-permute-done | bytes 28704 | tf_op jit(solution)/shard_map/ppermute | solution.py:503
  14.2 0.5 %collective-permute-done.4.ya = f32[7,8,128]{2,1,0:T(8,128)S(1)} collective-permute-done((f32[7,8,128]{2,1,0:T(8,128)S(1)}, f32[7,8,128]{2,1,0:T(8,128)S(1)}, u32[]{:S(2)}, u32[]{:S(2)}) %collective-permute-start.4) | collective-permute-done | bytes 28704 | tf_op jit(solution)/shard_map/ppermute | solution.py:504
  14.7 1.9 %edge.1 = (f32[16,32,128]{2,1,0:T(8,128)}, f32[16,32,128]{2,1,0:T(8,128)}) custom-call(f32[3,32,128]{2,1,0:T(8,128)S(1)} %get-tuple-element.24.pc, f32[3,32,128]{2,1,0:T(8,128)S(1)} %get-tuple-element.25.pb, f32[3,32,128]{2,1,0:T(8,128)S(1)} %get-tuple-element.26.ph, f32[3,8,128]{2,1,0:T(8,128)S(1)} %get-tuple-element.31.qc, ...), custom_call_target="tpu_custom_call" | custom-call | flops 1000000 | bytes 1048576 | tf_op jit(solution)/shard_map/edge/pallas_call | solution.py:459
  (1 shorter events, 0.0 us)
Async XLA Ops:
  0.6 1.2 %copy-start.3 = (f32[16,32,128]{2,1,0:T(8,128)S(1)}, f32[16,32,128]{2,1,0:T(8,128)}, u32[]{:S(2)}) copy-start(f32[16,32,128]{2,1,0:T(8,128)} %cot_h.1) | copy-start | bytes 786436
  0.6 1.2 %copy-start.2 = (f32[16,32,128]{2,1,0:T(8,128)S(1)}, f32[16,32,128]{2,1,0:T(8,128)}, u32[]{:S(2)}) copy-start(f32[16,32,128]{2,1,0:T(8,128)} %src_h.1) | copy-start | bytes 786436
  0.7 1.2 %copy-start.1 = (s32[16,32,128]{2,1,0:T(8,128)S(1)}, s32[16,32,128]{2,1,0:T(8,128)}, u32[]{:S(2)}) copy-start(s32[16,32,128]{2,1,0:T(8,128)} %sea_h.1) | copy-start | bytes 786436
  0.7 1.3 %copy-start = (f32[16,32,128]{2,1,0:T(8,128)S(1)}, f32[16,32,128]{2,1,0:T(8,128)}, u32[]{:S(2)}) copy-start(f32[16,32,128]{2,1,0:T(8,128)} %lr_h.1) | copy-start | bytes 786436
  1.7 1.4 %collective-permute-start = (f32[8,32,128]{2,1,0:T(8,128)S(1)}, f32[8,32,128]{2,1,0:T(8,128)S(1)}, u32[]{:S(2)}, u32[]{:S(2)}) collective-permute-start(f32[8,32,128]{2,1,0:T(8,128)S(1)} %prepare_z.1), channel_id=1, source_target_pairs={{0,1},{1,0},{2,3},{3,2},{4,5},{5,4},{6,7},{7,6},{8,9},{9,8},{10,11... | collective-permute-start | bytes 393224 | tf_op jit(solution)/shard_map/ppermute | solution.py:486
  3.2 4.4 %collective-permute-start.1 = (f32[17,8,128]{2,1,0:T(8,128)S(1)}, f32[17,8,128]{2,1,0:T(8,128)S(1)}, u32[]{:S(2)}, u32[]{:S(2)}) collective-permute-start(f32[17,8,128]{2,1,0:T(8,128)S(1)} %get-tuple-element.27), channel_id=1, source_target_pairs={{0,8},{1,9},{2,10},{3,11},{4,12},{5,13},{6,14},{7,15},{8,0},{9,1},... | collective-permute-start | bytes 208904 | tf_op jit(solution)/shard_map/ppermute | solution.py:488
  4.8 4.3 %collective-permute-start.2 = (f32[17,8,128]{2,1,0:T(8,128)S(1)}, f32[17,8,128]{2,1,0:T(8,128)S(1)}, u32[]{:S(2)}, u32[]{:S(2)}) collective-permute-start(f32[17,8,128]{2,1,0:T(8,128)S(1)} %get-tuple-element.28), channel_id=1, source_target_pairs={{0,1},{1,0},{2,3},{3,2},{4,5},{5,4},{6,7},{7,6},{8,16},{9,17},{10,... | collective-permute-start | bytes 208904 | tf_op jit(solution)/shard_map/ppermute | solution.py:489
  9.3 4.8 %collective-permute-start.3 = (f32[7,8,128]{2,1,0:T(8,128)S(1)}, f32[7,8,128]{2,1,0:T(8,128)S(1)}, u32[]{:S(2)}, u32[]{:S(2)}) collective-permute-start(f32[7,8,128]{2,1,0:T(8,128)S(1)} %get-tuple-element.34), channel_id=1, source_target_pairs={{0,1},{1,0},{2,4},{3,5},{4,2},{5,3},{6,7},{7,6},{8,9},{9,8},{10,12... | collective-permute-start | bytes 86024 | tf_op jit(solution)/shard_map/ppermute | solution.py:503
  10.8 3.9 %collective-permute-start.4 = (f32[7,8,128]{2,1,0:T(8,128)S(1)}, f32[7,8,128]{2,1,0:T(8,128)S(1)}, u32[]{:S(2)}, u32[]{:S(2)}) collective-permute-start(f32[7,8,128]{2,1,0:T(8,128)S(1)} %get-tuple-element.35), channel_id=1, source_target_pairs={{0,2},{1,3},{2,0},{3,1},{4,6},{5,7},{6,4},{7,5},{8,10},{9,11},{10,... | collective-permute-start | bytes 86024 | tf_op jit(solution)/shard_map/ppermute | solution.py:504

commit v6 on v5

--- a/solution.py
+++ b/solution.py
@@ -399,24 +399,25 @@
         sides = pltpu.roll(here, 1, 1) + pltpu.roll(here, LANES - 1, 1)
         return total + (down + up) + sides, here
 
-    def step(src, source, out):
+    def advance(v, t, src, source, out):
+        rows = tile_rows(t)
+        total, here = spread(src, v, t)
+        value = cs[v, rows, :] * total
+        if source is not None:
+            value = source[v, rows, :] + value
+        put(out, v, t, KEEP * here + value)
+
+    for chains in (((hs, None, h1), (bs, bs, y1)), ((h1, None, h2), (y1, bs, y2))):
+        for t in range(tiles):
+            for v in range(STRIDE):
+                for chain in chains:
+                    advance(v, t, *chain)
+    rim = (lane < DEPTH) | (lane >= LANES - DEPTH)
+    copies = []
+    for t in range(1, tiles):
+        rows, block = tile_rows(t), tile_rows(t - 1)
+        its, ss = [], []
         for v in range(STRIDE):
-            for t in range(tiles):
-                rows = tile_rows(t)
-                total, here = spread(src, v, t)
-                value = cs[v, rows, :] * total
-                if source is not None:
-                    value = source[v, rows, :] + value
-                put(out, v, t, KEEP * here + value)
-
-    step(hs, None, h1)
-    step(bs, bs, y1)
-    step(h1, None, h2)
-    step(y1, bs, y2)
-    its, ss = {}, {}
-    for v in range(STRIDE):
-        for t in range(1, tiles):
-            rows = tile_rows(t)
             c, b = cs[v, rows, :], bs[v, rows, :]
             total_h, g2 = spread(h2, v, t)
             total_y, x3 = spread(y2, v, t)
@@ -427,22 +428,20 @@
             s = (g1 * b + g2 * (x2 - KEEP * b)) + (
                 h1[v, rows, :] * (x3 - KEEP * x2) + hs[v, rows, :] * w3
             )
-            its[v, t] = jnp.where(place < OWN, it, pltpu.roll(it, LANES - OWN, 1))
-            ss[v, t] = jnp.where(place < OWN, s, pltpu.roll(s, LANES - OWN, 1))
-    rim = (lane < DEPTH) | (lane >= LANES - DEPTH)
-    copies = []
-    for k in range(lz):
-        z = level(k, lz)
-        g, v = (k + DEPTH) // STRIDE, (k + DEPTH) % STRIDE
-        shift = (LANES - DEPTH - (GROUP * g + DEPTH)) % LANES
-        for t in range(1, tiles):
-            block = tile_rows(t - 1)
-            it = jnp.where(rim, pltpu.roll(its[v, t], shift, 1), it_in[k, block, :])
-            s = jnp.where(rim, pltpu.roll(ss[v, t], shift, 1), s_in[k, block, :])
-            it_out[k, block, :] = it + land_in[k, block, :]
-            rg_out[k, block, :] = e_in[k, block, :] * s
+            its.append(jnp.where(place < OWN, it, pltpu.roll(it, LANES - OWN, 1)))
+            ss.append(jnp.where(place < OWN, s, pltpu.roll(s, LANES - OWN, 1)))
+        for k in range(lz):
+            z = level(k, lz)
+            g, v = (k + DEPTH) // STRIDE, (k + DEPTH) % STRIDE
+            shift = (LANES - DEPTH - (GROUP * g + DEPTH)) % LANES
+            it = jnp.where(rim, pltpu.roll(its[v], shift, 1), it_in[k, block, :])
+            s = jnp.where(rim, pltpu.roll(ss[v], shift, 1), s_in[k, block, :])
+            it_out[z, block, :] = it + land_in[k, block, :]
+            rg_out[z, block, :] = e_in[k, block, :] * s
         for i, (a, b) in enumerate(((it_out, it_hbm), (rg_out, rg_hbm))):
-            copies.append(pltpu.make_async_copy(a.at[k], b.at[z], sem.at[i, k]))
+            copies.append(
+                pltpu.make_async_copy(a.at[:, block], b.at[:, block], sem.at[i, t - 1])
+            )
             copies[-1].start()
     for copy in copies:
         copy.wait()
@@ -515,7 +514,7 @@
         [block] * 2,
         (pc, pb, ph, qc, qb, qh, yb, ya, it, s, e, land),
         "edge",
-        [strip] * 7 + [block] * 2 + [pltpu.SemaphoreType.DMA((2, lz))],
+        [strip] * 7 + [block] * 2 + [pltpu.SemaphoreType.DMA((2, lx // SUB))],
         outs=hbm,
     )
 

time: 16.8 us -> 16.4 us (0.976)
  Pallas kernels: 4.83 us -> 4.45 us
    pallas_call x7, Pallas kernels: 4.83 us -> 4.45 us  [call(): pl.pallas_call(kernel, out_shape=[jax.ShapeDtypeStruct(s, f32) for s in s...]
where the time goes in v6:
time: 16.4 us; the launch traced here: 16.2 us
  waiting for transfers between devices  7.54 us (46%)
  Pallas kernels  4.45 us (27%)
  starting transfers between devices  3.35 us (20%)
  between operations  0.73 us (4%)
    pallas_call x7, Pallas kernels, call(): pl.pallas_call(kernel, out_shape=[jax.ShapeDtypeStruct(s, f32) for s in s...  4.45 us
    ppermute x1, waiting for transfers between devices, body(): xa = lax.ppermute(xa, AXES, pair_swaps(sizes, 0, 0))  2.27 us
    ppermute x1, waiting for transfers between devices, body(): yb = lax.ppermute(yb, AXES, pair_swaps(sizes, 1, 1))  2.1 us
    ppermute x1, starting transfers between devices, body(): xa = lax.ppermute(xa, AXES, pair_swaps(sizes, 0, 0))  1.64 us
    ppermute x1, waiting for transfers between devices, body(): xb = lax.ppermute(xb, AXES, pair_swaps(sizes, 0, 1))  1.58 us
    ppermute x1, starting transfers between devices, body(): yb = lax.ppermute(yb, AXES, pair_swaps(sizes, 1, 1))  1.5 us
    ppermute x1, waiting for transfers between devices, body(): zin = lax.ppermute(zmsg, AXES, swap)  1.05 us
    ppermute x1, waiting for transfers between devices, body(): ya = lax.ppermute(ya, AXES, pair_swaps(sizes, 1, 0))  0.53 us
  transfers between devices with their start and end apart: 5, of which 5 were waited for; matrix products, arithmetic and copies ran while one was open for 0% of the time, Pallas kernels for 10%

profile of v6, /device:TPU:20, one launch (start us, length us, event | category | flops | bytes accessed | tf_op | source)
XLA Modules:
  0.0 16.2 jit_solution(1260437446843237435)
XLA Ops:
  0.6 0.0 copy-start.3
  0.6 0.0 copy-start.2
  0.7 0.0 copy-start.1
  0.7 0.0 copy-start
  0.7 1.0 %prepare_z.1 = f32[8,32,128]{2,1,0:T(8,128)S(1)} custom-call(f32[16,32,128]{2,1,0:T(8,128)} %lr_h.1, s32[16,32,128]{2,1,0:T(8,128)} %sea_h.1, f32[16,32,128]{2,1,0:T(8,128)} %src_h.1, f32[16,32,128]{2,1,0:T(8,128)} %cot_h.1), custom_call_target="tpu_custom_call" | custom-call | flops 1000000 | bytes 1048576 | tf_op jit(solution)/shard_map/prepare_z/pallas_call | solution.py:458
  1.7 0.1 collective-permute-start
  1.8 0.0 copy-done.3
  1.8 0.0 copy-done.2
  1.8 0.0 copy-done.1
  1.8 0.1 copy-done
  1.9 0.1 prepare.1
  2.1 1.1 %collective-permute-done.zin = f32[8,32,128]{2,1,0:T(8,128)S(1)} collective-permute-done((f32[8,32,128]{2,1,0:T(8,128)S(1)}, f32[8,32,128]{2,1,0:T(8,128)S(1)}, u32[]{:S(2)}, u32[]{:S(2)}) %collective-permute-start) | collective-permute-done | bytes 131104 | tf_op jit(solution)/shard_map/ppermute | solution.py:485
  3.2 1.6 %collective-permute-start.1 = (f32[17,8,128]{2,1,0:T(8,128)S(1)}, f32[17,8,128]{2,1,0:T(8,128)S(1)}, u32[]{:S(2)}, u32[]{:S(2)}) collective-permute-start(f32[17,8,128]{2,1,0:T(8,128)S(1)} %get-tuple-element.27), channel_id=1, source_target_pairs={{0,8},{1,9},{2,10},{3,11},{4,12},{5,13},{6,14},{7,15},{8,0},{9,1},... | collective-permute-start | bytes 208904 | tf_op jit(solution)/shard_map/ppermute | solution.py:487
  4.8 0.0 collective-permute-start.2
  4.8 0.5 %pack_block.1 = (f32[3,32,128]{2,1,0:T(8,128)S(1)}, f32[3,32,128]{2,1,0:T(8,128)S(1)}, f32[3,32,128]{2,1,0:T(8,128)S(1)}, f32[7,8,128]{2,1,0:T(8,128)S(1)}, f32[7,8,128]{2,1,0:T(8,128)S(1)}) custom-call(f32[16,32,128]{2,1,0:T(8,128)S(1)} %get-tuple-element.21.c_in, f32[16,32,128]{2,1,0:T(8,128)S(1)} %get-tuple-element.22.b_in, ...), custom_call_target="tpu_custom_call" | custom-call | flops 100000000 | bytes 1048576 | tf_op jit(solution)/shard_map/pack_block/pallas_call | solution.py:458
  5.3 2.3 %collective-permute-done.1.xa = f32[17,8,128]{2,1,0:T(8,128)S(1)} collective-permute-done((f32[17,8,128]{2,1,0:T(8,128)S(1)}, f32[17,8,128]{2,1,0:T(8,128)S(1)}, u32[]{:S(2)}, u32[]{:S(2)}) %collective-permute-start.1) | collective-permute-done | bytes 69664 | tf_op jit(solution)/shard_map/ppermute | solution.py:487
  7.5 1.6 %collective-permute-done.2.xb = f32[17,8,128]{2,1,0:T(8,128)S(1)} collective-permute-done((f32[17,8,128]{2,1,0:T(8,128)S(1)}, f32[17,8,128]{2,1,0:T(8,128)S(1)}, u32[]{:S(2)}, u32[]{:S(2)}) %collective-permute-start.2) | collective-permute-done | bytes 69664 | tf_op jit(solution)/shard_map/ppermute | solution.py:488
  9.1 0.2 %pack_halo.1 = (f32[3,8,128]{2,1,0:T(8,128)S(1)}, f32[3,8,128]{2,1,0:T(8,128)S(1)}, f32[3,8,128]{2,1,0:T(8,128)S(1)}, f32[7,8,128]{2,1,0:T(8,128)S(1)}, f32[7,8,128]{2,1,0:T(8,128)S(1)}) custom-call(f32[17,8,128]{2,1,0:T(8,128)S(1)} %collective-permute-done.1.xa, f32[17,8,128]{2,1,0:T(8,128)S(1)} %collective-permute-done.2.xb, ...), custom_call_target="tpu_custom_call" | custom-call | flops 1000000 | bytes 1048576 | tf_op jit(solution)/shard_map/pack_halo/pallas_call | solution.py:458
  9.3 1.5 %collective-permute-start.3 = (f32[7,8,128]{2,1,0:T(8,128)S(1)}, f32[7,8,128]{2,1,0:T(8,128)S(1)}, u32[]{:S(2)}, u32[]{:S(2)}) collective-permute-start(f32[7,8,128]{2,1,0:T(8,128)S(1)} %get-tuple-element.34), channel_id=1, source_target_pairs={{0,1},{1,0},{2,4},{3,5},{4,2},{5,3},{6,7},{7,6},{8,9},{9,8},{10,12... | collective-permute-start | bytes 86024 | tf_op jit(solution)/shard_map/ppermute | solution.py:502
  10.8 0.1 collective-permute-start.4
  11.0 1.1 %main.1 = (f32[16,32,128]{2,1,0:T(8,128)S(1)}, f32[16,32,128]{2,1,0:T(8,128)S(1)}) custom-call(f32[16,32,128]{2,1,0:T(8,128)S(1)} %get-tuple-element.21.c_in, f32[16,32,128]{2,1,0:T(8,128)S(1)} %get-tuple-element.22.b_in, f32[16,32,128]{2,1,0:T(8,128)S(1)} %get-tuple-element.23.h_in, f32[8,32,128]{2,1,0:T(8,128)S(1)} %collective-permute-done.zin, ...), custom_call_target="tpu_custom_call" | custom-call | flops 200000000 | bytes 1048576 | tf_op jit(solution)/shard_map/main/pallas_call | solution.py:458
  12.1 2.1 %collective-permute-done.3.yb = f32[7,8,128]{2,1,0:T(8,128)S(1)} collective-permute-done((f32[7,8,128]{2,1,0:T(8,128)S(1)}, f32[7,8,128]{2,1,0:T(8,128)S(1)}, u32[]{:S(2)}, u32[]{:S(2)}) %collective-permute-start.3) | collective-permute-done | bytes 28704 | tf_op jit(solution)/shard_map/ppermute | solution.py:502
  14.2 0.5 %collective-permute-done.4.ya = f32[7,8,128]{2,1,0:T(8,128)S(1)} collective-permute-done((f32[7,8,128]{2,1,0:T(8,128)S(1)}, f32[7,8,128]{2,1,0:T(8,128)S(1)}, u32[]{:S(2)}, u32[]{:S(2)}) %collective-permute-start.4) | collective-permute-done | bytes 28704 | tf_op jit(solution)/shard_map/ppermute | solution.py:503
  14.7 1.5 %edge.1 = (f32[16,32,128]{2,1,0:T(8,128)}, f32[16,32,128]{2,1,0:T(8,128)}) custom-call(f32[3,32,128]{2,1,0:T(8,128)S(1)} %get-tuple-element.24.pc, f32[3,32,128]{2,1,0:T(8,128)S(1)} %get-tuple-element.25.pb, f32[3,32,128]{2,1,0:T(8,128)S(1)} %get-tuple-element.26.ph, f32[3,8,128]{2,1,0:T(8,128)S(1)} %get-tuple-element.31.qc, ...), custom_call_target="tpu_custom_call" | custom-call | flops 1000000 | bytes 1048576 | tf_op jit(solution)/shard_map/edge/pallas_call | solution.py:458
  (1 shorter events, 0.0 us)
Async XLA Ops:
  0.6 1.2 %copy-start.3 = (f32[16,32,128]{2,1,0:T(8,128)S(1)}, f32[16,32,128]{2,1,0:T(8,128)}, u32[]{:S(2)}) copy-start(f32[16,32,128]{2,1,0:T(8,128)} %cot_h.1) | copy-start | bytes 786436
  0.6 1.2 %copy-start.2 = (f32[16,32,128]{2,1,0:T(8,128)S(1)}, f32[16,32,128]{2,1,0:T(8,128)}, u32[]{:S(2)}) copy-start(f32[16,32,128]{2,1,0:T(8,128)} %src_h.1) | copy-start | bytes 786436
  0.7 1.2 %copy-start.1 = (s32[16,32,128]{2,1,0:T(8,128)S(1)}, s32[16,32,128]{2,1,0:T(8,128)}, u32[]{:S(2)}) copy-start(s32[16,32,128]{2,1,0:T(8,128)} %sea_h.1) | copy-start | bytes 786436
  0.7 1.3 %copy-start = (f32[16,32,128]{2,1,0:T(8,128)S(1)}, f32[16,32,128]{2,1,0:T(8,128)}, u32[]{:S(2)}) copy-start(f32[16,32,128]{2,1,0:T(8,128)} %lr_h.1) | copy-start | bytes 786436
  1.7 1.4 %collective-permute-start = (f32[8,32,128]{2,1,0:T(8,128)S(1)}, f32[8,32,128]{2,1,0:T(8,128)S(1)}, u32[]{:S(2)}, u32[]{:S(2)}) collective-permute-start(f32[8,32,128]{2,1,0:T(8,128)S(1)} %prepare_z.1), channel_id=1, source_target_pairs={{0,1},{1,0},{2,3},{3,2},{4,5},{5,4},{6,7},{7,6},{8,9},{9,8},{10,11... | collective-permute-start | bytes 393224 | tf_op jit(solution)/shard_map/ppermute | solution.py:485
  3.2 4.4 %collective-permute-start.1 = (f32[17,8,128]{2,1,0:T(8,128)S(1)}, f32[17,8,128]{2,1,0:T(8,128)S(1)}, u32[]{:S(2)}, u32[]{:S(2)}) collective-permute-start(f32[17,8,128]{2,1,0:T(8,128)S(1)} %get-tuple-element.27), channel_id=1, source_target_pairs={{0,8},{1,9},{2,10},{3,11},{4,12},{5,13},{6,14},{7,15},{8,0},{9,1},... | collective-permute-start | bytes 208904 | tf_op jit(solution)/shard_map/ppermute | solution.py:487
  4.8 4.3 %collective-permute-start.2 = (f32[17,8,128]{2,1,0:T(8,128)S(1)}, f32[17,8,128]{2,1,0:T(8,128)S(1)}, u32[]{:S(2)}, u32[]{:S(2)}) collective-permute-start(f32[17,8,128]{2,1,0:T(8,128)S(1)} %get-tuple-element.28), channel_id=1, source_target_pairs={{0,1},{1,0},{2,3},{3,2},{4,5},{5,4},{6,7},{7,6},{8,16},{9,17},{10,... | collective-permute-start | bytes 208904 | tf_op jit(solution)/shard_map/ppermute | solution.py:488
  9.3 4.8 %collective-permute-start.3 = (f32[7,8,128]{2,1,0:T(8,128)S(1)}, f32[7,8,128]{2,1,0:T(8,128)S(1)}, u32[]{:S(2)}, u32[]{:S(2)}) collective-permute-start(f32[7,8,128]{2,1,0:T(8,128)S(1)} %get-tuple-element.34), channel_id=1, source_target_pairs={{0,1},{1,0},{2,4},{3,5},{4,2},{5,3},{6,7},{7,6},{8,9},{9,8},{10,12... | collective-permute-start | bytes 86024 | tf_op jit(solution)/shard_map/ppermute | solution.py:502
  10.8 3.9 %collective-permute-start.4 = (f32[7,8,128]{2,1,0:T(8,128)S(1)}, f32[7,8,128]{2,1,0:T(8,128)S(1)}, u32[]{:S(2)}, u32[]{:S(2)}) collective-permute-start(f32[7,8,128]{2,1,0:T(8,128)S(1)} %get-tuple-element.35), channel_id=1, source_target_pairs={{0,2},{1,3},{2,0},{3,1},{4,6},{5,7},{6,4},{7,5},{8,10},{9,11},{10,... | collective-permute-start | bytes 86024 | tf_op jit(solution)/shard_map/ppermute | solution.py:503

commit v7 on v6

--- a/solution.py
+++ b/solution.py
@@ -167,16 +167,21 @@
     return jnp.where(inside, group, -1), jnp.where(inside, lane - GROUP * group, -1)
 
 
-BLOCK_FIELDS = ((1, DEPTH, 0), (2, DEPTH, DEPTH), (0, DEPTH, 2 * DEPTH))
-HALO_FIELDS = ((1, DEPTH - 1, 0), (2, DEPTH - 1, DEPTH - 1), (0, DEPTH - 2, 2 * DEPTH - 2))
-
-
 def message_slot(v, t, tiles):
     if t == 0:
-        return 0, OWN * v
+        depth = DEPTH - 1
+        return 0, {
+            1: (depth * v, depth),
+            2: (depth * (STRIDE + v), depth),
+            0: (2 * depth * STRIDE + v + 1, depth - 1),
+        }
     if v < STRIDE - 1:
-        return t, GROUP // 2 * v
-    return tiles + (t - 1) // 2, GROUP // 2 * ((t - 1) % 2)
+        slot, second = t, v
+    else:
+        slot, second = tiles + (t - 1) // 2, (t - 1) % 2
+    return slot, {
+        f: (2 * DEPTH * i + DEPTH * second, DEPTH) for i, f in enumerate((1, 2, 0))
+    }
 
 
 def message_length(tiles):
@@ -187,41 +192,57 @@
     return pltpu.roll(x, shift % LANES, 1) if shift % LANES else x
 
 
-def pack_own(levels, first, count, tiles, place, group, sweep):
+def window(first, depth):
+    return first + depth - OWN
+
+
+def packed_own(packed, start, place):
+    return jnp.where(
+        place < OWN, lane_roll(packed, -start),
+        jnp.where(place >= GROUP - OWN, lane_roll(packed, OWN - start), 0.0),
+    )
+
+
+def pack_edges(levels, first, count, tiles, lane, place, sweep):
     zero = jnp.zeros((SUB, LANES), jnp.float32)
-    raw = jnp.where(place < 2 * OWN, group, -1)
-    acc = [[[zero] * count for _ in range(STRIDE)] for _ in range(3)]
+    groups = {}
+
+    def group_from(start):
+        if start not in groups:
+            at = lane - start
+            at = jnp.where(at < 0, at + LANES, jnp.where(at >= LANES, at - LANES, at))
+            group = at // GROUP
+            groups[start] = jnp.where(at - GROUP * group < 2 * OWN, group, -1)
+        return groups[start]
+
+    acc = {}
     for z in range(levels):
         g, v = z // STRIDE, z % STRIDE
         for f in range(3):
             for t, tile in enumerate(sweep(f, z)):
+                start = window(*message_slot(v, first + t, tiles)[1][f])
+                old = acc.get((f, v, t), zero)
                 if tile is not None:
-                    acc[f][v][t] = jnp.where(
-                        raw == g, pltpu.roll(tile, (GROUP * g + OWN) % LANES, 1), acc[f][v][t]
-                    )
-    own = [[[None] * count for _ in range(STRIDE)] for _ in range(3)]
+                    moved = lane_roll(tile, GROUP * g + start + OWN)
+                    old = jnp.where(group_from(start) == g, moved, old)
+                acc[f, v, t] = old
+    parts = [{}, {}]
+    for t in range(count):
+        for v in range(STRIDE):
+            slot, fields = message_slot(v, first + t, tiles)
+            for f, (at, depth) in fields.items():
+                for side in range(2):
+                    begin = (at + side * depth) % GROUP
+                    parts[side].setdefault(slot, []).append((begin, acc[f, v, t]))
     sides = [{}, {}]
-    for t in range(count):
-        fields = BLOCK_FIELDS if first + t else HALO_FIELDS
-        for v in range(STRIDE):
-            slot, base = message_slot(v, first + t, tiles)
-            for side in range(2):
-                message = sides[side].get(slot)
-                for f, depth, offset in fields:
-                    at = OWN - depth if side == 0 else OWN
-                    part = lane_roll(acc[f][v][t], base + offset - at)
-                    if message is None:
-                        message = part
-                    else:
-                        message = jnp.where(place >= base + offset, part, message)
-                sides[side][slot] = message
-            for f in range(3):
-                a = acc[f][v][t]
-                moved = pltpu.roll(a, GROUP - 2 * OWN, 1)
-                own[f][v][t] = jnp.where(
-                    place < OWN, a, jnp.where(place >= GROUP - OWN, moved, 0.0)
-                )
-    return own, sides
+    for side in range(2):
+        for slot, pieces in parts[side].items():
+            pieces.sort(key=lambda piece: piece[0])
+            message = pieces[0][1]
+            for begin, piece in pieces[1:]:
+                message = jnp.where(place >= begin, piece, message)
+            sides[side][slot] = message
+    return acc, sides
 
 
 def put_messages(ya, yb, sides, odd):
@@ -233,7 +254,8 @@
 
 def pack_block_kernel(c_in, b_in, h_in, zin, pc_out, pb_out, ph_out, ya, yb):
     lz, lx, _ = c_in.shape
-    group, place = packed_place(iota(1), lz)
+    lane = iota(1)
+    _, place = packed_place(lane, lz)
     odd = lax.axis_index("gy") % 2 == 1
     tiles = lx // SUB
 
@@ -245,17 +267,19 @@
         )[f])
         return [None if ref is None else ref[i, tile_rows(t), :] for t in range(tiles)]
 
-    own, sides = pack_own(lz + DEPTH, 1, tiles, tiles + 1, place, group, sweep)
+    packed, sides = pack_edges(lz + DEPTH, 1, tiles, tiles + 1, lane, place, sweep)
     put_messages(ya, yb, sides, odd)
     for t in range(tiles):
-        for f, ref in enumerate((pc_out, pb_out, ph_out)):
-            for v in range(STRIDE):
-                ref[v, tile_rows(t), :] = own[f][v][t]
+        for v in range(STRIDE):
+            _, fields = message_slot(v, t + 1, tiles + 1)
+            for f, ref in enumerate((pc_out, pb_out, ph_out)):
+                ref[v, tile_rows(t), :] = packed_own(packed[f, v, t], window(*fields[f]), place)
 
 
 def pack_halo_kernel(nx, lz, xa, xb, ya_in, yb_in, pc_out, pb_out, ph_out, yb, ya):
     ix = lax.axis_index("gx")
-    group, place = packed_place(iota(1), lz)
+    lane = iota(1)
+    _, place = packed_place(lane, lz)
     odd = lax.axis_index("gy") % 2 == 1
     row = iota(0)
     parts = {}
@@ -263,24 +287,29 @@
     def sweep(f, z):
         if z not in parts:
             parts[z] = x_halo(xa, xb, z, ix, nx, row)
-        return [parts[z][(f + 2) % 3]]
-
-    own, sides = pack_own(lz + DEPTH, 0, 1, 0, place, group, sweep)
+        return [parts[z][(f + 2) % 3] if z >= (2, 1, 1)[f] else None]
+
+    packed, sides = pack_edges(lz + DEPTH, 0, 1, 0, lane, place, sweep)
     put_messages(ya, yb, sides, odd)
     for src, dst in ((ya_in, ya), (yb_in, yb)):
         for i in range(1, src.shape[0]):
             dst[i] = src[i]
     for f, ref in enumerate((pc_out, pb_out, ph_out)):
         for v in range(STRIDE):
-            ref[v] = own[f][v][0]
-
-
-def main_kernel(nx, c_in, b_in, h_in, zin, xa, xb, it_out, s_out, cm, bm, hm, y1, y2, h1, h2):
+            ref[v] = packed[f, v, 0]
+
+
+def main_kernel(nx, c_in, b_in, h_in, zin, xa, xb, uc, ub, uh, it_out, s_out, qc, qb, qh, cm, bm, hm, y1, y2, h1, h2):
     lz, lx, _ = it_out.shape
     tiles = lx // SUB + 1
     halo = tile_rows(tiles)
     zero = jnp.zeros((SUB, LANES), jnp.float32)
     ix, row = lax.axis_index("gx"), iota(0)
+    _, place = packed_place(iota(1), lz)
+    for v in range(STRIDE):
+        _, fields = message_slot(v, 0, tiles)
+        for f, (src, dst) in enumerate(((uc, qc), (ub, qb), (uh, qh))):
+            dst[v] = packed_own(src[v], window(*fields[f]), place)
     for z in range(lz + DEPTH):
         parts = x_halo(xa, xb, z, ix, nx, row)
         local = (
@@ -374,14 +403,14 @@
     blocks, halos = (pc, pb, ph), (qc, qb, qh)
     for t in range(tiles):
         for v in range(STRIDE):
-            slot, base = message_slot(v, t, tiles)
+            slot, fields = message_slot(v, t, tiles)
             lo, hi = slots[slot]
-            for f, depth, offset in BLOCK_FIELDS if t else HALO_FIELDS:
+            for f, (first, depth) in fields.items():
                 end = OWN + 2 * DEPTH
                 before = (place >= end - depth) & (place < end)
                 after = (place >= OWN) & (place < OWN + depth)
-                from_lo = lane_roll(lo, end - depth - base - offset)
-                from_hi = lane_roll(hi, OWN - base - offset)
+                from_lo = lane_roll(lo, end - depth - first)
+                from_hi = lane_roll(hi, OWN - first - depth)
                 own = blocks[f][v, tile_rows(t - 1), :] if t else halos[f][v]
                 put(stores[f], v, t, jnp.where(before, from_lo, jnp.where(after, from_hi, own)))
 
@@ -493,7 +522,7 @@
         "pack_block",
         flops=10**8,
     )
-    qc, qb, qh, yb, ya = call(
+    uc, ub, uh, yb, ya = call(
         functools.partial(pack_halo_kernel, nx, lz),
         [(STRIDE, SUB, LANES)] * 3 + [(slots, SUB, LANES)] * 2,
         (xa, xb, ya, yb),
@@ -501,10 +530,10 @@
     )
     yb = lax.ppermute(yb, AXES, pair_swaps(sizes, 1, 1))
     ya = lax.ppermute(ya, AXES, pair_swaps(sizes, 1, 0))
-    it, s = call(
+    it, s, qc, qb, qh = call(
         functools.partial(main_kernel, nx),
-        [block] * 2,
-        (c, b, h, zin, xa, xb),
+        [block] * 2 + [(STRIDE, SUB, LANES)] * 3,
+        (c, b, h, zin, xa, xb, uc, ub, uh),
         "main",
         [store] * 7,
         flops=2 * 10**8,

time: 16.4 us -> 16.3 us (level)
  no operation moved by 1% of the time
where the time goes in v7:
time: 16.3 us; the launch traced here: 16.1 us
  waiting for transfers between devices  7.56 us (46%)
  Pallas kernels  4.35 us (27%)
  starting transfers between devices  3.35 us (21%)
  between operations  0.72 us (4%)
    pallas_call x7, Pallas kernels, call(): pl.pallas_call(kernel, out_shape=[jax.ShapeDtypeStruct(s, f32) for s in s...  4.35 us
    ppermute x1, waiting for transfers between devices, body(): xa = lax.ppermute(xa, AXES, pair_swaps(sizes, 0, 0))  2.3 us
    ppermute x1, waiting for transfers between devices, body(): yb = lax.ppermute(yb, AXES, pair_swaps(sizes, 1, 1))  2.1 us
    ppermute x1, starting transfers between devices, body(): xa = lax.ppermute(xa, AXES, pair_swaps(sizes, 0, 0))  1.64 us
    ppermute x1, waiting for transfers between devices, body(): xb = lax.ppermute(xb, AXES, pair_swaps(sizes, 0, 1))  1.58 us
    ppermute x1, starting transfers between devices, body(): yb = lax.ppermute(yb, AXES, pair_swaps(sizes, 1, 1))  1.5 us
    ppermute x1, waiting for transfers between devices, body(): zin = lax.ppermute(zmsg, AXES, swap)  1.05 us
    ppermute x1, waiting for transfers between devices, body(): ya = lax.ppermute(ya, AXES, pair_swaps(sizes, 1, 0))  0.53 us
  transfers between devices with their start and end apart: 5, of which 5 were waited for; matrix products, arithmetic and copies ran while one was open for 0% of the time, Pallas kernels for 10%

profile of v7, /device:TPU:20, one launch (start us, length us, event | category | flops | bytes accessed | tf_op | source)
XLA Modules:
  0.0 16.1 jit_solution(4769816721335577321)
XLA Ops:
  0.6 0.0 copy-start.3
  0.6 0.0 copy-start.2
  0.7 0.0 copy-start.1
  0.7 0.0 copy-start
  0.7 1.0 %prepare_z.1 = f32[8,32,128]{2,1,0:T(8,128)S(1)} custom-call(f32[16,32,128]{2,1,0:T(8,128)} %lr_h.1, s32[16,32,128]{2,1,0:T(8,128)} %sea_h.1, f32[16,32,128]{2,1,0:T(8,128)} %src_h.1, f32[16,32,128]{2,1,0:T(8,128)} %cot_h.1), custom_call_target="tpu_custom_call" | custom-call | flops 1000000 | bytes 1048576 | tf_op jit(solution)/shard_map/prepare_z/pallas_call | solution.py:487
  1.7 0.1 collective-permute-start
  1.8 0.0 copy-done.3
  1.8 0.0 copy-done.2
  1.8 0.0 copy-done.1
  1.8 0.1 copy-done
  1.9 0.1 prepare.1
  2.1 1.1 %collective-permute-done.zin = f32[8,32,128]{2,1,0:T(8,128)S(1)} collective-permute-done((f32[8,32,128]{2,1,0:T(8,128)S(1)}, f32[8,32,128]{2,1,0:T(8,128)S(1)}, u32[]{:S(2)}, u32[]{:S(2)}) %collective-permute-start) | collective-permute-done | bytes 131104 | tf_op jit(solution)/shard_map/ppermute | solution.py:514
  3.2 1.6 %collective-permute-start.1 = (f32[17,8,128]{2,1,0:T(8,128)S(1)}, f32[17,8,128]{2,1,0:T(8,128)S(1)}, u32[]{:S(2)}, u32[]{:S(2)}) collective-permute-start(f32[17,8,128]{2,1,0:T(8,128)S(1)} %get-tuple-element.30), channel_id=1, source_target_pairs={{0,8},{1,9},{2,10},{3,11},{4,12},{5,13},{6,14},{7,15},{8,0},{9,1},... | collective-permute-start | bytes 208904 | tf_op jit(solution)/shard_map/ppermute | solution.py:516
  4.8 0.0 collective-permute-start.2
  4.8 0.4 %pack_block.1 = (f32[3,32,128]{2,1,0:T(8,128)S(1)}, f32[3,32,128]{2,1,0:T(8,128)S(1)}, f32[3,32,128]{2,1,0:T(8,128)S(1)}, f32[7,8,128]{2,1,0:T(8,128)S(1)}, f32[7,8,128]{2,1,0:T(8,128)S(1)}) custom-call(f32[16,32,128]{2,1,0:T(8,128)S(1)} %get-tuple-element.24.c_in, f32[16,32,128]{2,1,0:T(8,128)S(1)} %get-tuple-element.25.b_in, ...), custom_call_target="tpu_custom_call" | custom-call | flops 100000000 | bytes 1048576 | tf_op jit(solution)/shard_map/pack_block/pallas_call | solution.py:487
  5.2 2.3 %collective-permute-done.1.xa = f32[17,8,128]{2,1,0:T(8,128)S(1)} collective-permute-done((f32[17,8,128]{2,1,0:T(8,128)S(1)}, f32[17,8,128]{2,1,0:T(8,128)S(1)}, u32[]{:S(2)}, u32[]{:S(2)}) %collective-permute-start.1) | collective-permute-done | bytes 69664 | tf_op jit(solution)/shard_map/ppermute | solution.py:516
  7.5 1.6 %collective-permute-done.2.xb = f32[17,8,128]{2,1,0:T(8,128)S(1)} collective-permute-done((f32[17,8,128]{2,1,0:T(8,128)S(1)}, f32[17,8,128]{2,1,0:T(8,128)S(1)}, u32[]{:S(2)}, u32[]{:S(2)}) %collective-permute-start.2) | collective-permute-done | bytes 69664 | tf_op jit(solution)/shard_map/ppermute | solution.py:517
  9.1 0.1 pack_halo.1
  9.2 1.5 %collective-permute-start.3 = (f32[7,8,128]{2,1,0:T(8,128)S(1)}, f32[7,8,128]{2,1,0:T(8,128)S(1)}, u32[]{:S(2)}, u32[]{:S(2)}) collective-permute-start(f32[7,8,128]{2,1,0:T(8,128)S(1)} %get-tuple-element.40), channel_id=1, source_target_pairs={{0,1},{1,0},{2,4},{3,5},{4,2},{5,3},{6,7},{7,6},{8,9},{9,8},{10,12... | collective-permute-start | bytes 86024 | tf_op jit(solution)/shard_map/ppermute | solution.py:531
  10.7 0.1 collective-permute-start.4
  10.9 1.1 %main.1 = (f32[16,32,128]{2,1,0:T(8,128)S(1)}, f32[16,32,128]{2,1,0:T(8,128)S(1)}, f32[3,8,128]{2,1,0:T(8,128)S(1)}, f32[3,8,128]{2,1,0:T(8,128)S(1)}, f32[3,8,128]{2,1,0:T(8,128)S(1)}) custom-call(f32[16,32,128]{2,1,0:T(8,128)S(1)} %get-tuple-element.24.c_in, f32[16,32,128]{2,1,0:T(8,128)S(1)} %get-tuple-element.25.b_in, ...), custom_call_target="tpu_custom_call" | custom-call | flops 200000000 | bytes 1048576 | tf_op jit(solution)/shard_map/main/pallas_call | solution.py:487
  12.0 2.1 %collective-permute-done.3.yb = f32[7,8,128]{2,1,0:T(8,128)S(1)} collective-permute-done((f32[7,8,128]{2,1,0:T(8,128)S(1)}, f32[7,8,128]{2,1,0:T(8,128)S(1)}, u32[]{:S(2)}, u32[]{:S(2)}) %collective-permute-start.3) | collective-permute-done | bytes 28704 | tf_op jit(solution)/shard_map/ppermute | solution.py:531
  14.1 0.5 %collective-permute-done.4.ya = f32[7,8,128]{2,1,0:T(8,128)S(1)} collective-permute-done((f32[7,8,128]{2,1,0:T(8,128)S(1)}, f32[7,8,128]{2,1,0:T(8,128)S(1)}, u32[]{:S(2)}, u32[]{:S(2)}) %collective-permute-start.4) | collective-permute-done | bytes 28704 | tf_op jit(solution)/shard_map/ppermute | solution.py:532
  14.6 1.5 %edge.1 = (f32[16,32,128]{2,1,0:T(8,128)}, f32[16,32,128]{2,1,0:T(8,128)}) custom-call(f32[3,32,128]{2,1,0:T(8,128)S(1)} %get-tuple-element.27.pc, f32[3,32,128]{2,1,0:T(8,128)S(1)} %get-tuple-element.28.pb, f32[3,32,128]{2,1,0:T(8,128)S(1)} %get-tuple-element.29.ph, f32[3,8,128]{2,1,0:T(8,128)S(1)} %get-tuple-element.37.qc, ...), custom_call_target="tpu_custom_call" | custom-call | flops 1000000 | bytes 1048576 | tf_op jit(solution)/shard_map/edge/pallas_call | solution.py:487
  (1 shorter events, 0.0 us)
Async XLA Ops:
  0.6 1.2 %copy-start.3 = (f32[16,32,128]{2,1,0:T(8,128)S(1)}, f32[16,32,128]{2,1,0:T(8,128)}, u32[]{:S(2)}) copy-start(f32[16,32,128]{2,1,0:T(8,128)} %cot_h.1) | copy-start | bytes 786436
  0.6 1.2 %copy-start.2 = (f32[16,32,128]{2,1,0:T(8,128)S(1)}, f32[16,32,128]{2,1,0:T(8,128)}, u32[]{:S(2)}) copy-start(f32[16,32,128]{2,1,0:T(8,128)} %src_h.1) | copy-start | bytes 786436
  0.7 1.2 %copy-start.1 = (s32[16,32,128]{2,1,0:T(8,128)S(1)}, s32[16,32,128]{2,1,0:T(8,128)}, u32[]{:S(2)}) copy-start(s32[16,32,128]{2,1,0:T(8,128)} %sea_h.1) | copy-start | bytes 786436
  0.7 1.3 %copy-start = (f32[16,32,128]{2,1,0:T(8,128)S(1)}, f32[16,32,128]{2,1,0:T(8,128)}, u32[]{:S(2)}) copy-start(f32[16,32,128]{2,1,0:T(8,128)} %lr_h.1) | copy-start | bytes 786436
  1.7 1.4 %collective-permute-start = (f32[8,32,128]{2,1,0:T(8,128)S(1)}, f32[8,32,128]{2,1,0:T(8,128)S(1)}, u32[]{:S(2)}, u32[]{:S(2)}) collective-permute-start(f32[8,32,128]{2,1,0:T(8,128)S(1)} %prepare_z.1), channel_id=1, source_target_pairs={{0,1},{1,0},{2,3},{3,2},{4,5},{5,4},{6,7},{7,6},{8,9},{9,8},{10,11... | collective-permute-start | bytes 393224 | tf_op jit(solution)/shard_map/ppermute | solution.py:514
  3.2 4.4 %collective-permute-start.1 = (f32[17,8,128]{2,1,0:T(8,128)S(1)}, f32[17,8,128]{2,1,0:T(8,128)S(1)}, u32[]{:S(2)}, u32[]{:S(2)}) collective-permute-start(f32[17,8,128]{2,1,0:T(8,128)S(1)} %get-tuple-element.30), channel_id=1, source_target_pairs={{0,8},{1,9},{2,10},{3,11},{4,12},{5,13},{6,14},{7,15},{8,0},{9,1},... | collective-permute-start | bytes 208904 | tf_op jit(solution)/shard_map/ppermute | solution.py:516
  4.8 4.3 %collective-permute-start.2 = (f32[17,8,128]{2,1,0:T(8,128)S(1)}, f32[17,8,128]{2,1,0:T(8,128)S(1)}, u32[]{:S(2)}, u32[]{:S(2)}) collective-permute-start(f32[17,8,128]{2,1,0:T(8,128)S(1)} %get-tuple-element.31), channel_id=1, source_target_pairs={{0,1},{1,0},{2,3},{3,2},{4,5},{5,4},{6,7},{7,6},{8,16},{9,17},{10,... | collective-permute-start | bytes 208904 | tf_op jit(solution)/shard_map/ppermute | solution.py:517
  9.2 4.8 %collective-permute-start.3 = (f32[7,8,128]{2,1,0:T(8,128)S(1)}, f32[7,8,128]{2,1,0:T(8,128)S(1)}, u32[]{:S(2)}, u32[]{:S(2)}) collective-permute-start(f32[7,8,128]{2,1,0:T(8,128)S(1)} %get-tuple-element.40), channel_id=1, source_target_pairs={{0,1},{1,0},{2,4},{3,5},{4,2},{5,3},{6,7},{7,6},{8,9},{9,8},{10,12... | collective-permute-start | bytes 86024 | tf_op jit(solution)/shard_map/ppermute | solution.py:531
  10.7 3.9 %collective-permute-start.4 = (f32[7,8,128]{2,1,0:T(8,128)S(1)}, f32[7,8,128]{2,1,0:T(8,128)S(1)}, u32[]{:S(2)}, u32[]{:S(2)}) collective-permute-start(f32[7,8,128]{2,1,0:T(8,128)S(1)} %get-tuple-element.41), channel_id=1, source_target_pairs={{0,2},{1,3},{2,0},{3,1},{4,6},{5,7},{6,4},{7,5},{8,10},{9,11},{10,... | collective-permute-start | bytes 86024 | tf_op jit(solution)/shard_map/ppermute | solution.py:532
